TPU v7x, 8 devices: a whole 2x2x1 slice. The times are simulated.
8 devices in a mesh: dp: 2 (over z, y), tp: 4 (over x, core).
Axes of the slice: x: 2, y: 2, z: 1, core: 2. Of those that a mesh axis runs over, the one named last changes fastest.
Arguments:
- hidden: bfloat16 [8, 4096, 2048], P('dp', 'tp'), parts along dimension 0
- attn_gain: float32 [2048], replicated
- w_q: bfloat16 [2048, 2048], P(None, 'tp')
- w_k: bfloat16 [2048, 2048], P(None, 'tp')
- w_v: bfloat16 [2048, 2048], P(None, 'tp')
- q_gain: float32 [2048], P('tp')
- k_gain: float32 [2048], P('tp')
- w_o: bfloat16 [2048, 2048], P('tp')
Outputs:
- output 1: bfloat16 [8, 4096, 2048], P('dp', 'tp'), parts along dimension 0
- output 2: bfloat16 [8, 4096, 16, 128], P('dp', None, 'tp'), parts along dimension 0
- output 3: bfloat16 [8, 4096, 16, 128], P('dp', None, 'tp'), parts along dimension 0
There are 2 independent parts. A program takes and returns all parts, laid end to end along the dimension named above; an argument that names none is the same for every part.
All inputs are finite; a program needn't handle non-finite values.
Results may differ from a plain program's by a relative error of at most 0.00850629.
Values are sent between devices in bfloat16 or wider.
A program may use at most 1 GiB of HBM per device.

v0:
```python
import jax
import jax.numpy as jnp
from jax import lax
from jax.sharding import PartitionSpec as P

HEAD_DIM = 128


def rope_tables(seq_len, head_dim):
    half_dim = head_dim // 2
    inv_freq = 10000.0 ** (-jnp.arange(half_dim, dtype=jnp.float32) * (2.0 / head_dim))
    angles = jnp.arange(seq_len, dtype=jnp.float32)[:, None] * inv_freq[None, :]
    return jnp.cos(angles), jnp.sin(angles)


def apply_rope(heads_in, cos_tab, sin_tab):
    half_dim = heads_in.shape[-1] // 2
    lower_half = heads_in[..., :half_dim]
    upper_half = heads_in[..., half_dim:]
    cos_bcast = cos_tab[None, :, None, :]
    sin_bcast = sin_tab[None, :, None, :]
    return jnp.concatenate([lower_half * cos_bcast - upper_half * sin_bcast, upper_half * cos_bcast + lower_half * sin_bcast], axis=-1)


def causal_attention(q_rot, k_rot, v_heads):
    seq_len = q_rot.shape[1]
    q_tile = min(seq_len, 128)
    score_scale = q_rot.shape[-1] ** -0.5
    tile_outs = []
    for tile_idx in range(seq_len // q_tile):
        q_start = tile_idx * q_tile
        q_stop = q_start + q_tile
        q_part = q_rot[:, q_start:q_stop]
        if tile_outs:
            q_part, prev_out = lax.optimization_barrier((q_part, tile_outs[-1]))
            tile_outs[-1] = prev_out
        scores = jnp.einsum('bqhd,bkhd->bhqk', q_part, k_rot[:, :q_stop], preferred_element_type=jnp.float32) * score_scale
        q_pos = q_start + jnp.arange(q_tile)
        k_pos = jnp.arange(q_stop)
        scores = jnp.where(q_pos[:, None] >= k_pos[None, :], scores, -1e30)
        prob_bf = jax.nn.softmax(scores, axis=-1).astype(jnp.bfloat16)
        tile_out = jnp.einsum('bhqk,bkhd->bqhd', prob_bf, v_heads[:, :q_stop], preferred_element_type=jnp.float32)
        tile_outs.append(tile_out.astype(jnp.bfloat16))
    return jnp.concatenate(tile_outs, axis=1)


def solution(mesh):
    def local_block(x_local, attn_gain, wq_cols, wk_cols, wv_cols, qg_cols, kg_cols, wo_rows):
        n_batch = x_local.shape[0]
        width = x_local.shape[2]
        x_f32 = x_local.astype(jnp.float32)
        inv_rms = lax.rsqrt(jnp.mean(x_f32 * x_f32, axis=-1, keepdims=True) + 1e-5)
        normed = (x_f32 * inv_rms * attn_gain).astype(jnp.bfloat16)
        h_full = lax.all_gather(normed, 'tp', axis=1, tiled=True)
        seq_len = h_full.shape[1]
        local_cols = wq_cols.shape[1]
        local_heads = local_cols // HEAD_DIM
        q_raw = jnp.einsum('btd,dc->btc', h_full, wq_cols, preferred_element_type=jnp.float32).astype(jnp.bfloat16)
        k_raw = jnp.einsum('btd,dc->btc', h_full, wk_cols, preferred_element_type=jnp.float32).astype(jnp.bfloat16)
        v_raw = jnp.einsum('btd,dc->btc', h_full, wv_cols, preferred_element_type=jnp.float32).astype(jnp.bfloat16)
        part_sq = jnp.stack([jnp.einsum('btc,btc->bt', q_raw, q_raw, preferred_element_type=jnp.float32), jnp.einsum('btc,btc->bt', k_raw, k_raw, preferred_element_type=jnp.float32)])
        total_sq = lax.psum(part_sq, 'tp')
        inv_norm = lax.rsqrt(total_sq / width + 1e-5)
        q_normed = q_raw.astype(jnp.float32) * inv_norm[0][..., None] * qg_cols
        k_normed = k_raw.astype(jnp.float32) * inv_norm[1][..., None] * kg_cols
        cos_tab, sin_tab = rope_tables(seq_len, HEAD_DIM)
        head_shape = (n_batch, seq_len, local_heads, HEAD_DIM)
        q_rot = apply_rope(q_normed.reshape(head_shape), cos_tab, sin_tab).astype(jnp.bfloat16)
        k_rot = apply_rope(k_normed.reshape(head_shape), cos_tab, sin_tab).astype(jnp.bfloat16)
        v_heads = v_raw.reshape(head_shape)
        attn_out = causal_attention(q_rot, k_rot, v_heads).reshape(n_batch, seq_len, local_cols)
        y_part = jnp.einsum('btc,cd->btd', attn_out, wo_rows, preferred_element_type=jnp.float32).astype(jnp.bfloat16)
        y_local = lax.psum_scatter(y_part, 'tp', scatter_dimension=1, tiled=True)
        hidden_out = (x_f32 + y_local.astype(jnp.float32)).astype(jnp.bfloat16)
        return (hidden_out, k_rot, v_heads)

    seq_spec = P('dp', 'tp', None)
    head_spec = P('dp', None, 'tp', None)
    col_spec = P(None, 'tp')
    return jax.shard_map(local_block, mesh=mesh, in_specs=(seq_spec, P(None), col_spec, col_spec, col_spec, P('tp'), P('tp'), P('tp', None)), out_specs=(seq_spec, head_spec, head_spec), check_vma=False)
```

profile of v0, /device:TPU:0, one launch (start us, length us, event | category | flops | bytes accessed | tf_op | source)
XLA Modules:
  0.0 2774.1 jit_solution(765906814032960650)
XLA Ops:
  65.0 353.9 %all-gather.2.cloned.1.call-done = bf16[4,4096,2048]{2,1,0:T(8,128)(2,1)} async-done(((bf16[4,1024,2048]{2,1,0:T(8,128)(2,1)}), bf16[4,4096,2048]{2,1,0:T(8,128)(2,1)}) %all-gather.2.cloned.1.call-update) | async-done | bytes 67108880 | tf_op jit(solution)/shard_map/all_gather | solution.py:54
  418.9 42.6 %fusion.34 = (f32[4,4096]{1,0:T(4,128)S(1)}, bf16[4,4096,512]{1,2,0:T(8,128)(2,1)}) fusion(bf16[4,4096,2048]{2,1,0:T(8,128)(2,1)} %all-gather.2.cloned.1.call-done, bf16[2048,512]{1,0:T(8,128)(2,1)} %param.11), kind=kOutput, calls=%fused_computation.42 | convolution fusion | flops 34393276416 | bytes 86048768 | tf_op jit(solution)/shard_map/btd,dc->btc/dot_general | solution.py:59
  461.5 42.1 %fusion.33 = (f32[4,4096]{1,0:T(4,128)S(1)}, bf16[4,4096,512]{1,2,0:T(8,128)(2,1)}) fusion(bf16[4,4096,2048]{2,1,0:T(8,128)(2,1)} %all-gather.2.cloned.1.call-done, bf16[2048,512]{1,0:T(8,128)(2,1)S(1)} %copy-done.83), kind=kOutput, calls=%fused_computation.41 | convolution fusion | flops 34393276416 | bytes 86048768 | tf_op jit(solution)/shard_map/btd,dc->btc/dot_general | solution.py:58
  504.3 42.6 %convolution_convert_fusion.1 = bf16[4,4096,512]{1,2,0:T(8,128)(2,1)} fusion(bf16[4,4096,2048]{2,1,0:T(8,128)(2,1)} %all-gather.2.cloned.1.call-done, bf16[2048,512]{1,0:T(8,128)(2,1)} %param.12), kind=kOutput, calls=%fused_computation.240 | convolution fusion | flops 34368126976 | bytes 85983232 | tf_op jit(solution)/shard_map/btd,dc->btc/dot_general | solution.py:60
  547.9 31.7 %fusion.32 = (f32[4,4096,512]{1,2,0:T(8,128)}, f32[4,4096,512]{1,2,0:T(8,128)}) fusion(bf16[4,4096,512]{1,2,0:T(8,128)(2,1)} %get-tuple-element.177, f32[512]{0:T(512)S(1)} %copy-done.81, f32[4,4096]{1,0:T(4,128)S(1)} %get-tuple-element.171, f32[512]{0:T(512)S(1)} %copy-done.82, f32[4,4096]{1,0:T(4,128)S(1)} %get-tuple-element.170, ...), kind=kLoop, calls=%fused_computation.40 | loop fusion | flops 50331648 | bytes 100798464 | tf_op jit(solution)/shard_map/mul | solution.py:64
  714.0 66.6 %subtract_convert_fusion = (bf16[4,4096,4,64]{3,1,2,0:T(8,128)(2,1)}, bf16[4,4096,4,64]{3,1,2,0:T(8,128)(2,1)}, bf16[4,4096,4,64]{3,1,2,0:T(8,128)(2,1)}, bf16[4,4096,4,64]{3,1,2,0:T(8,128)(2,1)}) fusion(f32[4,4096,4,64]{3,1,2,0:T(8,128)} %copy.45, f32[4,4096,4,64]{3,1,2,0:T(8,128)} %copy.44, f32[4096,64]{1,0:T(8,128)} %get-tuple-element.173, ...), kind=kLoop, calls=%fused_computation.52 | loop fusion | flops 67108864 | bytes 102760448 | tf_op jit(solution)/shard_map/convert
  1388.2 24.6 fusion.723
  1440.1 26.0 fusion.724
  1494.4 27.1 fusion.725
  1550.8 28.1 %fusion.726 = (f32[4,4,128]{2,1,0:T(4,128)S(1)}, f32[4,4,128,2944]{3,2,1,0:T(8,128)}) fusion(f32[4,4,128,2944]{3,2,1,0:T(8,128)} %fusion.133, pred[128,2944]{1,0:T(8,128)(4,1)S(1)} %copy-done.58), kind=kOutput, calls=%fused_computation.831 | output fusion | flops 36178816 | bytes 48619520 | tf_op jit(solution)/shard_map/sub | solution.py:41
  1614.1 29.1 %fusion.727 = (f32[4,4,128]{2,1,0:T(4,128)S(1)}, f32[4,4,128,3072]{3,2,1,0:T(8,128)}) fusion(f32[4,4,128,3072]{3,2,1,0:T(8,128)} %fusion.124, pred[128,3072]{1,0:T(8,128)(4,1)S(1)} %copy-done.57), kind=kOutput, calls=%fused_computation.832 | output fusion | flops 37751808 | bytes 50733056 | tf_op jit(solution)/shard_map/sub | solution.py:41
  1680.6 30.3 %fusion.728 = (f32[4,4,128]{2,1,0:T(4,128)S(1)}, f32[4,4,128,3200]{3,2,1,0:T(8,128)}) fusion(f32[4,4,128,3200]{3,2,1,0:T(8,128)} %fusion.114, pred[128,3200]{1,0:T(8,128)(4,1)S(1)} %copy-done.56), kind=kOutput, calls=%fused_computation.833 | output fusion | flops 39324800 | bytes 52846592 | tf_op jit(solution)/shard_map/sub | solution.py:41
  1749.2 31.2 %fusion.729 = (f32[4,4,128]{2,1,0:T(4,128)S(1)}, f32[4,4,128,3328]{3,2,1,0:T(8,128)}) fusion(f32[4,4,128,3328]{3,2,1,0:T(8,128)} %fusion.104, pred[128,3328]{1,0:T(8,128)(4,1)S(1)} %copy-done.55), kind=kOutput, calls=%fused_computation.834 | output fusion | flops 40897792 | bytes 54960128 | tf_op jit(solution)/shard_map/sub | solution.py:41
  1819.1 32.1 %fusion.730 = (f32[4,4,128]{2,1,0:T(4,128)S(1)}, f32[4,4,128,3456]{3,2,1,0:T(8,128)}) fusion(f32[4,4,128,3456]{3,2,1,0:T(8,128)} %fusion.95, pred[128,3456]{1,0:T(8,128)(4,1)S(1)} %copy-done.54), kind=kOutput, calls=%fused_computation.835 | output fusion | flops 42470784 | bytes 57073664 | tf_op jit(solution)/shard_map/sub | solution.py:41
  1867.3 25.4 fusion.85
  1892.7 33.3 %fusion.731 = (f32[4,4,128]{2,1,0:T(4,128)S(1)}, f32[4,4,128,3584]{3,2,1,0:T(8,128)}) fusion(f32[4,4,128,3584]{3,2,1,0:T(8,128)} %fusion.85, pred[128,3584]{1,0:T(8,128)(4,1)S(1)} %copy-done.53), kind=kOutput, calls=%fused_computation.836 | output fusion | flops 44043776 | bytes 59187200 | tf_op jit(solution)/shard_map/sub | solution.py:41
  1942.7 25.2 fusion.76
  1967.9 34.5 %fusion.732 = (f32[4,4,128]{2,1,0:T(4,128)S(1)}, f32[4,4,128,3712]{3,2,1,0:T(8,128)}) fusion(f32[4,4,128,3712]{3,2,1,0:T(8,128)} %fusion.76, pred[128,3712]{1,0:T(8,128)(4,1)S(1)} %copy-done.52), kind=kOutput, calls=%fused_computation.837 | output fusion | flops 45616768 | bytes 61300736 | tf_op jit(solution)/shard_map/sub | solution.py:41
  2019.4 25.1 fusion.66
  2044.5 35.4 %fusion.733 = (f32[4,4,128]{2,1,0:T(4,128)S(1)}, f32[4,4,128,3840]{3,2,1,0:T(8,128)}) fusion(f32[4,4,128,3840]{3,2,1,0:T(8,128)} %fusion.66, pred[128,3840]{1,0:T(8,128)(4,1)S(1)} %copy-done.51), kind=kOutput, calls=%fused_computation.838 | output fusion | flops 47189760 | bytes 63414272 | tf_op jit(solution)/shard_map/sub | solution.py:41
  2120.1 36.6 %fusion.734 = (f32[4,4,128]{2,1,0:T(4,128)S(1)}, f32[4,4,128,3968]{3,2,1,0:T(8,128)}) fusion(f32[4,4,128,3968]{3,2,1,0:T(8,128)} %fusion.56, pred[128,3968]{1,0:T(8,128)(4,1)S(1)} %copy-done.50), kind=kOutput, calls=%fused_computation.839 | output fusion | flops 48762752 | bytes 65527808 | tf_op jit(solution)/shard_map/sub | solution.py:41
  2258.9 47.7 %convolution_convert_fusion = bf16[4,4096,2048]{2,1,0:T(8,128)(2,1)} fusion(bf16[4,4096,512]{1,2,0:T(8,128)(2,1)} %bitcast.179, bf16[512,2048]{1,0:T(8,128)(2,1)S(1)} %copy-done), kind=kOutput, calls=%fused_computation.32 | convolution fusion | flops 34393292800 | bytes 85983232 | tf_op jit(solution)/shard_map/btc,cd->btd/dot_general | solution.py:72
  2306.6 26.0 copy.23
  2352.7 394.6 %reduce-scatter.2.cloned.1.call-done = bf16[4,1024,2048]{2,1,0:T(8,128)(2,1)} async-done(((bf16[4,4096,2048]{2,1,0:T(8,128)(2,1)}), bf16[4,1024,2048]{2,1,0:T(8,128)(2,1)}) %reduce-scatter.2.cloned.1.call-update) | async-done | bytes 16777232 | tf_op jit(solution)/shard_map/reduce_scatter | solution.py:73
  (406 shorter events, 1267.3 us)
Async XLA Ops:
  7.2 2251.8 %copy-start = (bf16[512,2048]{1,0:T(8,128)(2,1)S(1)}, bf16[512,2048]{1,0:T(8,128)(2,1)}, u32[]{:S(2)}) copy-start(bf16[512,2048]{1,0:T(8,128)(2,1)} %param.15) | copy-start | bytes 6291460
  7.2 411.7 %all-gather.2.cloned.1.call-start = ((), (), s32[]{:S(2)}) async-start(), calls=%async_computation.1 | async-start | bytes 83886080 | tf_op jit(solution)/shard_map/all_gather | solution.py:54
  26.2 520.7 %all-reduce.2.cloned.1.call-start = ((), (), s32[]{:S(2)}) async-start(), calls=%async_computation.2 | async-start | bytes 262144 | tf_op jit(solution)/shard_map/psum | solution.py:62
  418.9 42.6 %copy-start.83 = (bf16[2048,512]{1,0:T(8,128)(2,1)S(1)}, bf16[2048,512]{1,0:T(8,128)(2,1)}, u32[]{:S(2)}) copy-start(bf16[2048,512]{1,0:T(8,128)(2,1)} %param.10) | copy-start | bytes 6291460
  504.3 43.6 %copy-start.81 = (f32[512]{0:T(512)S(1)}, f32[512]{0:T(512)}, u32[]{:S(2)}) copy-start(f32[512]{0:T(512)} %param.13) | copy-start | bytes 6148
  504.3 43.6 %copy-start.82 = (f32[512]{0:T(512)S(1)}, f32[512]{0:T(512)}, u32[]{:S(2)}) copy-start(f32[512]{0:T(512)} %param.14) | copy-start | bytes 6148
  504.3 2243.1 %reduce-scatter.2.cloned.1.call-start = ((), (), s32[]{:S(2)}) async-start(), calls=%async_computation.3 | async-start | bytes 83886080 | tf_op jit(solution)/shard_map/reduce_scatter | solution.py:73
  1867.3 25.4 copy-start.53
  2174.9 31.8 %copy-start.35 = (bf16[4,128,4,128]{1,3,2,0:T(8,128)(2,1)S(1)}, bf16[4,128,4,128]{1,3,2,0:T(8,128)(2,1)}, u32[]{:S(2)}) copy-start(bf16[4,128,4,128]{1,3,2,0:T(8,128)(2,1)} %fusion.497) | copy-start | bytes 1572868
  2174.9 32.7 %copy-start.36 = (bf16[4,128,4,128]{1,3,2,0:T(8,128)(2,1)S(1)}, bf16[4,128,4,128]{1,3,2,0:T(8,128)(2,1)}, u32[]{:S(2)}) copy-start(bf16[4,128,4,128]{1,3,2,0:T(8,128)(2,1)} %fusion.494) | copy-start | bytes 1572868
  2174.9 33.6 %copy-start.37 = (bf16[4,128,4,128]{1,3,2,0:T(8,128)(2,1)S(1)}, bf16[4,128,4,128]{1,3,2,0:T(8,128)(2,1)}, u32[]{:S(2)}) copy-start(bf16[4,128,4,128]{1,3,2,0:T(8,128)(2,1)} %fusion.491) | copy-start | bytes 1572868
  2174.9 34.5 %copy-start.38 = (bf16[4,128,4,128]{1,3,2,0:T(8,128)(2,1)S(1)}, bf16[4,128,4,128]{1,3,2,0:T(8,128)(2,1)}, u32[]{:S(2)}) copy-start(bf16[4,128,4,128]{1,3,2,0:T(8,128)(2,1)} %fusion.488) | copy-start | bytes 1572868
  2174.9 35.4 %copy-start.39 = (bf16[4,128,4,128]{1,3,2,0:T(8,128)(2,1)S(1)}, bf16[4,128,4,128]{1,3,2,0:T(8,128)(2,1)}, u32[]{:S(2)}) copy-start(bf16[4,128,4,128]{1,3,2,0:T(8,128)(2,1)} %fusion.485) | copy-start | bytes 1572868
  2174.9 36.3 %copy-start.40 = (bf16[4,128,4,128]{1,3,2,0:T(8,128)(2,1)S(1)}, bf16[4,128,4,128]{1,3,2,0:T(8,128)(2,1)}, u32[]{:S(2)}) copy-start(bf16[4,128,4,128]{1,3,2,0:T(8,128)(2,1)} %fusion.442) | copy-start | bytes 1572868
  2174.9 37.2 %copy-start.42 = (bf16[4,128,4,128]{1,3,2,0:T(8,128)(2,1)S(1)}, bf16[4,128,4,128]{1,3,2,0:T(8,128)(2,1)}, u32[]{:S(2)}) copy-start(bf16[4,128,4,128]{1,3,2,0:T(8,128)(2,1)} %fusion.439) | copy-start | bytes 1572868
  2174.9 38.1 %copy-start.43 = (bf16[4,128,4,128]{1,3,2,0:T(8,128)(2,1)S(1)}, bf16[4,128,4,128]{1,3,2,0:T(8,128)(2,1)}, u32[]{:S(2)}) copy-start(bf16[4,128,4,128]{1,3,2,0:T(8,128)(2,1)} %fusion.482) | copy-start | bytes 1572868
  2175.0 38.9 %copy-start.44 = (bf16[4,128,4,128]{1,3,2,0:T(8,128)(2,1)S(1)}, bf16[4,128,4,128]{1,3,2,0:T(8,128)(2,1)}, u32[]{:S(2)}) copy-start(bf16[4,128,4,128]{1,3,2,0:T(8,128)(2,1)} %fusion.479) | copy-start | bytes 1572868
  2175.0 39.8 %copy-start.45 = (bf16[4,128,4,128]{1,3,2,0:T(8,128)(2,1)S(1)}, bf16[4,128,4,128]{1,3,2,0:T(8,128)(2,1)}, u32[]{:S(2)}) copy-start(bf16[4,128,4,128]{1,3,2,0:T(8,128)(2,1)} %fusion.476) | copy-start | bytes 1572868
  2175.0 40.7 %copy-start.46 = (bf16[4,128,4,128]{1,3,2,0:T(8,128)(2,1)S(1)}, bf16[4,128,4,128]{1,3,2,0:T(8,128)(2,1)}, u32[]{:S(2)}) copy-start(bf16[4,128,4,128]{1,3,2,0:T(8,128)(2,1)} %fusion.473) | copy-start | bytes 1572868
  2175.0 41.6 %copy-start.47 = (bf16[4,128,4,128]{1,3,2,0:T(8,128)(2,1)S(1)}, bf16[4,128,4,128]{1,3,2,0:T(8,128)(2,1)}, u32[]{:S(2)}) copy-start(bf16[4,128,4,128]{1,3,2,0:T(8,128)(2,1)} %fusion.470) | copy-start | bytes 1572868
  2175.0 42.4 %copy-start.48 = (bf16[4,128,4,128]{1,3,2,0:T(8,128)(2,1)S(1)}, bf16[4,128,4,128]{1,3,2,0:T(8,128)(2,1)}, u32[]{:S(2)}) copy-start(bf16[4,128,4,128]{1,3,2,0:T(8,128)(2,1)} %fusion.467) | copy-start | bytes 1572868
  2175.0 43.3 %copy-start.49 = (bf16[4,128,4,128]{1,3,2,0:T(8,128)(2,1)S(1)}, bf16[4,128,4,128]{1,3,2,0:T(8,128)(2,1)}, u32[]{:S(2)}) copy-start(bf16[4,128,4,128]{1,3,2,0:T(8,128)(2,1)} %fusion.464) | copy-start | bytes 1572868
  2175.0 44.2 %copy-start.33 = (bf16[4,128,4,128]{3,1,2,0:T(8,128)(2,1)S(1)}, bf16[4,128,4,128]{3,1,2,0:T(8,128)(2,1)}, u32[]{:S(2)}) copy-start(bf16[4,128,4,128]{3,1,2,0:T(8,128)(2,1)} %pad_maximum_fusion) | copy-start | bytes 1572868
  2175.0 44.2 %copy-start.34 = (pred[128,4096]{1,0:T(8,128)(4,1)S(1)}, pred[128,4096]{1,0:T(8,128)(4,1)}, u32[]{:S(2)}) copy-start(pred[128,4096]{1,0:T(8,128)(4,1)} %iota_compare_fusion) | copy-start | bytes 1572868
  (79 other events, 959.2 us)
Sparse Core Ops, SparseCore 0:
  26.3 392.4 all-gather.1
  504.4 26.1 all-reduce.1
  2306.8 440.5 reduce-scatter.1
where the time goes:
time: 2780 us; the launch traced here: 2770 us
  matrix products  970 us (35%)
  other arithmetic  793 us (29%)
  waiting for transfers between devices  749 us (27%)
  local copies, waits for them, and re-layouts  248 us (9%)
    sub x29, other arithmetic, causal_attention(): prob_bf = jax.nn.softmax(scores, axis=-1).astype(jnp.bfloat16)  585 us
    reduce_scatter x1, waiting for transfers between devices, local_block(): y_local = lax.psum_scatter(y_part, 'tp', scatter_dimension=1, tiled=True)  395 us
    dot_general x30, matrix products, causal_attention(): jnp.einsum('bqhd,bkhd->bhqk', q_part, k_rot[:, :q_stop], preferred_elemen...  392 us
    dot_general x32, matrix products, causal_attention(): jnp.einsum('bhqk,bkhd->bqhd', prob_bf, v_heads[:, :q_stop], preferred_ele...  368 us
    all_gather x1, waiting for transfers between devices, local_block(): h_full = lax.all_gather(normed, 'tp', axis=1, tiled=True)  354 us
    unnamed x237, local copies, waits for them, and re-layouts  205 us
    another operation x1, other arithmetic  66.6 us
  transfers between devices with their start and end apart: 3, of which 2 were waited for; matrix products, arithmetic and copies ran while one was open for 5% of the time, Pallas kernels for 0%

commit v1 on v0

v1 whole, which is shorter than its diff:
```python
import functools
import math

import jax
import jax.numpy as jnp
from jax import lax
from jax.experimental import pallas as pl
from jax.experimental.pallas import tpu as pltpu
from jax.sharding import PartitionSpec as P

HD = 128
LOG2E = math.log2(math.e)
F32 = jnp.float32
BF16 = jnp.bfloat16
VMEM_LIMIT = 60 * 1024 * 1024


def params(*sem):
    return pltpu.CompilerParams(dimension_semantics=sem, vmem_limit_bytes=VMEM_LIMIT)


def cost(flops, nbytes, trans=0):
    return pl.CostEstimate(flops=int(flops), bytes_accessed=int(nbytes), transcendentals=int(trans))


def rope_tables(seq_len):
    half_dim = HD // 2
    inv_freq = 10000.0 ** (-jnp.arange(half_dim, dtype=F32) * (2.0 / HD))
    angles = jnp.arange(seq_len, dtype=F32)[:, None] * inv_freq[None, :]
    c, s = jnp.cos(angles), jnp.sin(angles)
    return jnp.concatenate([c, c], axis=1), jnp.concatenate([-s, s], axis=1)


def sq_sum(a):
    part = None
    for g in range(a.shape[1] // HD):
        t = a[:, g * HD:(g + 1) * HD]
        part = t * t if part is None else part + t * t
    return jnp.sum(part.T, axis=0, keepdims=True)


def spread_heads(scr, blocks):
    n = len(blocks)
    rows = blocks[0].shape[0]
    for g, t in enumerate(blocks):
        scr[pl.ds(g, rows, stride=n), :] = t
    return scr[...].astype(BF16)


def qkv_kernel(h_ref, wq_ref, wk_ref, wv_ref, *refs):
    q_ref, k_ref, v_ref, vc_ref, ss_ref, scr = refs[-6:]
    h = h_ref[...]
    cols = wq_ref.shape[1]
    q = jnp.dot(h, wq_ref[...], preferred_element_type=F32).astype(BF16)
    q_ref[...] = q
    k = jnp.dot(h, wk_ref[...], preferred_element_type=F32).astype(BF16)
    k_ref[...] = k
    ss_ref[0:1, :] = sq_sum(q.astype(F32))
    v = jnp.dot(h, wv_ref[...], preferred_element_type=F32)
    v_ref[...] = v.astype(BF16)
    ss_ref[1:2, :] = sq_sum(k.astype(F32))
    vc_ref[...] = spread_heads(scr, [v[:, g * HD:(g + 1) * HD] for g in range(cols // HD)])


def qkv_call(h, wq, wk, wv, vc_prev, b, n_batch):
    seq, width = h.shape
    cols = wq.shape[1]
    heads = cols // HD
    bq = 512
    nq = seq // bq
    wspec = pl.BlockSpec((width, cols), lambda i: (0, 0))
    rspec = pl.BlockSpec((bq, cols), lambda i: (i, 0))
    in_specs = [pl.BlockSpec((bq, width), lambda i: (i, 0)), wspec, wspec, wspec]
    args = [h, wq, wk, wv]
    aliases = {}
    if vc_prev is not None:
        in_specs.append(pl.BlockSpec(memory_space=pl.ANY))
        args.append(vc_prev)
        aliases = {4: 3}
    base = b * nq
    return pl.pallas_call(
        qkv_kernel,
        grid=(nq,),
        in_specs=in_specs,
        out_specs=[rspec, rspec, rspec, pl.BlockSpec((bq * heads, HD), lambda i: (base + i, 0)), pl.BlockSpec((2, bq), lambda i: (0, i))],
        out_shape=[jax.ShapeDtypeStruct((seq, cols), BF16)] * 3 + [jax.ShapeDtypeStruct((n_batch * seq * heads, HD), BF16), jax.ShapeDtypeStruct((2, seq), F32)],
        scratch_shapes=[pltpu.VMEM((bq * heads, HD), F32)],
        input_output_aliases=aliases,
        compiler_params=params("arbitrary"),
        cost_estimate=cost(6 * seq * width * cols, 2 * (seq * width + 3 * width * cols + 4 * seq * cols)),
        name="qkv",
    )(*args)


def rope_kernel(width, q_ref, k_ref, ss_ref, qg_ref, kg_ref, c_ref, s_ref, *refs):
    qr_ref, kr_ref, kc_ref, scr = refs[-4:]
    ct, st = c_ref[...], s_ref[...]
    rows = q_ref.shape[0]
    inv = lax.rsqrt(ss_ref[...] * (1.0 / width) + 1e-5)
    inv_t = jnp.concatenate([inv, jnp.zeros((6, rows), F32)], axis=0).T

    def turn(x_ref, col, g_ref):
        scale = inv_t[:, col:col + 1]
        outs = []
        for g in range(x_ref.shape[1] // HD):
            sl = slice(g * HD, (g + 1) * HD)
            n = x_ref[:, sl].astype(F32) * scale * g_ref[:, sl]
            outs.append(n * ct + pltpu.roll(n, HD // 2, 1) * st)
        return outs

    for g, t in enumerate(turn(q_ref, 0, qg_ref)):
        qr_ref[:, g * HD:(g + 1) * HD] = t.astype(BF16)
    ks = turn(k_ref, 1, kg_ref)
    for g, t in enumerate(ks):
        kr_ref[:, g * HD:(g + 1) * HD] = t.astype(BF16)
    kc_ref[...] = spread_heads(scr, ks)


def rope_call(q, k, ss, qg, kg, ct, st, kc_prev, b, n_batch, width):
    seq, cols = q.shape
    heads = cols // HD
    bq = 512
    nq = seq // bq
    rspec = pl.BlockSpec((bq, cols), lambda i: (i, 0))
    tspec = pl.BlockSpec((bq, HD), lambda i: (i, 0))
    gspec = pl.BlockSpec((1, cols), lambda i: (0, 0))
    in_specs = [rspec, rspec, pl.BlockSpec((2, bq), lambda i: (0, i)), gspec, gspec, tspec, tspec]
    args = [q, k, ss, qg, kg, ct, st]
    aliases = {}
    if kc_prev is not None:
        in_specs.append(pl.BlockSpec(memory_space=pl.ANY))
        args.append(kc_prev)
        aliases = {7: 2}
    base = b * nq
    return pl.pallas_call(
        functools.partial(rope_kernel, width),
        grid=(nq,),
        in_specs=in_specs,
        out_specs=[rspec, rspec, pl.BlockSpec((bq * heads, HD), lambda i: (base + i, 0))],
        out_shape=[jax.ShapeDtypeStruct((seq, cols), BF16)] * 2 + [jax.ShapeDtypeStruct((n_batch * seq * heads, HD), BF16)],
        scratch_shapes=[pltpu.VMEM((bq * heads, HD), F32)],
        input_output_aliases=aliases,
        compiler_params=params("arbitrary"),
        cost_estimate=cost(7e9, 10 * seq * cols),
        name="rope",
    )(*args)


def attn_kernel(n_h, bq, q_ref, k_ref, v_ref, o_ref, m_s, l_s, acc_s):
    i = pl.program_id(1)
    c = HD ** -0.5 * LOG2E
    nl = bq // HD

    def step(j, first):
        rows = pl.ds(pl.multiple_of(j * bq, bq), bq)
        scores = []
        for g in range(n_h):
            sl = slice(g * HD, (g + 1) * HD)
            s = lax.dot_general(q_ref[:, sl], k_ref[rows, sl], (((1,), (1,)), ((), ())), preferred_element_type=F32)
            if first:
                keep = lax.broadcasted_iota(jnp.int32, (bq, bq), 0) >= lax.broadcasted_iota(jnp.int32, (bq, bq), 1)
                s = jnp.where(keep, s, -1e30)
            scores.append(s)
        for g in range(n_h):
            sl = slice(g * HD, (g + 1) * HD)
            s = scores[g]
            top = jnp.max(s, axis=1, keepdims=True) * c
            if first:
                m_new = jnp.broadcast_to(top, (bq, HD))
            else:
                m_old = m_s[g]
                m_new = jnp.maximum(m_old, top)
            parts = [jnp.exp2(s[:, t * HD:(t + 1) * HD] * c - m_new) for t in range(nl)]
            l_new = functools.reduce(lambda a, b2: a + b2, parts)
            p = jnp.concatenate([t.astype(BF16) for t in parts], axis=1)
            pv = jnp.dot(p, v_ref[rows, sl], preferred_element_type=F32)
            m_s[g] = m_new
            if first:
                l_s[g] = l_new
                acc_s[g] = pv
            else:
                alpha = jnp.exp2(m_old - m_new)
                l_s[g] = l_s[g] * alpha + l_new
                acc_s[g] = acc_s[g] * alpha + pv

    step(i, True)

    def body(j, carry):
        step(j, False)
        return carry

    lax.fori_loop(0, i, body, 0)
    for g in range(n_h):
        l = jnp.sum(l_s[g], axis=1, keepdims=True)
        o_ref[:, g * HD:(g + 1) * HD] = (acc_s[g] / l).astype(BF16)


def attn_call(q, k, v):
    seq, cols = q.shape
    bq = 512
    n_h = 2
    qspec = pl.BlockSpec((bq, n_h * HD), lambda h, i: (i, h))
    kspec = pl.BlockSpec((seq, n_h * HD), lambda h, i: (0, h))
    return pl.pallas_call(
        functools.partial(attn_kernel, n_h, bq),
        grid=(cols // (n_h * HD), seq // bq),
        in_specs=[qspec, kspec, kspec],
        out_specs=qspec,
        out_shape=jax.ShapeDtypeStruct((seq, cols), BF16),
        scratch_shapes=[pltpu.VMEM((n_h, bq, HD), F32)] * 3,
        compiler_params=params("arbitrary", "arbitrary"),
        cost_estimate=cost(4 * seq * seq * cols, 8 * seq * cols, seq * seq * cols // HD // 2),
        name="attn",
    )(q, k, v)


def out_kernel(o0, o1, o2, o3, w0, w1, w2, w3, x_ref, *refs):
    out_ref = refs[-1]
    acc = jnp.dot(o0[...], w0[...], preferred_element_type=F32)
    for o, w in ((o1, w1), (o2, w2), (o3, w3)):
        acc += jnp.dot(o[...], w[...], preferred_element_type=F32)
    y = acc.astype(BF16).astype(F32)
    out_ref[0] = (x_ref[0].astype(F32) + y).astype(BF16)


def out_call(os, ws, x, prev, b):
    n_batch, rows, width = x.shape
    cols = os[0].shape[1]
    bn = 512
    ospec = pl.BlockSpec((rows, cols), lambda n: (0, 0))
    wspec = pl.BlockSpec((cols, bn), lambda n: (0, n))
    xspec = pl.BlockSpec((1, rows, bn), lambda n: (b, 0, n))
    in_specs = [ospec] * 4 + [wspec] * 4 + [xspec]
    args = [*os, *ws, x]
    aliases = {}
    if prev is not None:
        in_specs.append(pl.BlockSpec(memory_space=pl.ANY))
        args.append(prev)
        aliases = {9: 0}
    return pl.pallas_call(
        out_kernel,
        grid=(width // bn,),
        in_specs=in_specs,
        out_specs=xspec,
        out_shape=jax.ShapeDtypeStruct(x.shape, BF16),
        input_output_aliases=aliases,
        compiler_params=params("arbitrary"),
        cost_estimate=cost(2 * rows * width * width, 2 * (width * width + 3 * rows * width)),
        name="outproj",
    )(*args)


def solution(mesh):
    n_tp = mesh.shape['tp']
    pairs = {r: [(d, d ^ r) for d in range(n_tp)] for r in range(1, n_tp)}

    def local_block(x_local, attn_gain, wq, wk, wv, qg, kg, wo_rows):
        n_batch, rows, width = x_local.shape
        seq = rows * n_tp
        cols = wq.shape[1]
        me = lax.axis_index('tp')
        ct, st = rope_tables(seq)

        def exchange(o):
            res = []
            for r in range(n_tp):
                piece = lax.dynamic_slice_in_dim(o, (me ^ r) * rows, rows, axis=0)
                res.append(piece if r == 0 else lax.ppermute(piece, 'tp', pairs[r]))
            return res

        qg, kg = qg.reshape(1, cols), kg.reshape(1, cols)
        hs = []
        for b in range(n_batch):
            xf = x_local[b].astype(F32)
            inv_rms = lax.rsqrt(jnp.mean(xf * xf, axis=-1, keepdims=True) + 1e-5)
            normed = (xf * inv_rms * attn_gain).astype(BF16)
            hs.append(lax.all_gather(normed, 'tp', axis=0, tiled=True))
        vc = kc = out = o_prev = ws = None
        pend = []
        for b in range(n_batch):
            if o_prev is not None:
                hs[b], o_prev = lax.optimization_barrier((hs[b], o_prev))
                pend.append((b - 1, exchange(o_prev)))
            q, k, v, vc, ss = qkv_call(hs[b], wq, wk, wv, vc, b, n_batch)
            s1 = lax.ppermute(ss, 'tp', pairs[1])
            pair_ss = ss + s1
            tot = pair_ss + lax.ppermute(pair_ss, 'tp', pairs[2])
            if b == 1:
                wo_rows, q = lax.optimization_barrier((wo_rows, q))
                w2 = lax.ppermute(wo_rows, 'tp', pairs[2])
                ws = [wo_rows, lax.ppermute(wo_rows, 'tp', pairs[1]), w2, lax.ppermute(w2, 'tp', pairs[1])]
            if len(pend) > 1:
                pb, pos = pend.pop(0)
                pos[0], q = lax.optimization_barrier((pos[0], q))
                out = out_call(pos, ws, x_local, out, pb)
                tot, out = lax.optimization_barrier((tot, out))
            qr, kr, kc = rope_call(q, k, tot, qg, kg, ct, st, kc, b, n_batch, width)
            o_prev = attn_call(qr, kr, v)
        pend.append((n_batch - 1, exchange(o_prev)))
        for pb, pos in pend:
            out = out_call(pos, ws, x_local, out, pb)
        shape = (n_batch, seq, cols // HD, HD)
        return (out, kc.reshape(shape), vc.reshape(shape))

    seq_spec = P('dp', 'tp', None)
    head_spec = P('dp', None, 'tp', None)
    col_spec = P(None, 'tp')
    return jax.shard_map(local_block, mesh=mesh, in_specs=(seq_spec, P(None), col_spec, col_spec, col_spec, P('tp'), P('tp'), P('tp', None)), out_specs=(seq_spec, head_spec, head_spec), check_vma=False)
```

time: 2780 us -> 871 us (0.31)
  matrix products: 970 us -> 0 us
  other arithmetic: 793 us -> 30.4 us
  Pallas kernels: 0 us -> 527 us
  waiting for transfers between devices: 749 us -> 262 us
  local copies, waits for them, and re-layouts: 248 us -> 18.1 us
    dot_general x66 -> x0, matrix products: 935 us -> none  [the longest x30 392 us: causal_attention(): jnp.einsum('bqhd,bkhd->bhqk', q_part, k_rot[:, :q_stop], preferred_elemen...]
    sub x29 -> x0, other arithmetic: 585 us -> none  [causal_attention(): prob_bf = jax.nn.softmax(scores, axis=-1).astype(jnp.bfloat16)]
    pallas_call x0 -> x16, Pallas kernels: none -> 527 us  [the longest x4 288 us: attn_call(): pl.pallas_call(functools.partial(attn_kernel, n_h, bq), grid=(cols // (n_...]
    reduce_scatter x1 -> x0, waiting for transfers between devices: 395 us -> none  [local_block(): y_local = lax.psum_scatter(y_part, 'tp', scatter_dimension=1, tiled=True)]
    all_gather x1 -> x4, waiting for transfers between devices: 354 us -> 105 us  [local_block(): hs.append(lax.all_gather(normed, 'tp', axis=0, tiled=True))]
    unnamed x237 -> x26, local copies, waits for them, and re-layouts: 205 us -> 3.89 us
    ppermute x0 -> x23, waiting for transfers between devices: none -> 155 us  [the longest x12 117 us: exchange(): res.append(piece if r == 0 else lax.ppermute(piece, 'tp', pairs[r]))]
    another operation x2 -> x0, other arithmetic: 67.2 us -> none
  transfers between devices with their start and end apart: 3 -> 27, of which waited for: 2 -> 10; matrix products, arithmetic and copies ran while one was open for 5% -> 3% of each run, Pallas kernels for 0% -> 59%
where the time goes in v1:
time: 871 us; the launch traced here: 867 us
  Pallas kernels  527 us (61%)
  waiting for transfers between devices  262 us (30%)
  other arithmetic  30.4 us (3%)
  local copies, waits for them, and re-layouts  18.1 us (2%)
  starting transfers between devices  14.6 us (2%)
  between operations  14.4 us (2%)
    pallas_call x4, Pallas kernels, attn_call(): pl.pallas_call(functools.partial(attn_kernel, n_h, bq), grid=(cols // (n_...  288 us
    pallas_call x4, Pallas kernels, qkv_call(): pl.pallas_call(qkv_kernel, grid=(nq,), in_specs=in_specs, out_specs=[rspe...  131 us
    ppermute x12, waiting for transfers between devices, exchange(): res.append(piece if r == 0 else lax.ppermute(piece, 'tp', pairs[r]))  117 us
    all_gather x4, waiting for transfers between devices, local_block(): hs.append(lax.all_gather(normed, 'tp', axis=0, tiled=True))  105 us
    pallas_call x4, Pallas kernels, out_call(): pl.pallas_call(out_kernel, grid=(width // bn,), in_specs=in_specs, out_sp...  55.5 us
    pallas_call x4, Pallas kernels, rope_call(): pl.pallas_call(functools.partial(rope_kernel, width), grid=(nq,), in_spec...  53 us
    ppermute x4, waiting for transfers between devices, local_block(): tot = pair_ss + lax.ppermute(pair_ss, 'tp', pairs[2])  35.8 us
  transfers between devices with their start and end apart: 27, of which 10 were waited for; matrix products, arithmetic and copies ran while one was open for 3% of the time, Pallas kernels for 59%

profile of v1, /device:TPU:0, one launch (start us, length us, event | category | flops | bytes accessed | tf_op | source)
XLA Modules:
  0.0 866.9 jit_solution(3044752907008855761)
XLA Ops:
  7.2 7.7 fusion.9
  27.6 105.1 %all-gather.9.cloned.1.call-done.h_ref = bf16[4096,2048]{1,0:T(8,128)(2,1)} async-done(((bf16[1024,2048]{1,0:T(8,128)(2,1)}), bf16[4096,2048]{1,0:T(8,128)(2,1)}) %all-gather.9.cloned.1.call-update) | async-done | bytes 16777232 | tf_op jit(solution)/shard_map/all_gather | solution.py:277
  132.7 32.5 %qkv.4 = (bf16[4096,512]{1,0:T(8,128)(2,1)}, bf16[4096,512]{1,0:T(8,128)(2,1)}, bf16[4096,512]{1,0:T(8,128)(2,1)}, bf16[65536,128]{1,0:T(8,128)(2,1)}, f32[2,4096]{1,0:T(2,128)}) custom-call(bf16[4096,2048]{1,0:T(8,128)(2,1)} %all-gather.9.cloned.1.call-done.h_ref, bf16[2048,512]{1,0:T(8,128)(2,1)} %wq_ref.7, bf16[2048,512]{1,0:T(8,128)(2,1)} %wk_ref.7, ...), custom_call_target="tpu_custom_call" | custom-call | flops 25769803776 | bytes 39845888 | tf_op jit(solution)/shard_map/qkv/pallas_call | solution.py:81
  165.5 7.8 fusion.14
  178.7 13.2 %rope.4 = (bf16[4096,512]{1,0:T(8,128)(2,1)}, bf16[4096,512]{1,0:T(8,128)(2,1)}, bf16[65536,128]{1,0:T(8,128)(2,1)}) custom-call(bf16[4096,512]{1,0:T(8,128)(2,1)} %get-tuple-element.51.q_ref, bf16[4096,512]{1,0:T(8,128)(2,1)} %get-tuple-element.52.k_ref, f32[2,4096]{1,0:T(2,128)} %add.84.ss_ref, f32[1,512]{1,0:T(1,128)} %bitcast.21, f32[1,512]{1,0:T(1,128)} %bitcast.25, ...), custom_call_target="tpu_custom_call" | custom-call | flops 7000000000 | bytes 20971520 | tf_op jit(solution)/shard_map/rope/pallas_call | solution.py:135
  191.9 72.0 %attn.4 = bf16[4096,512]{1,0:T(8,128)(2,1)} custom-call(bf16[4096,512]{1,0:T(8,128)(2,1)} %get-tuple-element.54.q_ref, bf16[4096,512]{1,0:T(8,128)(2,1)} %get-tuple-element.55.k_ref, bf16[4096,512]{1,0:T(8,128)(2,1)} %get-tuple-element.56.v_ref), custom_call_target="tpu_custom_call" | custom-call | flops 34359738368 | bytes 16777216 | tf_op jit(solution)/shard_map/attn/pallas_call | solution.py:204
  264.0 32.9 %qkv.5 = (bf16[4096,512]{1,0:T(8,128)(2,1)}, bf16[4096,512]{1,0:T(8,128)(2,1)}, bf16[4096,512]{1,0:T(8,128)(2,1)}, bf16[65536,128]{1,0:T(8,128)(2,1)}, f32[2,4096]{1,0:T(2,128)}) custom-call(bf16[4096,2048]{1,0:T(8,128)(2,1)} %all-gather.7.cloned.1.call-done.h_ref, bf16[2048,512]{1,0:T(8,128)(2,1)} %wq_ref.7, ...), custom_call_target="tpu_custom_call", output_to_operand_aliasing={{3}: (4, {})} | custom-call | flops 25769803776 | bytes 39845888 | tf_op jit(solution)/shard_map/qkv/pallas_call | solution.py:81
  304.5 13.2 %rope.5 = (bf16[4096,512]{1,0:T(8,128)(2,1)}, bf16[4096,512]{1,0:T(8,128)(2,1)}, bf16[65536,128]{1,0:T(8,128)(2,1)}) custom-call(bf16[4096,512]{1,0:T(8,128)(2,1)} %get-tuple-element.60.q_ref, bf16[4096,512]{1,0:T(8,128)(2,1)} %get-tuple-element.61.k_ref, f32[2,4096]{1,0:T(2,128)} %add.86.ss_ref, ...), custom_call_target="tpu_custom_call", output_to_operand_aliasing={{2}: (7, {})} | custom-call | flops 7000000000 | bytes 20971520 | tf_op jit(solution)/shard_map/rope/pallas_call | solution.py:135
  317.7 72.0 %attn.5 = bf16[4096,512]{1,0:T(8,128)(2,1)} custom-call(bf16[4096,512]{1,0:T(8,128)(2,1)} %get-tuple-element.64.q_ref, bf16[4096,512]{1,0:T(8,128)(2,1)} %get-tuple-element.65.k_ref, bf16[4096,512]{1,0:T(8,128)(2,1)} %get-tuple-element.66.v_ref), custom_call_target="tpu_custom_call" | custom-call | flops 34359738368 | bytes 16777216 | tf_op jit(solution)/shard_map/attn/pallas_call | solution.py:204
  389.7 32.6 %qkv.6 = (bf16[4096,512]{1,0:T(8,128)(2,1)}, bf16[4096,512]{1,0:T(8,128)(2,1)}, bf16[4096,512]{1,0:T(8,128)(2,1)}, bf16[65536,128]{1,0:T(8,128)(2,1)}, f32[2,4096]{1,0:T(2,128)}) custom-call(bf16[4096,2048]{1,0:T(8,128)(2,1)} %all-gather.5.cloned.1.call-done.h_ref, bf16[2048,512]{1,0:T(8,128)(2,1)} %wq_ref.7, ...), custom_call_target="tpu_custom_call", output_to_operand_aliasing={{3}: (4, {})} | custom-call | flops 25769803776 | bytes 39845888 | tf_op jit(solution)/shard_map/qkv/pallas_call | solution.py:81
  433.4 43.6 %collective-permute-done.7.o2 = bf16[1024,512]{1,0:T(8,128)(2,1)S(1)} collective-permute-done((bf16[1024,512]{1,0:T(8,128)(2,1)S(1)}, bf16[1024,512]{1,0:T(8,128)(2,1)S(1)}, u32[]{:S(2)}, u32[]{:S(2)}) %collective-permute-start.7) | collective-permute-done | bytes 1048608 | tf_op jit(solution)/shard_map/ppermute | solution.py:268
  478.5 42.8 %collective-permute-done.8.o3 = bf16[1024,512]{1,0:T(8,128)(2,1)S(1)} collective-permute-done((bf16[1024,512]{1,0:T(8,128)(2,1)S(1)}, bf16[1024,512]{1,0:T(8,128)(2,1)S(1)}, u32[]{:S(2)}, u32[]{:S(2)}) %collective-permute-start.8) | collective-permute-done | bytes 1048608 | tf_op jit(solution)/shard_map/ppermute | solution.py:268
  523.3 13.9 %outproj.4.refs_0_ = bf16[4,1024,2048]{2,1,0:T(8,128)(2,1)} custom-call(bf16[1024,512]{1,0:T(8,128)(2,1)} %get-tuple-element.75.o0, bf16[1024,512]{1,0:T(8,128)(2,1)} %copy-done.7, bf16[1024,512]{1,0:T(8,128)(2,1)} %copy-done.8, bf16[1024,512]{1,0:T(8,128)(2,1)} %copy-done.9, bf16[512,2048]{1,0:T(8,128)(2,1)} %w0.3, ...), custom_call_target="tpu_custom_call" | custom-call | flops 8589934592 | bytes 20971520 | tf_op jit(solution)/shard_map/outproj/pallas_call | solution.py:240
  537.2 13.3 %rope.6 = (bf16[4096,512]{1,0:T(8,128)(2,1)}, bf16[4096,512]{1,0:T(8,128)(2,1)}, bf16[65536,128]{1,0:T(8,128)(2,1)}) custom-call(bf16[4096,512]{1,0:T(8,128)(2,1)} %get-tuple-element.72.q_ref, bf16[4096,512]{1,0:T(8,128)(2,1)} %get-tuple-element.73.k_ref, f32[2,4096]{1,0:T(2,128)} %add.90.ss_ref, ...), custom_call_target="tpu_custom_call", output_to_operand_aliasing={{2}: (7, {})} | custom-call | flops 7000000000 | bytes 20971520 | tf_op jit(solution)/shard_map/rope/pallas_call | solution.py:135
  550.4 72.3 %attn.6 = bf16[4096,512]{1,0:T(8,128)(2,1)} custom-call(bf16[4096,512]{1,0:T(8,128)(2,1)} %get-tuple-element.79.q_ref, bf16[4096,512]{1,0:T(8,128)(2,1)} %get-tuple-element.80.k_ref, bf16[4096,512]{1,0:T(8,128)(2,1)} %get-tuple-element.81.v_ref), custom_call_target="tpu_custom_call" | custom-call | flops 34359738368 | bytes 16777216 | tf_op jit(solution)/shard_map/attn/pallas_call | solution.py:204
  622.7 32.6 %qkv.7 = (bf16[4096,512]{1,0:T(8,128)(2,1)}, bf16[4096,512]{1,0:T(8,128)(2,1)}, bf16[4096,512]{1,0:T(8,128)(2,1)}, bf16[65536,128]{1,0:T(8,128)(2,1)}, f32[2,4096]{1,0:T(2,128)}) custom-call(bf16[4096,2048]{1,0:T(8,128)(2,1)} %all-gather.11.cloned.1.call-done.h_ref, bf16[2048,512]{1,0:T(8,128)(2,1)} %wq_ref.7, ...), custom_call_target="tpu_custom_call", output_to_operand_aliasing={{3}: (4, {})} | custom-call | flops 25769803776 | bytes 39845888 | tf_op jit(solution)/shard_map/qkv/pallas_call | solution.py:81
  662.8 13.9 %outproj.5.refs_0_ = bf16[4,1024,2048]{2,1,0:T(8,128)(2,1)} custom-call(bf16[1024,512]{1,0:T(8,128)(2,1)} %get-tuple-element.88.o0, bf16[1024,512]{1,0:T(8,128)(2,1)} %copy-done.3, bf16[1024,512]{1,0:T(8,128)(2,1)} %collective-permute-done.15.o2, bf16[1024,512]{1,0:T(8,128)(2,1)} %collective-permute-done.16.o3, ...), custom_call_target="tpu_custom_call", output_to_operand_aliasing={{}: (9, {})} | custom-call | flops 8589934592 | bytes 20971520 | tf_op jit(solution)/shard_map/outproj/pallas_call | solution.py:240
  676.7 31.6 %collective-permute-done.13 = f32[2,4096]{1,0:T(2,128)S(1)} collective-permute-done((f32[2,4096]{1,0:T(2,128)S(1)}, f32[2,4096]{1,0:T(2,128)S(1)}, u32[]{:S(2)}, u32[]{:S(2)}) %collective-permute-start.13) | collective-permute-done | bytes 32800 | tf_op jit(solution)/shard_map/ppermute | solution.py:287
  708.9 13.2 %rope.7 = (bf16[4096,512]{1,0:T(8,128)(2,1)}, bf16[4096,512]{1,0:T(8,128)(2,1)}, bf16[65536,128]{1,0:T(8,128)(2,1)}) custom-call(bf16[4096,512]{1,0:T(8,128)(2,1)} %get-tuple-element.85.q_ref, bf16[4096,512]{1,0:T(8,128)(2,1)} %get-tuple-element.86.k_ref, f32[2,4096]{1,0:T(2,128)} %add.95.ss_ref, ...), custom_call_target="tpu_custom_call", output_to_operand_aliasing={{2}: (7, {})} | custom-call | flops 7000000000 | bytes 20971520 | tf_op jit(solution)/shard_map/rope/pallas_call | solution.py:135
  722.1 72.1 %attn.7 = bf16[4096,512]{1,0:T(8,128)(2,1)} custom-call(bf16[4096,512]{1,0:T(8,128)(2,1)} %get-tuple-element.92.q_ref, bf16[4096,512]{1,0:T(8,128)(2,1)} %get-tuple-element.93.k_ref, bf16[4096,512]{1,0:T(8,128)(2,1)} %get-tuple-element.94.v_ref), custom_call_target="tpu_custom_call" | custom-call | flops 34359738368 | bytes 16777216 | tf_op jit(solution)/shard_map/attn/pallas_call | solution.py:204
  801.4 13.9 %outproj.6.refs_0_ = bf16[4,1024,2048]{2,1,0:T(8,128)(2,1)} custom-call(bf16[1024,512]{1,0:T(8,128)(2,1)} %get-tuple-element.110.o0, bf16[1024,512]{1,0:T(8,128)(2,1)} %copy-done.4, bf16[1024,512]{1,0:T(8,128)(2,1)} %copy-done.5, bf16[1024,512]{1,0:T(8,128)(2,1)} %collective-permute-done.22.o3, ...), custom_call_target="tpu_custom_call", output_to_operand_aliasing={{}: (9, {})} | custom-call | flops 8589934592 | bytes 20971520 | tf_op jit(solution)/shard_map/outproj/pallas_call | solution.py:240
  815.2 9.3 %collective-permute-done.18.o2 = bf16[1024,512]{1,0:T(8,128)(2,1)} collective-permute-done((bf16[1024,512]{1,0:T(8,128)(2,1)}, bf16[1024,512]{1,0:T(8,128)(2,1)}, u32[]{:S(2)}, u32[]{:S(2)}) %collective-permute-start.18) | collective-permute-done | bytes 1048608 | tf_op jit(solution)/shard_map/ppermute | solution.py:268
  824.5 21.5 %collective-permute-done.19.o3 = bf16[1024,512]{1,0:T(8,128)(2,1)} collective-permute-done((bf16[1024,512]{1,0:T(8,128)(2,1)}, bf16[1024,512]{1,0:T(8,128)(2,1)}, u32[]{:S(2)}, u32[]{:S(2)}) %collective-permute-start.19) | collective-permute-done | bytes 1048608 | tf_op jit(solution)/shard_map/ppermute | solution.py:268
  846.1 13.9 %outproj.7 = bf16[4,1024,2048]{2,1,0:T(8,128)(2,1)} custom-call(bf16[1024,512]{1,0:T(8,128)(2,1)} %get-tuple-element.114.o0, bf16[1024,512]{1,0:T(8,128)(2,1)} %copy-done.6, bf16[1024,512]{1,0:T(8,128)(2,1)} %collective-permute-done.18.o2, bf16[1024,512]{1,0:T(8,128)(2,1)} %collective-permute-done.19.o3, ...), custom_call_target="tpu_custom_call", output_to_operand_aliasing={{}: (9, {})} | custom-call | flops 8589934592 | bytes 20971520 | tf_op jit(solution)/shard_map/outproj/pallas_call | solution.py:240
  (95 shorter events, 55.6 us)
Async XLA Ops:
  7.2 125.5 %all-gather.9.cloned.1.call-start = ((), (), s32[]{:S(2)}) async-start(), calls=%async_computation.2 | async-start | bytes 20971520 | tf_op jit(solution)/shard_map/all_gather | solution.py:277
  25.5 238.5 %all-gather.7.cloned.1.call-start = ((), (), s32[]{:S(2)}) async-start(), calls=%async_computation.1 | async-start | bytes 20971520 | tf_op jit(solution)/shard_map/all_gather | solution.py:277
  26.3 363.5 %all-gather.5.cloned.1.call-start = ((), (), s32[]{:S(2)}) async-start(), calls=%async_computation | async-start | bytes 20971520 | tf_op jit(solution)/shard_map/all_gather | solution.py:277
  27.0 595.7 %all-gather.11.cloned.1.call-start = ((), (), s32[]{:S(2)}) async-start(), calls=%async_computation.3 | async-start | bytes 20971520 | tf_op jit(solution)/shard_map/all_gather | solution.py:277
  165.2 8.1 collective-permute-start
  173.3 4.8 collective-permute-start.1
  298.8 5.0 collective-permute-start.3
  299.3 90.4 %collective-permute-start.10 = (bf16[512,2048]{1,0:T(8,128)(2,1)S(1)}, bf16[512,2048]{1,0:T(8,128)(2,1)}, u32[]{:S(2)}, u32[]{:S(2)}) collective-permute-start(bf16[512,2048]{1,0:T(8,128)(2,1)S(1)} %copy-done.1), channel_id=1, source_target_pairs={{0,2},{1,3},{2,0},{3,1},{4,6},{5,7},{6,4},{7,5}} | collective-permute-start | bytes 6291464 | tf_op jit(solution)/shard_map/ppermute | solution.py:290
  300.9 222.3 %collective-permute-start.9 = (bf16[512,2048]{1,0:T(8,128)(2,1)S(1)}, bf16[512,2048]{1,0:T(8,128)(2,1)}, u32[]{:S(2)}, u32[]{:S(2)}) collective-permute-start(bf16[512,2048]{1,0:T(8,128)(2,1)S(1)} %copy-done.1), channel_id=1, source_target_pairs={{0,1},{1,0},{2,3},{3,2},{4,5},{5,4},{6,7},{7,6}} | collective-permute-start | bytes 6291464 | tf_op jit(solution)/shard_map/ppermute | solution.py:291
  389.7 133.5 %collective-permute-start.11 = (bf16[512,2048]{1,0:T(8,128)(2,1)}, bf16[512,2048]{1,0:T(8,128)(2,1)}, u32[]{:S(2)}, u32[]{:S(2)}) collective-permute-start(bf16[512,2048]{1,0:T(8,128)(2,1)} %collective-permute-done.10.w2), channel_id=1, source_target_pairs={{0,1},{1,0},{2,3},{3,2},{4,5},{5,4},{6,7},{7,6}} | collective-permute-start | bytes 6291464 | tf_op jit(solution)/shard_map/ppermute | solution.py:291
  424.4 5.5 collective-permute-start.5
  428.5 48.5 %collective-permute-start.7 = (bf16[1024,512]{1,0:T(8,128)(2,1)S(1)}, bf16[1024,512]{1,0:T(8,128)(2,1)S(1)}, u32[]{:S(2)}, u32[]{:S(2)}) collective-permute-start(bf16[1024,512]{1,0:T(8,128)(2,1)S(1)} %get-tuple-element.120), channel_id=1, source_target_pairs={{0,2},{1,3},{2,0},{3,1},{4,6},{5,7},{6,4},{7,5}} | collective-permute-start | bytes 3145736 | tf_op jit(solution)/shard_map/ppermute | solution.py:268
  430.0 91.3 %collective-permute-start.8 = (bf16[1024,512]{1,0:T(8,128)(2,1)S(1)}, bf16[1024,512]{1,0:T(8,128)(2,1)S(1)}, u32[]{:S(2)}, u32[]{:S(2)}) collective-permute-start(bf16[1024,512]{1,0:T(8,128)(2,1)S(1)} %get-tuple-element.119), channel_id=1, source_target_pairs={{0,3},{1,2},{2,1},{3,0},{4,7},{5,6},{6,5},{7,4}} | collective-permute-start | bytes 3145736 | tf_op jit(solution)/shard_map/ppermute | solution.py:268
  433.1 227.9 %collective-permute-start.14 = (bf16[1024,512]{1,0:T(8,128)(2,1)}, bf16[1024,512]{1,0:T(8,128)(2,1)S(1)}, u32[]{:S(2)}, u32[]{:S(2)}) collective-permute-start(bf16[1024,512]{1,0:T(8,128)(2,1)} %get-tuple-element.117), channel_id=1, source_target_pairs={{0,1},{1,0},{2,3},{3,2},{4,5},{5,4},{6,7},{7,6}} | collective-permute-start | bytes 3145736 | tf_op jit(solution)/shard_map/ppermute | solution.py:268
  477.0 184.5 %collective-permute-start.15 = (bf16[1024,512]{1,0:T(8,128)(2,1)}, bf16[1024,512]{1,0:T(8,128)(2,1)}, u32[]{:S(2)}, u32[]{:S(2)}) collective-permute-start(bf16[1024,512]{1,0:T(8,128)(2,1)} %get-tuple-element.116), channel_id=1, source_target_pairs={{0,2},{1,3},{2,0},{3,1},{4,6},{5,7},{6,4},{7,5}} | collective-permute-start | bytes 3145736 | tf_op jit(solution)/shard_map/ppermute | solution.py:268
  521.3 141.5 %collective-permute-start.16 = (bf16[1024,512]{1,0:T(8,128)(2,1)}, bf16[1024,512]{1,0:T(8,128)(2,1)}, u32[]{:S(2)}, u32[]{:S(2)}) collective-permute-start(bf16[1024,512]{1,0:T(8,128)(2,1)} %get-tuple-element.115), channel_id=1, source_target_pairs={{0,3},{1,2},{2,1},{3,0},{4,7},{5,6},{6,5},{7,4}} | collective-permute-start | bytes 3145736 | tf_op jit(solution)/shard_map/ppermute | solution.py:268
  655.3 4.7 collective-permute-start.12
  659.5 140.3 %collective-permute-start.20 = (bf16[1024,512]{1,0:T(8,128)(2,1)}, bf16[1024,512]{1,0:T(8,128)(2,1)S(1)}, u32[]{:S(2)}, u32[]{:S(2)}) collective-permute-start(bf16[1024,512]{1,0:T(8,128)(2,1)} %get-tuple-element.109), channel_id=1, source_target_pairs={{0,1},{1,0},{2,3},{3,2},{4,5},{5,4},{6,7},{7,6}} | collective-permute-start | bytes 3145736 | tf_op jit(solution)/shard_map/ppermute | solution.py:268
  660.0 140.4 %collective-permute-start.21 = (bf16[1024,512]{1,0:T(8,128)(2,1)}, bf16[1024,512]{1,0:T(8,128)(2,1)S(1)}, u32[]{:S(2)}, u32[]{:S(2)}) collective-permute-start(bf16[1024,512]{1,0:T(8,128)(2,1)} %get-tuple-element.108), channel_id=1, source_target_pairs={{0,2},{1,3},{2,0},{3,1},{4,6},{5,7},{6,4},{7,5}} | collective-permute-start | bytes 3145736 | tf_op jit(solution)/shard_map/ppermute | solution.py:268
  660.9 139.5 %collective-permute-start.22 = (bf16[1024,512]{1,0:T(8,128)(2,1)}, bf16[1024,512]{1,0:T(8,128)(2,1)}, u32[]{:S(2)}, u32[]{:S(2)}) collective-permute-start(bf16[1024,512]{1,0:T(8,128)(2,1)} %get-tuple-element.107), channel_id=1, source_target_pairs={{0,3},{1,2},{2,1},{3,0},{4,7},{5,6},{6,5},{7,4}} | collective-permute-start | bytes 3145736 | tf_op jit(solution)/shard_map/ppermute | solution.py:268
  661.5 46.8 %collective-permute-start.13 = (f32[2,4096]{1,0:T(2,128)S(1)}, f32[2,4096]{1,0:T(2,128)S(1)}, u32[]{:S(2)}, u32[]{:S(2)}) collective-permute-start(f32[2,4096]{1,0:T(2,128)S(1)} %add.94), channel_id=1, source_target_pairs={{0,2},{1,3},{2,0},{3,1},{4,6},{5,7},{6,4},{7,5}} | collective-permute-start | bytes 98312 | tf_op jit(solution)/shard_map/ppermute | solution.py:287
  798.5 16.7 %collective-permute-start.17 = (bf16[1024,512]{1,0:T(8,128)(2,1)}, bf16[1024,512]{1,0:T(8,128)(2,1)S(1)}, u32[]{:S(2)}, u32[]{:S(2)}) collective-permute-start(bf16[1024,512]{1,0:T(8,128)(2,1)} %get-tuple-element.113), channel_id=1, source_target_pairs={{0,1},{1,0},{2,3},{3,2},{4,5},{5,4},{6,7},{7,6}} | collective-permute-start | bytes 3145736 | tf_op jit(solution)/shard_map/ppermute | solution.py:268
  798.5 26.0 %collective-permute-start.18 = (bf16[1024,512]{1,0:T(8,128)(2,1)}, bf16[1024,512]{1,0:T(8,128)(2,1)}, u32[]{:S(2)}, u32[]{:S(2)}) collective-permute-start(bf16[1024,512]{1,0:T(8,128)(2,1)} %get-tuple-element.112), channel_id=1, source_target_pairs={{0,2},{1,3},{2,0},{3,1},{4,6},{5,7},{6,4},{7,5}} | collective-permute-start | bytes 3145736 | tf_op jit(solution)/shard_map/ppermute | solution.py:268
  799.8 46.3 %collective-permute-start.19 = (bf16[1024,512]{1,0:T(8,128)(2,1)}, bf16[1024,512]{1,0:T(8,128)(2,1)}, u32[]{:S(2)}, u32[]{:S(2)}) collective-permute-start(bf16[1024,512]{1,0:T(8,128)(2,1)} %get-tuple-element.111), channel_id=1, source_target_pairs={{0,3},{1,2},{2,1},{3,0},{4,7},{5,6},{6,5},{7,4}} | collective-permute-start | bytes 3145736 | tf_op jit(solution)/shard_map/ppermute | solution.py:268
  (16 other events, 253.6 us)
Sparse Core Ops, SparseCore 0:
  25.6 107.0 all-gather.8
  134.8 104.8 all-gather.6
  241.2 146.1 all-gather.4
  388.8 165.4 all-gather.10

commit v2 on v1

v2 whole, which is shorter than its diff:
```python
import functools
import math

import jax
import jax.numpy as jnp
from jax import lax
from jax.experimental import pallas as pl
from jax.experimental.pallas import tpu as pltpu
from jax.sharding import PartitionSpec as P


HD = 128
LOG2E = math.log2(math.e)
F32 = jnp.float32
BF16 = jnp.bfloat16
VMEM_LIMIT = 60 * 1024 * 1024


def params(*sem):
    return pltpu.CompilerParams(dimension_semantics=sem, vmem_limit_bytes=VMEM_LIMIT)


def cost(flops, nbytes, trans=0):
    return pl.CostEstimate(flops=int(flops), bytes_accessed=int(nbytes), transcendentals=int(trans))


def rope_tables(seq_len):
    half_dim = HD // 2
    inv_freq = 10000.0 ** (-jnp.arange(half_dim, dtype=F32) * (2.0 / HD))
    angles = jnp.arange(seq_len, dtype=F32)[:, None] * inv_freq[None, :]
    c, s = jnp.cos(angles), jnp.sin(angles)
    return jnp.concatenate([c, c], axis=1), jnp.concatenate([-s, s], axis=1)


def sq_sum(a):
    part = None
    for g in range(a.shape[1] // HD):
        t = a[:, g * HD:(g + 1) * HD]
        part = t * t if part is None else part + t * t
    return jnp.sum(part.T, axis=0, keepdims=True)


def spread_heads(scr, blocks):
    n = len(blocks)
    rows = blocks[0].shape[0]
    for g, t in enumerate(blocks):
        scr[pl.ds(g, rows, stride=n), :] = t
    return scr[...].astype(BF16)


def qkv_kernel(me_ref, ha_ref, hb_ref, wq_ref, wk_ref, wv_ref, *refs):
    q_ref, k_ref, vt_ref, vc_ref, ss_ref, scr = refs[-6:]
    h = jnp.where(pl.program_id(0) == 0, ha_ref[...], hb_ref[...])
    cols = wq_ref.shape[1]
    q = jnp.dot(h, wq_ref[...], preferred_element_type=F32).astype(BF16)
    q_ref[...] = q
    k = jnp.dot(h, wk_ref[...], preferred_element_type=F32).astype(BF16)
    k_ref[...] = k
    ss_ref[0:1, :] = sq_sum(q.astype(F32))
    v = jnp.dot(h, wv_ref[...], preferred_element_type=F32)
    ss_ref[1:2, :] = sq_sum(k.astype(F32))
    vt_ref[...] = v.T.astype(BF16)
    vc_ref[...] = spread_heads(scr, [v[:, g * HD:(g + 1) * HD] for g in range(cols // HD)])


def qkv_call(me, ha, hb, ws, r0, bufs, vc_prev, b, n_batch, seq):
    rows, width = ha.shape
    cols = ws[0].shape[1]
    heads = cols // HD
    bq = 512
    nq = rows // bq
    base = b * (seq // bq)

    def pos(c, i, m):
        return (m[0] ^ (r0 + c)) * nq + i

    wspec = pl.BlockSpec((width, cols), lambda c, i, m: (0, 0))
    rspec = pl.BlockSpec((bq, cols), lambda c, i, m: (pos(c, i, m), 0))
    in_specs = [
        pl.BlockSpec((bq, width), lambda c, i, m: (jnp.where(c == 0, i, nq - 1), 0)),
        pl.BlockSpec((bq, width), lambda c, i, m: (jnp.where(c == 0, 0, i), 0)),
        wspec, wspec, wspec,
    ]
    args = [me, ha, hb, *ws]
    aliases = {}
    for n, buf in enumerate([*(bufs or [None] * 4)[:3], vc_prev, (bufs or [None] * 4)[3]]):
        if buf is not None:
            aliases[len(args)] = n
            args.append(buf)
            in_specs.append(pl.BlockSpec(memory_space=pl.ANY))
    q, k, vt, vc, ss = pl.pallas_call(
        qkv_kernel,
        grid_spec=pltpu.PrefetchScalarGridSpec(
            num_scalar_prefetch=1,
            grid=(2, nq),
            in_specs=in_specs,
            out_specs=[
                rspec, rspec,
                pl.BlockSpec((cols, bq), lambda c, i, m: (0, pos(c, i, m))),
                pl.BlockSpec((bq * heads, HD), lambda c, i, m: (base + pos(c, i, m), 0)),
                pl.BlockSpec((2, bq), lambda c, i, m: (0, pos(c, i, m))),
            ],
            scratch_shapes=[pltpu.VMEM((bq * heads, HD), F32)],
        ),
        out_shape=[
            jax.ShapeDtypeStruct((seq, cols), BF16), jax.ShapeDtypeStruct((seq, cols), BF16), jax.ShapeDtypeStruct((cols, seq), BF16),
            jax.ShapeDtypeStruct((n_batch * seq * heads, HD), BF16), jax.ShapeDtypeStruct((2, seq), F32),
        ],
        input_output_aliases=aliases,
        compiler_params=params("arbitrary", "arbitrary"),
        cost_estimate=cost(12 * rows * width * cols, 4 * rows * width + 6 * width * cols + 16 * rows * cols),
        name="qkv",
    )(*args)
    return [q, k, vt, ss], vc


def rope_kernel(width, q_ref, k_ref, ss_ref, qg_ref, kg_ref, c_ref, s_ref, *refs):
    qr_ref, kr_ref, kc_ref, scr = refs[-4:]
    ct, st = c_ref[...], s_ref[...]
    rows = q_ref.shape[0]
    inv = lax.rsqrt(ss_ref[...] * (1.0 / width) + 1e-5)
    inv_t = jnp.concatenate([inv, jnp.zeros((6, rows), F32)], axis=0).T

    def turn(x_ref, col, g_ref):
        scale = inv_t[:, col:col + 1]
        outs = []
        for g in range(x_ref.shape[1] // HD):
            sl = slice(g * HD, (g + 1) * HD)
            n = x_ref[:, sl].astype(F32) * scale * g_ref[:, sl]
            outs.append(n * ct + pltpu.roll(n, HD // 2, 1) * st)
        return outs

    for g, t in enumerate(turn(q_ref, 0, qg_ref)):
        qr_ref[:, g * HD:(g + 1) * HD] = t.astype(BF16)
    ks = turn(k_ref, 1, kg_ref)
    for g, t in enumerate(ks):
        kr_ref[:, g * HD:(g + 1) * HD] = t.astype(BF16)
    kc_ref[...] = spread_heads(scr, ks)


def rope_call(q, k, ss, qg, kg, ct, st, kc_prev, b, n_batch, width):
    seq, cols = q.shape
    heads = cols // HD
    bq = 512
    nq = seq // bq
    rspec = pl.BlockSpec((bq, cols), lambda i: (i, 0))
    tspec = pl.BlockSpec((bq, HD), lambda i: (i, 0))
    gspec = pl.BlockSpec((1, cols), lambda i: (0, 0))
    in_specs = [rspec, rspec, pl.BlockSpec((2, bq), lambda i: (0, i)), gspec, gspec, tspec, tspec]
    args = [q, k, ss, qg, kg, ct, st]
    aliases = {}
    if kc_prev is not None:
        in_specs.append(pl.BlockSpec(memory_space=pl.ANY))
        args.append(kc_prev)
        aliases = {7: 2}
    base = b * nq
    return pl.pallas_call(
        functools.partial(rope_kernel, width),
        grid=(nq,),
        in_specs=in_specs,
        out_specs=[rspec, rspec, pl.BlockSpec((bq * heads, HD), lambda i: (base + i, 0))],
        out_shape=[jax.ShapeDtypeStruct((seq, cols), BF16)] * 2 + [jax.ShapeDtypeStruct((n_batch * seq * heads, HD), BF16)],
        scratch_shapes=[pltpu.VMEM((bq * heads, HD), F32)],
        input_output_aliases=aliases,
        compiler_params=params("arbitrary"),
        cost_estimate=cost(7e9, 10 * seq * cols),
        name="rope",
    )(*args)


def attn_kernel(n_h, bq, ch, q_ref, k_ref, vt_ref, o_ref, l_s, acc_s, m_s, *stage_refs):
    s_s, mx_s = stage_refs[:n_h], stage_refs[n_h:]
    i = pl.program_id(1)
    c = HD ** -0.5 * LOG2E
    n_c = bq // ch

    def heads(g):
        return slice(g * HD, (g + 1) * HD)

    def span(j, t):
        return pl.ds(pl.multiple_of(j * bq + t * ch, ch), ch)

    def score_chunk(g, j, t, diag, top):
        s = lax.dot_general(k_ref[span(j, t), heads(g)], q_ref[:, heads(g)], (((1,), (1,)), ((), ())), preferred_element_type=F32)
        if diag:
            k_pos = lax.broadcasted_iota(jnp.int32, (ch, bq), 0) + t * ch
            s = jnp.where(lax.broadcasted_iota(jnp.int32, (ch, bq), 1) >= k_pos, s, -1e30)
        s_s[g][t * ch:(t + 1) * ch, :] = s
        part = jnp.max(s.reshape(ch // 8, 8, bq), axis=0)
        return part if top is None else jnp.maximum(top, part)

    def stage(g, j, first, g_next, j_next, diag_next):
        m_new = jnp.max(mx_s[g][...], axis=0, keepdims=True) * c
        if not first:
            m_old = m_s[g]
            m_new = jnp.maximum(m_old, m_new)
            alpha = jnp.exp2(m_old - m_new)
        m_s[g] = m_new
        top = l_new = pv = None
        for t in range(n_c):
            top = score_chunk(g_next, j_next, t, diag_next, top)
            p = jnp.exp2(s_s[g][t * ch:(t + 1) * ch, :] * c - m_new)
            part = jnp.sum(p.reshape(ch // 8, 8, bq), axis=0)
            l_new = part if l_new is None else l_new + part
            part = jnp.dot(vt_ref[heads(g), span(j, t)], p.astype(BF16), preferred_element_type=F32)
            pv = part if pv is None else pv + part
        mx_s[g_next][...] = top
        if first:
            l_s[g] = l_new
            acc_s[g] = pv
        else:
            l_s[g] = l_s[g] * alpha + l_new
            acc_s[g] = acc_s[g] * alpha + pv

    top = None
    for t in range(n_c):
        top = score_chunk(0, i, t, True, top)
    mx_s[0][...] = top
    for g in range(n_h):
        last = g == n_h - 1
        stage(g, i, True, 0 if last else g + 1, 0 if last else i, not last)

    def body(j, carry):
        for g in range(n_h):
            last = g == n_h - 1
            stage(g, j, False, 0 if last else g + 1, jnp.minimum(j + 1, i - 1) if last else j, False)
        return carry

    lax.fori_loop(0, i, body, 0)
    for g in range(n_h):
        l = jnp.sum(l_s[g], axis=0, keepdims=True)
        o_ref[:, heads(g)] = (acc_s[g] / l).T.astype(BF16)


def attn_call(q, k, vt):
    seq, cols = q.shape
    bq, ch, n_h = 512, 256, min(4, cols // HD)
    qspec = pl.BlockSpec((bq, n_h * HD), lambda h, i: (i, h))
    return pl.pallas_call(
        functools.partial(attn_kernel, n_h, bq, ch),
        grid=(cols // (n_h * HD), seq // bq),
        in_specs=[qspec, pl.BlockSpec((seq, n_h * HD), lambda h, i: (0, h)), pl.BlockSpec((n_h * HD, seq), lambda h, i: (h, 0))],
        out_specs=qspec,
        out_shape=jax.ShapeDtypeStruct((seq, cols), BF16),
        scratch_shapes=[pltpu.VMEM((n_h, 8, bq), F32), pltpu.VMEM((n_h, HD, bq), F32), pltpu.VMEM((n_h, 1, bq), F32)]
        + [pltpu.VMEM((bq, bq), F32)] * n_h + [pltpu.VMEM((8, bq), F32)] * n_h,
        compiler_params=params("arbitrary", "arbitrary"),
        cost_estimate=cost(4 * seq * seq * cols, 8 * seq * cols, seq * seq * cols // HD // 2),
        name="attn",
    )(q, k, vt)


def out_kernel(o0, o1, o2, o3, w0, w1, w2, w3, x_ref, *refs):
    out_ref = refs[-1]
    acc = jnp.dot(o0[...], w0[...], preferred_element_type=F32)
    for o, w in ((o1, w1), (o2, w2), (o3, w3)):
        acc += jnp.dot(o[...], w[...], preferred_element_type=F32)
    y = acc.astype(BF16).astype(F32)
    out_ref[0] = (x_ref[0].astype(F32) + y).astype(BF16)


def out_call(os, ws, x, prev, b):
    _, rows, width = x.shape
    cols = os[0].shape[1]
    bn = 512
    ospec = pl.BlockSpec((rows, cols), lambda n: (0, 0))
    wspec = pl.BlockSpec((cols, bn), lambda n: (0, n))
    xspec = pl.BlockSpec((1, rows, bn), lambda n: (b, 0, n))
    in_specs = [ospec] * 4 + [wspec] * 4 + [xspec]
    args = [*os, *ws, x]
    aliases = {}
    if prev is not None:
        in_specs.append(pl.BlockSpec(memory_space=pl.ANY))
        args.append(prev)
        aliases = {9: 0}
    return pl.pallas_call(
        out_kernel,
        grid=(width // bn,),
        in_specs=in_specs,
        out_specs=xspec,
        out_shape=jax.ShapeDtypeStruct(x.shape, BF16),
        input_output_aliases=aliases,
        compiler_params=params("arbitrary"),
        cost_estimate=cost(2 * rows * width * width, 2 * (width * width + 3 * rows * width)),
        name="outproj",
    )(*args)


def solution(mesh):
    n_tp = mesh.shape['tp']
    pairs = {r: [(d, d ^ r) for d in range(n_tp)] for r in range(1, n_tp)}

    def block(x_local, attn_gain, wq, wk, wv, qg, kg, wo_rows):
        n_batch, rows, width = x_local.shape
        seq = rows * n_tp
        cols = wq.shape[1]
        me = lax.axis_index('tp')
        ct, st = rope_tables(seq)

        qg, kg = qg.reshape(1, cols), kg.reshape(1, cols)
        me_arr = me.astype(jnp.int32).reshape(1)
        w_qkv = [wq, wk, wv]

        def after(val, *deps):
            return lax.optimization_barrier((val, *deps))[0]

        def send(val, hop):
            return lax.ppermute(val, 'tp', pairs[hop])

        own = []
        for b in range(n_batch):
            xf = (x_local if b == 0 else after(x_local, own[0]))[b].astype(F32)
            inv_rms = lax.rsqrt(jnp.mean(xf * xf, axis=-1, keepdims=True) + 1e-5)
            own.append((xf * inv_rms * attn_gain).astype(BF16))
        far = [send(own[b], 2) for b in range(2)]
        near = [send(h, 1) for h in own]
        bufs, late, ex, stats = [], [], [], []
        vc = kc = out = ws = None

        def early(b, h1, vc):
            buf, vc = qkv_call(me_arr, own[b], h1, w_qkv, 0, None, vc, b, n_batch, seq)
            bufs.append(buf)
            return vc

        def project(b, vc, *deps):
            h2 = after(far[b], *deps)
            h3 = send(h2, 1)
            buf, vc = qkv_call(me_arr, h2, h3, w_qkv, 2, bufs[b], vc, b, n_batch, seq)
            late.append(buf)
            stats.append(send(buf[3], 2))
            return vc

        def attend(b, kc, *deps):
            q, k, vt, ss = late[b]
            pair_ss = after(stats[b], *deps) + ss
            tot = pair_ss + send(pair_ss, 1)
            qr, kr, kc = rope_call(q, k, tot, qg, kg, ct, st, kc, b, n_batch, width)
            o = attn_call(qr, kr, vt)
            return o, kc

        def exchange(o, *deps):
            pos = []
            for r in range(n_tp):
                piece = lax.dynamic_slice_in_dim(o, (me ^ r) * rows, rows, axis=0)
                pos.append(piece if r == 0 else send(after(piece, *deps), r))
            ex.append(pos)

        for b in range(3):
            vc = early(b, near[b] if b == 0 else after(near[b], vc), vc)
        vc = project(0, vc, vc)
        far.append(send(after(own[2], late[0][3]), 2))
        vc = early(3, after(near[3], vc), vc)
        vc = project(1, vc, vc)
        far.append(send(after(own[3], late[1][3]), 2))
        o0, kc = attend(0, kc, late[1][3])
        vc = project(2, vc, o0)
        w2 = send(after(wo_rows, late[2][3]), 2)
        ws = [wo_rows, send(after(wo_rows, late[2][3]), 1), w2]
        o1, kc = attend(1, kc, late[2][3])
        vc = project(3, vc, o1)
        exchange(o0, late[3][3])
        exchange(o1, late[3][3])
        o2, kc = attend(2, kc, late[3][3])
        exchange(o2)
        ws.append(send(after(w2, o2), 1))
        o3, kc = attend(3, kc, o2)
        exchange(o3)
        for b, pos in enumerate(ex):
            pos[0] = after(pos[0], o3)
            out = out_call(pos, ws, x_local, out, b)
        shape = (n_batch, seq, cols // HD, HD)
        return (out, kc.reshape(shape), vc.reshape(shape))

    seq_spec = P('dp', 'tp', None)
    head_spec = P('dp', None, 'tp', None)
    col_spec = P(None, 'tp')
    return jax.shard_map(block, mesh=mesh, in_specs=(seq_spec, P(None), col_spec, col_spec, col_spec, P('tp'), P('tp'), P('tp', None)), out_specs=(seq_spec, head_spec, head_spec), check_vma=False)
```

time: 871 us -> 716 us (0.82)
  waiting for transfers between devices: 262 us -> 143 us
  Pallas kernels: 527 us -> 482 us
  between operations: 14.4 us -> 1.02 us
  starting transfers between devices: 14.6 us -> 24.4 us
    all_gather x4 -> x0, waiting for transfers between devices: 105 us -> none  [local_block(): hs.append(lax.all_gather(normed, 'tp', axis=0, tiled=True))]
    pallas_call x8 -> x12, Pallas kernels: 419 us -> 373 us  [the longest x4 215 us: attn_call(): pl.pallas_call(functools.partial(attn_kernel, n_h, bq, ch), grid=(cols //...]
    ppermute x23 -> x35, waiting for transfers between devices: 155 us -> 143 us  [send(): return lax.ppermute(val, 'tp', pairs[hop])]
    ppermute x23 -> x35, starting transfers between devices: 14.3 us -> 24.4 us  [send(): return lax.ppermute(val, 'tp', pairs[hop])]
  transfers between devices with their start and end apart: 27 -> 35, of which waited for: 10 -> 10; matrix products, arithmetic and copies ran while one was open for 3% -> 7% of each run, Pallas kernels for 59% -> 66%
where the time goes in v2:
time: 716 us; the launch traced here: 706 us
  Pallas kernels  482 us (67%)
  waiting for transfers between devices  143 us (20%)
  other arithmetic  37.7 us (5%)
  starting transfers between devices  24.4 us (3%)
  local copies, waits for them, and re-layouts  18.4 us (3%)
    pallas_call x4, Pallas kernels, attn_call(): pl.pallas_call(functools.partial(attn_kernel, n_h, bq, ch), grid=(cols //...  215 us
    pallas_call x8, Pallas kernels, qkv_call(): pl.pallas_call(qkv_kernel, grid_spec=pltpu.PrefetchScalarGridSpec(num_sca...  159 us
    ppermute x35, waiting for transfers between devices, send(): return lax.ppermute(val, 'tp', pairs[hop])  143 us
    pallas_call x4, Pallas kernels, out_call(): pl.pallas_call(out_kernel, grid=(width // bn,), in_specs=in_specs, out_sp...  55.6 us
    pallas_call x4, Pallas kernels, rope_call(): pl.pallas_call(functools.partial(rope_kernel, width), grid=(nq,), in_spec...  53 us
    ppermute x35, starting transfers between devices, send(): return lax.ppermute(val, 'tp', pairs[hop])  24.4 us
    dynamic_slice x4, local copies, waits for them, and re-layouts, exchange(): piece = lax.dynamic_slice_in_dim(o, (me ^ r) * rows, rows, axis=0)  17 us
  transfers between devices with their start and end apart: 35, of which 10 were waited for; matrix products, arithmetic and copies ran while one was open for 7% of the time, Pallas kernels for 66%

profile of v2, /device:TPU:0, one launch (start us, length us, event | category | flops | bytes accessed | tf_op | source)
XLA Modules:
  0.0 706.1 jit_solution(2930116763498359487)
XLA Ops:
  25.7 19.7 %qkv.8 = (bf16[4096,512]{1,0:T(8,128)(2,1)}, bf16[4096,512]{1,0:T(8,128)(2,1)}, bf16[512,4096]{1,0:T(8,128)(2,1)}, bf16[65536,128]{1,0:T(8,128)(2,1)}, f32[2,4096]{1,0:T(2,128)}) custom-call(s32[1]{0:T(128)} %bitcast.me_ref, bf16[1024,2048]{1,0:T(8,128)(2,1)} %fusion.2.ha_ref, bf16[1024,2048]{1,0:T(8,128)(2,1)} %collective-permute-done.5.hb_ref, ...), custom_call_target="tpu_custom_call" | custom-call | flops 12884901888 | bytes 23068672 | tf_op jit(solution)/shard_map/qkv/pallas_call | solution.py:91
  45.4 19.8 %qkv.9 = (bf16[4096,512]{1,0:T(8,128)(2,1)}, bf16[4096,512]{1,0:T(8,128)(2,1)}, bf16[512,4096]{1,0:T(8,128)(2,1)}, bf16[65536,128]{1,0:T(8,128)(2,1)}, f32[2,4096]{1,0:T(2,128)}) custom-call(s32[1]{0:T(128)} %bitcast.me_ref, bf16[1024,2048]{1,0:T(8,128)(2,1)} %get-tuple-element.164.ha_ref, ...), custom_call_target="tpu_custom_call", output_to_operand_aliasing={{3}: (6, {})} | custom-call | flops 12884901888 | bytes 23068672 | tf_op jit(solution)/shard_map/qkv/pallas_call | solution.py:91
  65.2 19.7 %qkv.10 = (bf16[4096,512]{1,0:T(8,128)(2,1)}, bf16[4096,512]{1,0:T(8,128)(2,1)}, bf16[512,4096]{1,0:T(8,128)(2,1)}, bf16[65536,128]{1,0:T(8,128)(2,1)}, f32[2,4096]{1,0:T(2,128)}) custom-call(s32[1]{0:T(128)} %bitcast.me_ref, bf16[1024,2048]{1,0:T(8,128)(2,1)} %get-tuple-element.105.ha_ref, ...), custom_call_target="tpu_custom_call", output_to_operand_aliasing={{3}: (6, {})} | custom-call | flops 12884901888 | bytes 23068672 | tf_op jit(solution)/shard_map/qkv/pallas_call | solution.py:91
  85.0 31.8 %collective-permute-done.2.ha_ref = bf16[1024,2048]{1,0:T(8,128)(2,1)} collective-permute-done((bf16[1024,2048]{1,0:T(8,128)(2,1)}, bf16[1024,2048]{1,0:T(8,128)(2,1)}, u32[]{:S(2)}, u32[]{:S(2)}) %collective-permute-start.2) | collective-permute-done | bytes 4194336 | tf_op jit(solution)/shard_map/ppermute | solution.py:308
  124.2 19.9 %qkv.11 = (bf16[4096,512]{1,0:T(8,128)(2,1)}, bf16[4096,512]{1,0:T(8,128)(2,1)}, bf16[512,4096]{1,0:T(8,128)(2,1)}, bf16[65536,128]{1,0:T(8,128)(2,1)}, f32[2,4096]{1,0:T(2,128)}) custom-call(s32[1]{0:T(128)} %bitcast.me_ref, ...), custom_call_target="tpu_custom_call", output_to_operand_aliasing={{0}: (6, {}), {1}: (7, {}), {2}: (8, {}), {3}: (9, {}), {4}... | custom-call | flops 12884901888 | bytes 23068672 | tf_op jit(solution)/shard_map/qkv/pallas_call | solution.py:91
  144.1 19.8 %qkv.12 = (bf16[4096,512]{1,0:T(8,128)(2,1)}, bf16[4096,512]{1,0:T(8,128)(2,1)}, bf16[512,4096]{1,0:T(8,128)(2,1)}, bf16[65536,128]{1,0:T(8,128)(2,1)}, f32[2,4096]{1,0:T(2,128)}) custom-call(s32[1]{0:T(128)} %bitcast.me_ref, bf16[1024,2048]{1,0:T(8,128)(2,1)} %get-tuple-element.101.ha_ref, ...), custom_call_target="tpu_custom_call", output_to_operand_aliasing={{3}: (6, {})} | custom-call | flops 12884901888 | bytes 23068672 | tf_op jit(solution)/shard_map/qkv/pallas_call | solution.py:91
  163.9 46.1 %collective-permute-done.ha_ref = bf16[1024,2048]{1,0:T(8,128)(2,1)} collective-permute-done((bf16[1024,2048]{1,0:T(8,128)(2,1)}, bf16[1024,2048]{1,0:T(8,128)(2,1)}, u32[]{:S(2)}, u32[]{:S(2)}) %collective-permute-start) | collective-permute-done | bytes 4194336 | tf_op jit(solution)/shard_map/ppermute | solution.py:308
  220.9 19.7 %qkv.13 = (bf16[4096,512]{1,0:T(8,128)(2,1)}, bf16[4096,512]{1,0:T(8,128)(2,1)}, bf16[512,4096]{1,0:T(8,128)(2,1)}, bf16[65536,128]{1,0:T(8,128)(2,1)}, f32[2,4096]{1,0:T(2,128)}) custom-call(s32[1]{0:T(128)} %bitcast.me_ref, ...), custom_call_target="tpu_custom_call", output_to_operand_aliasing={{0}: (6, {}), {1}: (7, {}), {2}: (8, {}), {3}: (9, {}), {4}... | custom-call | flops 12884901888 | bytes 23068672 | tf_op jit(solution)/shard_map/qkv/pallas_call | solution.py:91
  247.4 13.3 %rope.4 = (bf16[4096,512]{1,0:T(8,128)(2,1)}, bf16[4096,512]{1,0:T(8,128)(2,1)}, bf16[65536,128]{1,0:T(8,128)(2,1)}) custom-call(bf16[4096,512]{1,0:T(8,128)(2,1)} %get-tuple-element.106.q_ref, bf16[4096,512]{1,0:T(8,128)(2,1)} %get-tuple-element.107.k_ref, f32[2,4096]{1,0:T(2,128)} %add.85.ss_ref, f32[1,512]{1,0:T(1,128)} %bitcast.22, f32[1,512]{1,0:T(1,128)} %bitcast.26, ...), custom_call_target="tpu_custom_call" | custom-call | flops 7000000000 | bytes 20971520 | tf_op jit(solution)/shard_map/rope/pallas_call | solution.py:157
  260.6 53.8 %attn.4 = bf16[4096,512]{1,0:T(8,128)(2,1)} custom-call(bf16[4096,512]{1,0:T(8,128)(2,1)} %get-tuple-element.109.q_ref, bf16[4096,512]{1,0:T(8,128)(2,1)} %get-tuple-element.110.k_ref, bf16[512,4096]{1,0:T(8,128)(2,1)} %get-tuple-element.111.vt_ref), custom_call_target="tpu_custom_call" | custom-call | flops 34359738368 | bytes 16777216 | tf_op jit(solution)/shard_map/attn/pallas_call | solution.py:239
  322.1 19.7 %qkv.14 = (bf16[4096,512]{1,0:T(8,128)(2,1)}, bf16[4096,512]{1,0:T(8,128)(2,1)}, bf16[512,4096]{1,0:T(8,128)(2,1)}, bf16[65536,128]{1,0:T(8,128)(2,1)}, f32[2,4096]{1,0:T(2,128)}) custom-call(s32[1]{0:T(128)} %bitcast.me_ref, ...), custom_call_target="tpu_custom_call", output_to_operand_aliasing={{0}: (6, {}), {1}: (7, {}), {2}: (8, {}), {3}: (9, {}), {4}... | custom-call | flops 12884901888 | bytes 23068672 | tf_op jit(solution)/shard_map/qkv/pallas_call | solution.py:91
  343.7 13.3 %rope.5 = (bf16[4096,512]{1,0:T(8,128)(2,1)}, bf16[4096,512]{1,0:T(8,128)(2,1)}, bf16[65536,128]{1,0:T(8,128)(2,1)}) custom-call(bf16[4096,512]{1,0:T(8,128)(2,1)} %get-tuple-element.102.q_ref, bf16[4096,512]{1,0:T(8,128)(2,1)} %get-tuple-element.103.k_ref, f32[2,4096]{1,0:T(2,128)} %add.87.ss_ref, ...), custom_call_target="tpu_custom_call", output_to_operand_aliasing={{2}: (7, {})} | custom-call | flops 7000000000 | bytes 20971520 | tf_op jit(solution)/shard_map/rope/pallas_call | solution.py:157
  357.0 53.6 %attn.5 = bf16[4096,512]{1,0:T(8,128)(2,1)} custom-call(bf16[4096,512]{1,0:T(8,128)(2,1)} %get-tuple-element.121.q_ref, bf16[4096,512]{1,0:T(8,128)(2,1)} %get-tuple-element.122.k_ref, bf16[512,4096]{1,0:T(8,128)(2,1)} %get-tuple-element.123.vt_ref), custom_call_target="tpu_custom_call" | custom-call | flops 34359738368 | bytes 16777216 | tf_op jit(solution)/shard_map/attn/pallas_call | solution.py:239
  418.1 20.1 %qkv.15 = (bf16[4096,512]{1,0:T(8,128)(2,1)}, bf16[4096,512]{1,0:T(8,128)(2,1)}, bf16[512,4096]{1,0:T(8,128)(2,1)}, bf16[65536,128]{1,0:T(8,128)(2,1)}, f32[2,4096]{1,0:T(2,128)}) custom-call(s32[1]{0:T(128)} %bitcast.me_ref, ...), custom_call_target="tpu_custom_call", output_to_operand_aliasing={{0}: (6, {}), {1}: (7, {}), {2}: (8, {}), {3}: (9, {}), {4}... | custom-call | flops 12884901888 | bytes 23068672 | tf_op jit(solution)/shard_map/qkv/pallas_call | solution.py:91
  446.7 13.2 %rope.6 = (bf16[4096,512]{1,0:T(8,128)(2,1)}, bf16[4096,512]{1,0:T(8,128)(2,1)}, bf16[65536,128]{1,0:T(8,128)(2,1)}) custom-call(bf16[4096,512]{1,0:T(8,128)(2,1)} %get-tuple-element.133.q_ref, bf16[4096,512]{1,0:T(8,128)(2,1)} %get-tuple-element.134.k_ref, f32[2,4096]{1,0:T(2,128)} %add.89.ss_ref, ...), custom_call_target="tpu_custom_call", output_to_operand_aliasing={{2}: (7, {})} | custom-call | flops 7000000000 | bytes 20971520 | tf_op jit(solution)/shard_map/rope/pallas_call | solution.py:157
  466.2 53.6 %attn.6 = bf16[4096,512]{1,0:T(8,128)(2,1)} custom-call(bf16[4096,512]{1,0:T(8,128)(2,1)} %get-tuple-element.137.q_ref, bf16[4096,512]{1,0:T(8,128)(2,1)} %get-tuple-element.138.k_ref, bf16[512,4096]{1,0:T(8,128)(2,1)} %get-tuple-element.139.vt_ref), custom_call_target="tpu_custom_call" | custom-call | flops 34359738368 | bytes 16777216 | tf_op jit(solution)/shard_map/attn/pallas_call | solution.py:239
  525.5 13.2 %rope.7 = (bf16[4096,512]{1,0:T(8,128)(2,1)}, bf16[4096,512]{1,0:T(8,128)(2,1)}, bf16[65536,128]{1,0:T(8,128)(2,1)}) custom-call(bf16[4096,512]{1,0:T(8,128)(2,1)} %get-tuple-element.130.q_ref, bf16[4096,512]{1,0:T(8,128)(2,1)} %get-tuple-element.131.k_ref, f32[2,4096]{1,0:T(2,128)} %add.91.ss_ref, ...), custom_call_target="tpu_custom_call", output_to_operand_aliasing={{2}: (7, {})} | custom-call | flops 7000000000 | bytes 20971520 | tf_op jit(solution)/shard_map/rope/pallas_call | solution.py:157
  540.9 53.7 %attn.7 = bf16[4096,512]{1,0:T(8,128)(2,1)} custom-call(bf16[4096,512]{1,0:T(8,128)(2,1)} %get-tuple-element.142.q_ref, bf16[4096,512]{1,0:T(8,128)(2,1)} %get-tuple-element.143.k_ref, bf16[512,4096]{1,0:T(8,128)(2,1)} %get-tuple-element.144.vt_ref), custom_call_target="tpu_custom_call" | custom-call | flops 34359738368 | bytes 16777216 | tf_op jit(solution)/shard_map/attn/pallas_call | solution.py:239
  600.8 14.0 %outproj.4.refs_0_ = bf16[4,1024,2048]{2,1,0:T(8,128)(2,1)} custom-call(bf16[1024,512]{1,0:T(8,128)(2,1)} %get-tuple-element.153.o0, bf16[1024,512]{1,0:T(8,128)(2,1)} %collective-permute-done.32.o1, bf16[1024,512]{1,0:T(8,128)(2,1)} %collective-permute-done.33.o2, bf16[1024,512]{1,0:T(8,128)(2,1)} %collective-permute-done.34.o3, bf16[512,2048]{1,0:T(8,128)(2,1)} %w0.7, ...), custom_call_target="tpu_custom_call" | custom-call | flops 8589934592 | bytes 20971520 | tf_op jit(solution)/shard_map/outproj/pallas_call | solution.py:276
  616.7 13.9 %outproj.5.refs_0_ = bf16[4,1024,2048]{2,1,0:T(8,128)(2,1)} custom-call(bf16[1024,512]{1,0:T(8,128)(2,1)} %get-tuple-element.149.o0, bf16[1024,512]{1,0:T(8,128)(2,1)} %collective-permute-done.29.o1, bf16[1024,512]{1,0:T(8,128)(2,1)} %collective-permute-done.30.o2, bf16[1024,512]{1,0:T(8,128)(2,1)} %copy-done.3, ...), custom_call_target="tpu_custom_call", output_to_operand_aliasing={{}: (9, {})} | custom-call | flops 8589934592 | bytes 20971520 | tf_op jit(solution)/shard_map/outproj/pallas_call | solution.py:276
  630.6 15.7 %collective-permute-done.28.o3 = bf16[1024,512]{1,0:T(8,128)(2,1)} collective-permute-done((bf16[1024,512]{1,0:T(8,128)(2,1)}, bf16[1024,512]{1,0:T(8,128)(2,1)}, u32[]{:S(2)}, u32[]{:S(2)}) %collective-permute-start.28) | collective-permute-done | bytes 1048608 | tf_op jit(solution)/shard_map/ppermute | solution.py:308
  646.3 13.9 %outproj.6.refs_0_ = bf16[4,1024,2048]{2,1,0:T(8,128)(2,1)} custom-call(bf16[1024,512]{1,0:T(8,128)(2,1)} %get-tuple-element.148.o0, bf16[1024,512]{1,0:T(8,128)(2,1)} %collective-permute-done.26.o1, bf16[1024,512]{1,0:T(8,128)(2,1)} %collective-permute-done.27.o2, bf16[1024,512]{1,0:T(8,128)(2,1)} %collective-permute-done.28.o3, ...), custom_call_target="tpu_custom_call", output_to_operand_aliasing={{}: (9, {})} | custom-call | flops 8589934592 | bytes 20971520 | tf_op jit(solution)/shard_map/outproj/pallas_call | solution.py:276
  669.9 21.2 %collective-permute-done.22.o3 = bf16[1024,512]{1,0:T(8,128)(2,1)S(1)} collective-permute-done((bf16[1024,512]{1,0:T(8,128)(2,1)}, bf16[1024,512]{1,0:T(8,128)(2,1)S(1)}, u32[]{:S(2)}, u32[]{:S(2)}) %collective-permute-start.22) | collective-permute-done | bytes 1048608 | tf_op jit(solution)/shard_map/ppermute | solution.py:308
  692.1 13.9 %outproj.7 = bf16[4,1024,2048]{2,1,0:T(8,128)(2,1)} custom-call(bf16[1024,512]{1,0:T(8,128)(2,1)} %get-tuple-element.145.o0, bf16[1024,512]{1,0:T(8,128)(2,1)} %copy-done.4, bf16[1024,512]{1,0:T(8,128)(2,1)} %copy-done.5, bf16[1024,512]{1,0:T(8,128)(2,1)} %copy-done.6, bf16[512,2048]{1,0:T(8,128)(2,1)} %w0.7, ...), custom_call_target="tpu_custom_call", output_to_operand_aliasing={{}: (9, {})} | custom-call | flops 8589934592 | bytes 20971520 | tf_op jit(solution)/shard_map/outproj/pallas_call | solution.py:276
  (112 shorter events, 108.6 us)
Async XLA Ops:
  21.9 23.6 %collective-permute-start.4 = (bf16[1024,2048]{1,0:T(8,128)(2,1)}, bf16[1024,2048]{1,0:T(8,128)(2,1)}, u32[]{:S(2)}, u32[]{:S(2)}) collective-permute-start(bf16[1024,2048]{1,0:T(8,128)(2,1)} %get-tuple-element.164.ha_ref), channel_id=1, source_target_pairs={{0,1},{1,0},{2,3},{3,2},{4,5},{5,4},{6,7},{7,6}} | collective-permute-start | bytes 12582920 | tf_op jit(solution)/shard_map/ppermute | solution.py:308
  22.7 42.5 %collective-permute-start.3 = (bf16[1024,2048]{1,0:T(8,128)(2,1)}, bf16[1024,2048]{1,0:T(8,128)(2,1)}, u32[]{:S(2)}, u32[]{:S(2)}) collective-permute-start(bf16[1024,2048]{1,0:T(8,128)(2,1)} %get-tuple-element.105.ha_ref), channel_id=1, source_target_pairs={{0,1},{1,0},{2,3},{3,2},{4,5},{5,4},{6,7},{7,6}} | collective-permute-start | bytes 12582920 | tf_op jit(solution)/shard_map/ppermute | solution.py:308
  22.7 94.0 %collective-permute-start.2 = (bf16[1024,2048]{1,0:T(8,128)(2,1)}, bf16[1024,2048]{1,0:T(8,128)(2,1)}, u32[]{:S(2)}, u32[]{:S(2)}) collective-permute-start(bf16[1024,2048]{1,0:T(8,128)(2,1)} %fusion.2.ha_ref), channel_id=1, source_target_pairs={{0,2},{1,3},{2,0},{3,1},{4,6},{5,7},{6,4},{7,5}} | collective-permute-start | bytes 12582920 | tf_op jit(solution)/shard_map/ppermute | solution.py:308
  116.7 27.4 %collective-permute-start.1 = (bf16[1024,2048]{1,0:T(8,128)(2,1)}, bf16[1024,2048]{1,0:T(8,128)(2,1)}, u32[]{:S(2)}, u32[]{:S(2)}) collective-permute-start(bf16[1024,2048]{1,0:T(8,128)(2,1)} %get-tuple-element.101.ha_ref), channel_id=1, source_target_pairs={{0,1},{1,0},{2,3},{3,2},{4,5},{5,4},{6,7},{7,6}} | collective-permute-start | bytes 12582920 | tf_op jit(solution)/shard_map/ppermute | solution.py:308
  117.3 92.8 %collective-permute-start = (bf16[1024,2048]{1,0:T(8,128)(2,1)}, bf16[1024,2048]{1,0:T(8,128)(2,1)}, u32[]{:S(2)}, u32[]{:S(2)}) collective-permute-start(bf16[1024,2048]{1,0:T(8,128)(2,1)} %get-tuple-element.164.ha_ref), channel_id=1, source_target_pairs={{0,2},{1,3},{2,0},{3,1},{4,6},{5,7},{6,4},{7,5}} | collective-permute-start | bytes 12582920 | tf_op jit(solution)/shard_map/ppermute | solution.py:308
  220.6 93.9 %collective-permute-start.10 = (bf16[1024,2048]{1,0:T(8,128)(2,1)}, bf16[1024,2048]{1,0:T(8,128)(2,1)}, u32[]{:S(2)}, u32[]{:S(2)}) collective-permute-start(bf16[1024,2048]{1,0:T(8,128)(2,1)} %get-tuple-element.105.ha_ref), channel_id=1, source_target_pairs={{0,2},{1,3},{2,0},{3,1},{4,6},{5,7},{6,4},{7,5}} | collective-permute-start | bytes 12582920 | tf_op jit(solution)/shard_map/ppermute | solution.py:308
  315.0 26.9 %collective-permute-start.9 = (f32[2,4096]{1,0:T(2,128)S(1)}, f32[2,4096]{1,0:T(2,128)S(1)}, u32[]{:S(2)}, u32[]{:S(2)}) collective-permute-start(f32[2,4096]{1,0:T(2,128)S(1)} %copy-done.10), channel_id=1, source_target_pairs={{0,2},{1,3},{2,0},{3,1},{4,6},{5,7},{6,4},{7,5}} | collective-permute-start | bytes 98312 | tf_op jit(solution)/shard_map/ppermute | solution.py:308
  316.7 93.9 %collective-permute-start.8 = (bf16[1024,2048]{1,0:T(8,128)(2,1)}, bf16[1024,2048]{1,0:T(8,128)(2,1)}, u32[]{:S(2)}, u32[]{:S(2)}) collective-permute-start(bf16[1024,2048]{1,0:T(8,128)(2,1)} %get-tuple-element.101.ha_ref), channel_id=1, source_target_pairs={{0,2},{1,3},{2,0},{3,1},{4,6},{5,7},{6,4},{7,5}} | collective-permute-start | bytes 12582920 | tf_op jit(solution)/shard_map/ppermute | solution.py:308
  417.0 102.8 %collective-permute-start.24 = (bf16[512,2048]{1,0:T(8,128)(2,1)S(1)}, bf16[512,2048]{1,0:T(8,128)(2,1)}, u32[]{:S(2)}, u32[]{:S(2)}) collective-permute-start(bf16[512,2048]{1,0:T(8,128)(2,1)S(1)} %copy-done.1), channel_id=1, source_target_pairs={{0,2},{1,3},{2,0},{3,1},{4,6},{5,7},{6,4},{7,5}} | collective-permute-start | bytes 6291464 | tf_op jit(solution)/shard_map/ppermute | solution.py:308
  417.3 121.4 %collective-permute-start.23 = (bf16[512,2048]{1,0:T(8,128)(2,1)S(1)}, bf16[512,2048]{1,0:T(8,128)(2,1)}, u32[]{:S(2)}, u32[]{:S(2)}) collective-permute-start(bf16[512,2048]{1,0:T(8,128)(2,1)S(1)} %copy-done.1), channel_id=1, source_target_pairs={{0,1},{1,0},{2,3},{3,2},{4,5},{5,4},{6,7},{7,6}} | collective-permute-start | bytes 6291464 | tf_op jit(solution)/shard_map/ppermute | solution.py:308
  442.9 23.4 %collective-permute-start.16 = (f32[2,4096]{1,0:T(2,128)S(1)}, f32[2,4096]{1,0:T(2,128)S(1)}, u32[]{:S(2)}, u32[]{:S(2)}) collective-permute-start(f32[2,4096]{1,0:T(2,128)S(1)} %copy-done.8), channel_id=1, source_target_pairs={{0,2},{1,3},{2,0},{3,1},{4,6},{5,7},{6,4},{7,5}} | collective-permute-start | bytes 98312 | tf_op jit(solution)/shard_map/ppermute | solution.py:308
  444.5 95.6 %collective-permute-start.34 = (bf16[1024,512]{1,0:T(8,128)(2,1)}, bf16[1024,512]{1,0:T(8,128)(2,1)}, u32[]{:S(2)}, u32[]{:S(2)}) collective-permute-start(bf16[1024,512]{1,0:T(8,128)(2,1)} %get-tuple-element.156), channel_id=1, source_target_pairs={{0,3},{1,2},{2,1},{3,0},{4,7},{5,6},{6,5},{7,4}} | collective-permute-start | bytes 3145736 | tf_op jit(solution)/shard_map/ppermute | solution.py:308
  444.5 95.8 %collective-permute-start.33 = (bf16[1024,512]{1,0:T(8,128)(2,1)}, bf16[1024,512]{1,0:T(8,128)(2,1)}, u32[]{:S(2)}, u32[]{:S(2)}) collective-permute-start(bf16[1024,512]{1,0:T(8,128)(2,1)} %get-tuple-element.155), channel_id=1, source_target_pairs={{0,2},{1,3},{2,0},{3,1},{4,6},{5,7},{6,4},{7,5}} | collective-permute-start | bytes 3145736 | tf_op jit(solution)/shard_map/ppermute | solution.py:308
  466.2 74.4 %collective-permute-start.32 = (bf16[1024,512]{1,0:T(8,128)(2,1)}, bf16[1024,512]{1,0:T(8,128)(2,1)}, u32[]{:S(2)}, u32[]{:S(2)}) collective-permute-start(bf16[1024,512]{1,0:T(8,128)(2,1)} %get-tuple-element.154), channel_id=1, source_target_pairs={{0,1},{1,0},{2,3},{3,2},{4,5},{5,4},{6,7},{7,6}} | collective-permute-start | bytes 3145736 | tf_op jit(solution)/shard_map/ppermute | solution.py:308
  524.6 74.2 %collective-permute-start.31 = (bf16[1024,512]{1,0:T(8,128)(2,1)}, bf16[1024,512]{1,0:T(8,128)(2,1)S(1)}, u32[]{:S(2)}, u32[]{:S(2)}) collective-permute-start(bf16[1024,512]{1,0:T(8,128)(2,1)} %get-tuple-element.152), channel_id=1, source_target_pairs={{0,3},{1,2},{2,1},{3,0},{4,7},{5,6},{6,5},{7,4}} | collective-permute-start | bytes 3145736 | tf_op jit(solution)/shard_map/ppermute | solution.py:308
  538.8 76.0 %collective-permute-start.30 = (bf16[1024,512]{1,0:T(8,128)(2,1)}, bf16[1024,512]{1,0:T(8,128)(2,1)}, u32[]{:S(2)}, u32[]{:S(2)}) collective-permute-start(bf16[1024,512]{1,0:T(8,128)(2,1)} %get-tuple-element.151), channel_id=1, source_target_pairs={{0,2},{1,3},{2,0},{3,1},{4,6},{5,7},{6,4},{7,5}} | collective-permute-start | bytes 3145736 | tf_op jit(solution)/shard_map/ppermute | solution.py:308
  540.1 74.8 %collective-permute-start.29 = (bf16[1024,512]{1,0:T(8,128)(2,1)}, bf16[1024,512]{1,0:T(8,128)(2,1)}, u32[]{:S(2)}, u32[]{:S(2)}) collective-permute-start(bf16[1024,512]{1,0:T(8,128)(2,1)} %get-tuple-element.150), channel_id=1, source_target_pairs={{0,1},{1,0},{2,3},{3,2},{4,5},{5,4},{6,7},{7,6}} | collective-permute-start | bytes 3145736 | tf_op jit(solution)/shard_map/ppermute | solution.py:308
  540.3 59.1 %collective-permute-start.25 = (bf16[512,2048]{1,0:T(8,128)(2,1)}, bf16[512,2048]{1,0:T(8,128)(2,1)S(1)}, u32[]{:S(2)}, u32[]{:S(2)}) collective-permute-start(bf16[512,2048]{1,0:T(8,128)(2,1)} %collective-permute-done.24.w2), channel_id=1, source_target_pairs={{0,1},{1,0},{2,3},{3,2},{4,5},{5,4},{6,7},{7,6}} | collective-permute-start | bytes 6291464 | tf_op jit(solution)/shard_map/ppermute | solution.py:308
  540.7 75.6 %collective-permute-start.26 = (bf16[1024,512]{1,0:T(8,128)(2,1)}, bf16[1024,512]{1,0:T(8,128)(2,1)}, u32[]{:S(2)}, u32[]{:S(2)}) collective-permute-start(bf16[1024,512]{1,0:T(8,128)(2,1)} %get-tuple-element.175), channel_id=1, source_target_pairs={{0,1},{1,0},{2,3},{3,2},{4,5},{5,4},{6,7},{7,6}} | collective-permute-start | bytes 3145736 | tf_op jit(solution)/shard_map/ppermute | solution.py:308
  598.7 31.8 %collective-permute-start.27 = (bf16[1024,512]{1,0:T(8,128)(2,1)}, bf16[1024,512]{1,0:T(8,128)(2,1)}, u32[]{:S(2)}, u32[]{:S(2)}) collective-permute-start(bf16[1024,512]{1,0:T(8,128)(2,1)} %get-tuple-element.174), channel_id=1, source_target_pairs={{0,2},{1,3},{2,0},{3,1},{4,6},{5,7},{6,4},{7,5}} | collective-permute-start | bytes 3145736 | tf_op jit(solution)/shard_map/ppermute | solution.py:308
  599.4 46.8 %collective-permute-start.28 = (bf16[1024,512]{1,0:T(8,128)(2,1)}, bf16[1024,512]{1,0:T(8,128)(2,1)}, u32[]{:S(2)}, u32[]{:S(2)}) collective-permute-start(bf16[1024,512]{1,0:T(8,128)(2,1)} %get-tuple-element.173), channel_id=1, source_target_pairs={{0,3},{1,2},{2,1},{3,0},{4,7},{5,6},{6,5},{7,4}} | collective-permute-start | bytes 3145736 | tf_op jit(solution)/shard_map/ppermute | solution.py:308
  614.8 45.3 %collective-permute-start.20 = (bf16[1024,512]{1,0:T(8,128)(2,1)}, bf16[1024,512]{1,0:T(8,128)(2,1)S(1)}, u32[]{:S(2)}, u32[]{:S(2)}) collective-permute-start(bf16[1024,512]{1,0:T(8,128)(2,1)} %get-tuple-element.179), channel_id=1, source_target_pairs={{0,1},{1,0},{2,3},{3,2},{4,5},{5,4},{6,7},{7,6}} | collective-permute-start | bytes 3145736 | tf_op jit(solution)/shard_map/ppermute | solution.py:308
  615.0 55.0 %collective-permute-start.21 = (bf16[1024,512]{1,0:T(8,128)(2,1)}, bf16[1024,512]{1,0:T(8,128)(2,1)S(1)}, u32[]{:S(2)}, u32[]{:S(2)}) collective-permute-start(bf16[1024,512]{1,0:T(8,128)(2,1)} %get-tuple-element.178), channel_id=1, source_target_pairs={{0,2},{1,3},{2,0},{3,1},{4,6},{5,7},{6,4},{7,5}} | collective-permute-start | bytes 3145736 | tf_op jit(solution)/shard_map/ppermute | solution.py:308
  616.2 74.9 %collective-permute-start.22 = (bf16[1024,512]{1,0:T(8,128)(2,1)}, bf16[1024,512]{1,0:T(8,128)(2,1)S(1)}, u32[]{:S(2)}, u32[]{:S(2)}) collective-permute-start(bf16[1024,512]{1,0:T(8,128)(2,1)} %get-tuple-element.177), channel_id=1, source_target_pairs={{0,3},{1,2},{2,1},{3,0},{4,7},{5,6},{6,5},{7,4}} | collective-permute-start | bytes 3145736 | tf_op jit(solution)/shard_map/ppermute | solution.py:308
  (23 other events, 324.1 us)

commit v3 on v2

--- a/solution.py
+++ b/solution.py
@@ -13,6 +13,7 @@
 LOG2E = math.log2(math.e)
 F32 = jnp.float32
 BF16 = jnp.bfloat16
+QKV_ROWS = 256
 VMEM_LIMIT = 60 * 1024 * 1024
 
 
@@ -48,9 +49,14 @@
     return scr[...].astype(BF16)
 
 
-def qkv_kernel(me_ref, ha_ref, hb_ref, wq_ref, wk_ref, wv_ref, *refs):
-    q_ref, k_ref, vt_ref, vc_ref, ss_ref, scr = refs[-6:]
-    h = jnp.where(pl.program_id(0) == 0, ha_ref[...], hb_ref[...])
+def qkv_kernel(n_sub, me_ref, h0_ref, h1_ref, h2_ref, h3_ref, wq_ref, wk_ref, wv_ref, *refs):
+    q_ref, k_ref, vt_ref, vc_ref, ss_ref, scr, h_ref = refs[-7:]
+    step = pl.program_id(0)
+    for n, src in enumerate((h0_ref, h1_ref, h2_ref, h3_ref)):
+        @pl.when(step // n_sub == n)
+        def _(src=src):
+            h_ref[...] = src[...]
+    h = h_ref[...]
     cols = wq_ref.shape[1]
     q = jnp.dot(h, wq_ref[...], preferred_element_type=F32).astype(BF16)
     q_ref[...] = q
@@ -63,25 +69,24 @@
     vc_ref[...] = spread_heads(scr, [v[:, g * HD:(g + 1) * HD] for g in range(cols // HD)])
 
 
-def qkv_call(me, ha, hb, ws, r0, bufs, vc_prev, b, n_batch, seq):
-    rows, width = ha.shape
+def qkv_call(me, hs, ws, r0, bufs, vc_prev, b, n_batch, seq):
+    part, width = hs[0].shape
     cols = ws[0].shape[1]
     heads = cols // HD
-    bq = 512
-    nq = rows // bq
+    bq = QKV_ROWS
+    n_sub = part // bq
     base = b * (seq // bq)
 
-    def pos(c, i, m):
-        return (m[0] ^ (r0 + c)) * nq + i
-
-    wspec = pl.BlockSpec((width, cols), lambda c, i, m: (0, 0))
-    rspec = pl.BlockSpec((bq, cols), lambda c, i, m: (pos(c, i, m), 0))
-    in_specs = [
-        pl.BlockSpec((bq, width), lambda c, i, m: (jnp.where(c == 0, i, nq - 1), 0)),
-        pl.BlockSpec((bq, width), lambda c, i, m: (jnp.where(c == 0, 0, i), 0)),
-        wspec, wspec, wspec,
-    ]
-    args = [me, ha, hb, *ws]
+    def pos(s, m):
+        return (m[0] ^ (r0 + s // (2 * n_sub))) * (2 * n_sub) + s % (2 * n_sub)
+
+    def hspec(n):
+        return pl.BlockSpec((bq, width), lambda s, m: (jnp.clip(s - n * n_sub, 0, n_sub - 1), 0))
+
+    wspec = pl.BlockSpec((width, cols), lambda s, m: (0, 0))
+    rspec = pl.BlockSpec((bq, cols), lambda s, m: (pos(s, m), 0))
+    in_specs = [hspec(n) for n in range(4)] + [wspec, wspec, wspec]
+    args = [me, *hs, *ws]
     aliases = {}
     for n, buf in enumerate([*(bufs or [None] * 4)[:3], vc_prev, (bufs or [None] * 4)[3]]):
         if buf is not None:
@@ -89,26 +94,26 @@
             args.append(buf)
             in_specs.append(pl.BlockSpec(memory_space=pl.ANY))
     q, k, vt, vc, ss = pl.pallas_call(
-        qkv_kernel,
+        functools.partial(qkv_kernel, n_sub),
         grid_spec=pltpu.PrefetchScalarGridSpec(
             num_scalar_prefetch=1,
-            grid=(2, nq),
+            grid=(4 * n_sub,),
             in_specs=in_specs,
             out_specs=[
                 rspec, rspec,
-                pl.BlockSpec((cols, bq), lambda c, i, m: (0, pos(c, i, m))),
-                pl.BlockSpec((bq * heads, HD), lambda c, i, m: (base + pos(c, i, m), 0)),
-                pl.BlockSpec((2, bq), lambda c, i, m: (0, pos(c, i, m))),
+                pl.BlockSpec((cols, bq), lambda s, m: (0, pos(s, m))),
+                pl.BlockSpec((bq * heads, HD), lambda s, m: (base + pos(s, m), 0)),
+                pl.BlockSpec((2, bq), lambda s, m: (0, pos(s, m))),
             ],
-            scratch_shapes=[pltpu.VMEM((bq * heads, HD), F32)],
+            scratch_shapes=[pltpu.VMEM((bq * heads, HD), F32), pltpu.VMEM((bq, width), BF16)],
         ),
         out_shape=[
             jax.ShapeDtypeStruct((seq, cols), BF16), jax.ShapeDtypeStruct((seq, cols), BF16), jax.ShapeDtypeStruct((cols, seq), BF16),
             jax.ShapeDtypeStruct((n_batch * seq * heads, HD), BF16), jax.ShapeDtypeStruct((2, seq), F32),
         ],
         input_output_aliases=aliases,
-        compiler_params=params("arbitrary", "arbitrary"),
-        cost_estimate=cost(12 * rows * width * cols, 4 * rows * width + 6 * width * cols + 16 * rows * cols),
+        compiler_params=params("arbitrary"),
+        cost_estimate=cost(24 * part * width * cols, 8 * part * width + 6 * width * cols + 32 * part * cols),
         name="qkv",
     )(*args)
     return [q, k, vt, ss], vc
@@ -307,25 +312,39 @@
         def send(val, hop):
             return lax.ppermute(val, 'tp', pairs[hop])
 
+        half = rows // 2
         own = []
         for b in range(n_batch):
-            xf = (x_local if b == 0 else after(x_local, own[0]))[b].astype(F32)
-            inv_rms = lax.rsqrt(jnp.mean(xf * xf, axis=-1, keepdims=True) + 1e-5)
-            own.append((xf * inv_rms * attn_gain).astype(BF16))
-        far = [send(own[b], 2) for b in range(2)]
-        near = [send(h, 1) for h in own]
+            xs = x_local if b == 0 else after(x_local, own[0][0])
+            parts = []
+            for p in range(2):
+                xf = xs[b, p * half:(p + 1) * half].astype(F32)
+                inv_rms = lax.rsqrt(jnp.mean(xf * xf, axis=-1, keepdims=True) + 1e-5)
+                parts.append((xf * inv_rms * attn_gain).astype(BF16))
+            own.append(parts)
+        far = [[None, None] for _ in own]
+
+        def push(b, p, *deps):
+            far[b][p] = send(after(own[b][p], *deps) if deps else own[b][p], 2)
+
+        push(0, 0)
+        push(0, 1)
+        push(1, 0)
+        near = [[send(h, 1) for h in parts] for parts in own]
         bufs, late, ex, stats = [], [], [], []
         vc = kc = out = ws = None
 
-        def early(b, h1, vc):
-            buf, vc = qkv_call(me_arr, own[b], h1, w_qkv, 0, None, vc, b, n_batch, seq)
+        def early(b, vc, *deps):
+            n0 = after(near[b][0], *deps) if deps else near[b][0]
+            buf, vc = qkv_call(me_arr, [*own[b], n0, near[b][1]], w_qkv, 0, None, vc, b, n_batch, seq)
             bufs.append(buf)
             return vc
 
         def project(b, vc, *deps):
-            h2 = after(far[b], *deps)
-            h3 = send(h2, 1)
-            buf, vc = qkv_call(me_arr, h2, h3, w_qkv, 2, bufs[b], vc, b, n_batch, seq)
+            h30 = send(far[b][0], 1)
+            f1 = after(far[b][1], *deps)
+            h31 = send(f1, 1)
+            buf, vc = qkv_call(me_arr, [far[b][0], f1, h30, h31], w_qkv, 2, bufs[b], vc, b, n_batch, seq)
             late.append(buf)
             stats.append(send(buf[3], 2))
             return vc
@@ -338,35 +357,48 @@
             o = attn_call(qr, kr, vt)
             return o, kc
 
-        def exchange(o, *deps):
-            pos = []
-            for r in range(n_tp):
-                piece = lax.dynamic_slice_in_dim(o, (me ^ r) * rows, rows, axis=0)
-                pos.append(piece if r == 0 else send(after(piece, *deps), r))
-            ex.append(pos)
-
-        for b in range(3):
-            vc = early(b, near[b] if b == 0 else after(near[b], vc), vc)
+        def cut(o, r):
+            return lax.dynamic_slice_in_dim(o, (me ^ r) * rows, rows, axis=0)
+
+        def exchange(o, dep):
+            o = after(o, dep)
+            pieces = [cut(o, r) for r in range(n_tp)]
+            return [pieces[0]] + [send(pieces[r], r) for r in range(1, n_tp)]
+
+        vc = early(0, None)
+        vc = early(1, vc, vc, ct, st)
+        vc = early(2, vc, vc)
         vc = project(0, vc, vc)
-        far.append(send(after(own[2], late[0][3]), 2))
-        vc = early(3, after(near[3], vc), vc)
-        vc = project(1, vc, vc)
-        far.append(send(after(own[3], late[1][3]), 2))
-        o0, kc = attend(0, kc, late[1][3])
-        vc = project(2, vc, o0)
-        w2 = send(after(wo_rows, late[2][3]), 2)
-        ws = [wo_rows, send(after(wo_rows, late[2][3]), 1), w2]
-        o1, kc = attend(1, kc, late[2][3])
-        vc = project(3, vc, o1)
-        exchange(o0, late[3][3])
-        exchange(o1, late[3][3])
-        o2, kc = attend(2, kc, late[3][3])
-        exchange(o2)
-        ws.append(send(after(w2, o2), 1))
-        o3, kc = attend(3, kc, o2)
-        exchange(o3)
+        done = late[0][3]
+        push(1, 1, done)
+        push(2, 0, done)
+        vc = early(3, vc, done)
+        o0, kc = attend(0, kc, vc)
+        pos0 = [cut(o0, r) for r in range(3)]
+        pos0 = [pos0[0], send(pos0[1], 1), send(pos0[2], 2)]
+        vc = project(1, vc, o0)
+        done = late[1][3]
+        push(2, 1, done)
+        push(3, 0, done)
+        piece = cut(after(o0, done), 3)
+        ex.append(pos0 + [send(piece, 3)])
+        o1, kc = attend(1, kc, piece)
+        vc = project(2, vc, o1)
+        done = late[2][3]
+        push(3, 1, done)
+        ex.append(exchange(o1, done))
+        o2, kc = attend(2, kc, ex[1][0])
+        vc = project(3, vc, o2)
+        done = late[3][3]
+        wo_late = after(wo_rows, done)
+        w2 = send(wo_late, 2)
+        ws = [wo_rows, send(wo_late, 1), w2]
+        ex.append(exchange(o2, done))
+        o3, kc = attend(3, kc, ex[2][0])
+        ws.append(send(after(w2, o3), 1))
+        ex.append(exchange(o3, o3))
         for b, pos in enumerate(ex):
-            pos[0] = after(pos[0], o3)
+            pos = [after(pos[0], o3), *pos[1:]]
             out = out_call(pos, ws, x_local, out, b)
         shape = (n_batch, seq, cols // HD, HD)
         return (out, kc.reshape(shape), vc.reshape(shape))

time: 716 us -> 777 us (1.085)
  waiting for transfers between devices: 143 us -> 178 us
  Pallas kernels: 482 us -> 498 us
    ppermute x35 -> x47, waiting for transfers between devices: 143 us -> 178 us  [send(): return lax.ppermute(val, 'tp', pairs[hop])]
    pallas_call x8, Pallas kernels: 159 us -> 175 us  [qkv_call(): pl.pallas_call(functools.partial(qkv_kernel, n_sub), grid_spec=pltpu.Pref...]
    ppermute x35 -> x47, starting transfers between devices: 24.4 us -> 29.5 us  [send(): return lax.ppermute(val, 'tp', pairs[hop])]
    dynamic_slice x4 -> x5, local copies, waits for them, and re-layouts: 17 us -> 17.2 us  [cut(): return lax.dynamic_slice_in_dim(o, (me ^ r) * rows, rows, axis=0)]
  transfers between devices with their start and end apart: 35 -> 47, of which waited for: 10 -> 16; matrix products, arithmetic and copies ran while one was open for 7% -> 6% of each run, Pallas kernels for 66% -> 60%
where the time goes in v3:
time: 777 us; the launch traced here: 767 us
  Pallas kernels  498 us (64%)
  waiting for transfers between devices  178 us (23%)
  other arithmetic  37.6 us (5%)
  starting transfers between devices  29.5 us (4%)
  local copies, waits for them, and re-layouts  22.3 us (3%)
    pallas_call x4, Pallas kernels, attn_call(): pl.pallas_call(functools.partial(attn_kernel, n_h, bq, ch), grid=(cols //...  215 us
    ppermute x47, waiting for transfers between devices, send(): return lax.ppermute(val, 'tp', pairs[hop])  178 us
    pallas_call x8, Pallas kernels, qkv_call(): pl.pallas_call(functools.partial(qkv_kernel, n_sub), grid_spec=pltpu.Pref...  175 us
    pallas_call x4, Pallas kernels, out_call(): pl.pallas_call(out_kernel, grid=(width // bn,), in_specs=in_specs, out_sp...  55.4 us
    pallas_call x4, Pallas kernels, rope_call(): pl.pallas_call(functools.partial(rope_kernel, width), grid=(nq,), in_spec...  53.2 us
    ppermute x47, starting transfers between devices, send(): return lax.ppermute(val, 'tp', pairs[hop])  29.5 us
    dynamic_slice x5, local copies, waits for them, and re-layouts, cut(): return lax.dynamic_slice_in_dim(o, (me ^ r) * rows, rows, axis=0)  17.2 us
  transfers between devices with their start and end apart: 47, of which 16 were waited for; matrix products, arithmetic and copies ran while one was open for 6% of the time, Pallas kernels for 60%

profile of v3, /device:TPU:0, one launch (start us, length us, event | category | flops | bytes accessed | tf_op | source)
XLA Modules:
  0.0 767.2 jit_solution(12124248093478340186)
XLA Ops:
  39.6 21.7 %qkv.8 = (bf16[4096,512]{1,0:T(8,128)(2,1)}, bf16[4096,512]{1,0:T(8,128)(2,1)}, bf16[512,4096]{1,0:T(8,128)(2,1)}, bf16[65536,128]{1,0:T(8,128)(2,1)}, f32[2,4096]{1,0:T(2,128)}) custom-call(s32[1]{0:T(128)} %bitcast.me_ref, bf16[512,2048]{1,0:T(8,128)(2,1)} %get-tuple-element.176.h0_ref, bf16[512,2048]{1,0:T(8,128)(2,1)} %get-tuple-element.175.h1_ref, ...), custom_call_target="tpu_custom_call" | custom-call | flops 12884901888 | bytes 23068672 | tf_op jit(solution)/shard_map/qkv/pallas_call | solution.py:96
  62.8 21.9 %qkv.9 = (bf16[4096,512]{1,0:T(8,128)(2,1)}, bf16[4096,512]{1,0:T(8,128)(2,1)}, bf16[512,4096]{1,0:T(8,128)(2,1)}, bf16[65536,128]{1,0:T(8,128)(2,1)}, f32[2,4096]{1,0:T(2,128)}) custom-call(s32[1]{0:T(128)} %bitcast.me_ref, bf16[512,2048]{1,0:T(8,128)(2,1)} %get-tuple-element.171.h0_ref, ...), custom_call_target="tpu_custom_call", output_to_operand_aliasing={{3}: (8, {})} | custom-call | flops 12884901888 | bytes 23068672 | tf_op jit(solution)/shard_map/qkv/pallas_call | solution.py:96
  86.0 22.0 %qkv.10 = (bf16[4096,512]{1,0:T(8,128)(2,1)}, bf16[4096,512]{1,0:T(8,128)(2,1)}, bf16[512,4096]{1,0:T(8,128)(2,1)}, bf16[65536,128]{1,0:T(8,128)(2,1)}, f32[2,4096]{1,0:T(2,128)}) custom-call(s32[1]{0:T(128)} %bitcast.me_ref, bf16[512,2048]{1,0:T(8,128)(2,1)} %get-tuple-element.111.h0_ref, ...), custom_call_target="tpu_custom_call", output_to_operand_aliasing={{3}: (8, {})} | custom-call | flops 12884901888 | bytes 23068672 | tf_op jit(solution)/shard_map/qkv/pallas_call | solution.py:96
  115.5 22.3 %qkv.11 = (bf16[4096,512]{1,0:T(8,128)(2,1)}, bf16[4096,512]{1,0:T(8,128)(2,1)}, bf16[512,4096]{1,0:T(8,128)(2,1)}, bf16[65536,128]{1,0:T(8,128)(2,1)}, f32[2,4096]{1,0:T(2,128)}) custom-call(s32[1]{0:T(128)} %bitcast.me_ref, ...), custom_call_target="tpu_custom_call", output_to_operand_aliasing={{0}: (8, {}), {1}: (9, {}), {2}: (10, {}), {3}: (11, {}), {... | custom-call | flops 12884901888 | bytes 23068672 | tf_op jit(solution)/shard_map/qkv/pallas_call | solution.py:96
  138.5 21.9 %qkv.12 = (bf16[4096,512]{1,0:T(8,128)(2,1)}, bf16[4096,512]{1,0:T(8,128)(2,1)}, bf16[512,4096]{1,0:T(8,128)(2,1)}, bf16[65536,128]{1,0:T(8,128)(2,1)}, f32[2,4096]{1,0:T(2,128)}) custom-call(s32[1]{0:T(128)} %bitcast.me_ref, bf16[512,2048]{1,0:T(8,128)(2,1)} %get-tuple-element.110.h0_ref, ...), custom_call_target="tpu_custom_call", output_to_operand_aliasing={{3}: (8, {})} | custom-call | flops 12884901888 | bytes 23068672 | tf_op jit(solution)/shard_map/qkv/pallas_call | solution.py:96
  176.2 53.6 %attn.4 = bf16[4096,512]{1,0:T(8,128)(2,1)} custom-call(bf16[4096,512]{1,0:T(8,128)(2,1)} %get-tuple-element.101.q_ref, bf16[4096,512]{1,0:T(8,128)(2,1)} %get-tuple-element.102.k_ref, bf16[512,4096]{1,0:T(8,128)(2,1)} %get-tuple-element.103.vt_ref), custom_call_target="tpu_custom_call" | custom-call | flops 34359738368 | bytes 16777216 | tf_op jit(solution)/shard_map/attn/pallas_call | solution.py:244
  234.3 21.8 %qkv.13 = (bf16[4096,512]{1,0:T(8,128)(2,1)}, bf16[4096,512]{1,0:T(8,128)(2,1)}, bf16[512,4096]{1,0:T(8,128)(2,1)}, bf16[65536,128]{1,0:T(8,128)(2,1)}, f32[2,4096]{1,0:T(2,128)}) custom-call(s32[1]{0:T(128)} %bitcast.me_ref, ...), custom_call_target="tpu_custom_call", output_to_operand_aliasing={{0}: (8, {}), {1}: (9, {}), {2}: (10, {}), {3}: (11, {}), {... | custom-call | flops 12884901888 | bytes 23068672 | tf_op jit(solution)/shard_map/qkv/pallas_call | solution.py:96
  259.1 19.7 %collective-permute-done.21 = f32[2,4096]{1,0:T(2,128)S(1)} collective-permute-done((f32[2,4096]{1,0:T(2,128)}, f32[2,4096]{1,0:T(2,128)S(1)}, u32[]{:S(2)}, u32[]{:S(2)}) %collective-permute-start.21) | collective-permute-done | bytes 32800 | tf_op jit(solution)/shard_map/ppermute | solution.py:313
  294.7 53.8 %attn.5 = bf16[4096,512]{1,0:T(8,128)(2,1)} custom-call(bf16[4096,512]{1,0:T(8,128)(2,1)} %get-tuple-element.118.q_ref, bf16[4096,512]{1,0:T(8,128)(2,1)} %get-tuple-element.119.k_ref, bf16[512,4096]{1,0:T(8,128)(2,1)} %get-tuple-element.120.vt_ref), custom_call_target="tpu_custom_call" | custom-call | flops 34359738368 | bytes 16777216 | tf_op jit(solution)/shard_map/attn/pallas_call | solution.py:244
  353.0 21.8 %qkv.14 = (bf16[4096,512]{1,0:T(8,128)(2,1)}, bf16[4096,512]{1,0:T(8,128)(2,1)}, bf16[512,4096]{1,0:T(8,128)(2,1)}, bf16[65536,128]{1,0:T(8,128)(2,1)}, f32[2,4096]{1,0:T(2,128)}) custom-call(s32[1]{0:T(128)} %bitcast.me_ref, bf16[512,2048]{1,0:T(8,128)(2,1)} %copy-done.16, ...), custom_call_target="tpu_custom_call", output_to_operand_aliasing={{0}: (8, {}), {1}: (9, {}), {2}: (10, {}), {3}: (11, {}), {... | custom-call | flops 12884901888 | bytes 23068672 | tf_op jit(solution)/shard_map/qkv/pallas_call | solution.py:96
  380.4 17.1 %collective-permute-done.26 = f32[2,4096]{1,0:T(2,128)S(1)} collective-permute-done((f32[2,4096]{1,0:T(2,128)}, f32[2,4096]{1,0:T(2,128)S(1)}, u32[]{:S(2)}, u32[]{:S(2)}) %collective-permute-start.26) | collective-permute-done | bytes 32800 | tf_op jit(solution)/shard_map/ppermute | solution.py:313
  413.2 53.6 %attn.6 = bf16[4096,512]{1,0:T(8,128)(2,1)} custom-call(bf16[4096,512]{1,0:T(8,128)(2,1)} %get-tuple-element.134.q_ref, bf16[4096,512]{1,0:T(8,128)(2,1)} %get-tuple-element.135.k_ref, bf16[512,4096]{1,0:T(8,128)(2,1)} %get-tuple-element.136.vt_ref), custom_call_target="tpu_custom_call" | custom-call | flops 34359738368 | bytes 16777216 | tf_op jit(solution)/shard_map/attn/pallas_call | solution.py:244
  472.5 21.8 %qkv.15 = (bf16[4096,512]{1,0:T(8,128)(2,1)}, bf16[4096,512]{1,0:T(8,128)(2,1)}, bf16[512,4096]{1,0:T(8,128)(2,1)}, bf16[65536,128]{1,0:T(8,128)(2,1)}, f32[2,4096]{1,0:T(2,128)}) custom-call(s32[1]{0:T(128)} %bitcast.me_ref, ...), custom_call_target="tpu_custom_call", output_to_operand_aliasing={{0}: (8, {}), {1}: (9, {}), {2}: (10, {}), {3}: (11, {}), {... | custom-call | flops 12884901888 | bytes 23068672 | tf_op jit(solution)/shard_map/qkv/pallas_call | solution.py:96
  503.8 13.4 %rope.7 = (bf16[4096,512]{1,0:T(8,128)(2,1)}, bf16[4096,512]{1,0:T(8,128)(2,1)}, bf16[65536,128]{1,0:T(8,128)(2,1)}) custom-call(bf16[4096,512]{1,0:T(8,128)(2,1)} %get-tuple-element.143.q_ref, bf16[4096,512]{1,0:T(8,128)(2,1)} %get-tuple-element.144.k_ref, f32[2,4096]{1,0:T(2,128)} %add.129.ss_ref, ...), custom_call_target="tpu_custom_call", output_to_operand_aliasing={{2}: (7, {})} | custom-call | flops 7000000000 | bytes 20971520 | tf_op jit(solution)/shard_map/rope/pallas_call | solution.py:162
  517.2 53.6 %attn.7 = bf16[4096,512]{1,0:T(8,128)(2,1)} custom-call(bf16[4096,512]{1,0:T(8,128)(2,1)} %get-tuple-element.149.q_ref, bf16[4096,512]{1,0:T(8,128)(2,1)} %get-tuple-element.150.k_ref, bf16[512,4096]{1,0:T(8,128)(2,1)} %get-tuple-element.151.vt_ref), custom_call_target="tpu_custom_call" | custom-call | flops 34359738368 | bytes 16777216 | tf_op jit(solution)/shard_map/attn/pallas_call | solution.py:244
  574.5 23.1 %collective-permute-done.45.o2 = bf16[1024,512]{1,0:T(8,128)(2,1)S(1)} collective-permute-done((bf16[1024,512]{1,0:T(8,128)(2,1)}, bf16[1024,512]{1,0:T(8,128)(2,1)S(1)}, u32[]{:S(2)}, u32[]{:S(2)}) %collective-permute-start.45) | collective-permute-done | bytes 1048608 | tf_op jit(solution)/shard_map/ppermute | solution.py:313
  598.8 20.1 %collective-permute-done.46.o3 = bf16[1024,512]{1,0:T(8,128)(2,1)S(1)} collective-permute-done((bf16[1024,512]{1,0:T(8,128)(2,1)}, bf16[1024,512]{1,0:T(8,128)(2,1)S(1)}, u32[]{:S(2)}, u32[]{:S(2)}) %collective-permute-start.46) | collective-permute-done | bytes 1048608 | tf_op jit(solution)/shard_map/ppermute | solution.py:313
  626.8 13.9 %outproj.4.refs_0_ = bf16[4,1024,2048]{2,1,0:T(8,128)(2,1)} custom-call(bf16[1024,512]{1,0:T(8,128)(2,1)} %get-tuple-element.158.o0, bf16[1024,512]{1,0:T(8,128)(2,1)} %copy-done.9, bf16[1024,512]{1,0:T(8,128)(2,1)} %copy-done.10, bf16[1024,512]{1,0:T(8,128)(2,1)} %copy-done.11, bf16[512,2048]{1,0:T(8,128)(2,1)} %w0.7, ...), custom_call_target="tpu_custom_call" | custom-call | flops 8589934592 | bytes 20971520 | tf_op jit(solution)/shard_map/outproj/pallas_call | solution.py:281
  642.6 21.1 %collective-permute-done.43.o3 = bf16[1024,512]{1,0:T(8,128)(2,1)} collective-permute-done((bf16[1024,512]{1,0:T(8,128)(2,1)}, bf16[1024,512]{1,0:T(8,128)(2,1)}, u32[]{:S(2)}, u32[]{:S(2)}) %collective-permute-start.43) | collective-permute-done | bytes 1048608 | tf_op jit(solution)/shard_map/ppermute | solution.py:313
  666.3 13.9 %outproj.5.refs_0_ = bf16[4,1024,2048]{2,1,0:T(8,128)(2,1)} custom-call(bf16[1024,512]{1,0:T(8,128)(2,1)} %get-tuple-element.157.o0, bf16[1024,512]{1,0:T(8,128)(2,1)} %copy-done.5, bf16[1024,512]{1,0:T(8,128)(2,1)} %collective-permute-done.42.o2, bf16[1024,512]{1,0:T(8,128)(2,1)} %collective-permute-done.43.o3, ...), custom_call_target="tpu_custom_call", output_to_operand_aliasing={{}: (9, {})} | custom-call | flops 8589934592 | bytes 20971520 | tf_op jit(solution)/shard_map/outproj/pallas_call | solution.py:281
  687.5 21.3 %collective-permute-done.40.o3 = bf16[1024,512]{1,0:T(8,128)(2,1)S(1)} collective-permute-done((bf16[1024,512]{1,0:T(8,128)(2,1)}, bf16[1024,512]{1,0:T(8,128)(2,1)S(1)}, u32[]{:S(2)}, u32[]{:S(2)}) %collective-permute-start.40) | collective-permute-done | bytes 1048608 | tf_op jit(solution)/shard_map/ppermute | solution.py:313
  709.7 13.9 %outproj.6.refs_0_ = bf16[4,1024,2048]{2,1,0:T(8,128)(2,1)} custom-call(bf16[1024,512]{1,0:T(8,128)(2,1)} %get-tuple-element.156.o0, bf16[1024,512]{1,0:T(8,128)(2,1)} %collective-permute-done.38.o1, bf16[1024,512]{1,0:T(8,128)(2,1)} %copy-done.6, bf16[1024,512]{1,0:T(8,128)(2,1)} %copy-done.8, ...), custom_call_target="tpu_custom_call", output_to_operand_aliasing={{}: (9, {})} | custom-call | flops 8589934592 | bytes 20971520 | tf_op jit(solution)/shard_map/outproj/pallas_call | solution.py:281
  732.5 20.6 %collective-permute-done.34.o3 = bf16[1024,512]{1,0:T(8,128)(2,1)} collective-permute-done((bf16[1024,512]{1,0:T(8,128)(2,1)}, bf16[1024,512]{1,0:T(8,128)(2,1)}, u32[]{:S(2)}, u32[]{:S(2)}) %collective-permute-start.34) | collective-permute-done | bytes 1048608 | tf_op jit(solution)/shard_map/ppermute | solution.py:313
  753.1 13.9 %outproj.7 = bf16[4,1024,2048]{2,1,0:T(8,128)(2,1)} custom-call(bf16[1024,512]{1,0:T(8,128)(2,1)} %get-tuple-element.153.o0, bf16[1024,512]{1,0:T(8,128)(2,1)} %copy-done.7, bf16[1024,512]{1,0:T(8,128)(2,1)} %collective-permute-done.33.o2, bf16[1024,512]{1,0:T(8,128)(2,1)} %collective-permute-done.34.o3, ...), custom_call_target="tpu_custom_call", output_to_operand_aliasing={{}: (9, {})} | custom-call | flops 8589934592 | bytes 20971520 | tf_op jit(solution)/shard_map/outproj/pallas_call | solution.py:281
  (155 shorter events, 164.4 us)
Async XLA Ops:
  9.2 98.8 %collective-permute-start.2 = (bf16[512,2048]{1,0:T(8,128)(2,1)}, bf16[512,2048]{1,0:T(8,128)(2,1)}, u32[]{:S(2)}, u32[]{:S(2)}) collective-permute-start(bf16[512,2048]{1,0:T(8,128)(2,1)} %get-tuple-element.175.h1_ref), channel_id=1, source_target_pairs={{0,2},{1,3},{2,0},{3,1},{4,6},{5,7},{6,4},{7,5}} | collective-permute-start | bytes 6291464 | tf_op jit(solution)/shard_map/ppermute | solution.py:313
  39.1 45.6 %collective-permute-start.3 = (bf16[512,2048]{1,0:T(8,128)(2,1)}, bf16[512,2048]{1,0:T(8,128)(2,1)S(1)}, u32[]{:S(2)}, u32[]{:S(2)}) collective-permute-start(bf16[512,2048]{1,0:T(8,128)(2,1)} %get-tuple-element.111.h0_ref), channel_id=1, source_target_pairs={{0,1},{1,0},{2,3},{3,2},{4,5},{5,4},{6,7},{7,6}} | collective-permute-start | bytes 6291464 | tf_op jit(solution)/shard_map/ppermute | solution.py:313
  39.4 46.6 %collective-permute-start.8 = (bf16[512,2048]{1,0:T(8,128)(2,1)}, bf16[512,2048]{1,0:T(8,128)(2,1)}, u32[]{:S(2)}, u32[]{:S(2)}) collective-permute-start(bf16[512,2048]{1,0:T(8,128)(2,1)} %get-tuple-element.112.h1_ref), channel_id=1, source_target_pairs={{0,1},{1,0},{2,3},{3,2},{4,5},{5,4},{6,7},{7,6}} | collective-permute-start | bytes 6291464 | tf_op jit(solution)/shard_map/ppermute | solution.py:313
  61.3 48.2 %collective-permute-start.1 = (bf16[512,2048]{1,0:T(8,128)(2,1)}, bf16[512,2048]{1,0:T(8,128)(2,1)}, u32[]{:S(2)}, u32[]{:S(2)}) collective-permute-start(bf16[512,2048]{1,0:T(8,128)(2,1)} %get-tuple-element.176.h0_ref), channel_id=1, source_target_pairs={{0,2},{1,3},{2,0},{3,1},{4,6},{5,7},{6,4},{7,5}} | collective-permute-start | bytes 6291464 | tf_op jit(solution)/shard_map/ppermute | solution.py:313
  110.0 50.4 %collective-permute-start = (bf16[512,2048]{1,0:T(8,128)(2,1)}, bf16[512,2048]{1,0:T(8,128)(2,1)}, u32[]{:S(2)}, u32[]{:S(2)}) collective-permute-start(bf16[512,2048]{1,0:T(8,128)(2,1)} %get-tuple-element.171.h0_ref), channel_id=1, source_target_pairs={{0,2},{1,3},{2,0},{3,1},{4,6},{5,7},{6,4},{7,5}} | collective-permute-start | bytes 6291464 | tf_op jit(solution)/shard_map/ppermute | solution.py:313
  160.5 70.3 %collective-permute-start.16 = (bf16[512,2048]{1,0:T(8,128)(2,1)}, bf16[512,2048]{1,0:T(8,128)(2,1)}, u32[]{:S(2)}, u32[]{:S(2)}) collective-permute-start(bf16[512,2048]{1,0:T(8,128)(2,1)} %collective-permute-done.h0_ref), channel_id=1, source_target_pairs={{0,1},{1,0},{2,3},{3,2},{4,5},{5,4},{6,7},{7,6}} | collective-permute-start | bytes 6291464 | tf_op jit(solution)/shard_map/ppermute | solution.py:313
  160.9 68.9 %collective-permute-start.11 = (bf16[512,2048]{1,0:T(8,128)(2,1)}, bf16[512,2048]{1,0:T(8,128)(2,1)}, u32[]{:S(2)}, u32[]{:S(2)}) collective-permute-start(bf16[512,2048]{1,0:T(8,128)(2,1)} %get-tuple-element.94.h1_ref), channel_id=1, source_target_pairs={{0,2},{1,3},{2,0},{3,1},{4,6},{5,7},{6,4},{7,5}} | collective-permute-start | bytes 6291464 | tf_op jit(solution)/shard_map/ppermute | solution.py:313
  229.8 49.8 %collective-permute-start.19 = (bf16[512,2048]{1,0:T(8,128)(2,1)}, bf16[512,2048]{1,0:T(8,128)(2,1)S(1)}, u32[]{:S(2)}, u32[]{:S(2)}) collective-permute-start(bf16[512,2048]{1,0:T(8,128)(2,1)} %get-tuple-element.111.h0_ref), channel_id=1, source_target_pairs={{0,2},{1,3},{2,0},{3,1},{4,6},{5,7},{6,4},{7,5}} | collective-permute-start | bytes 6291464 | tf_op jit(solution)/shard_map/ppermute | solution.py:313
  279.6 70.2 %collective-permute-start.23 = (bf16[512,2048]{1,0:T(8,128)(2,1)S(1)}, bf16[512,2048]{1,0:T(8,128)(2,1)}, u32[]{:S(2)}, u32[]{:S(2)}) collective-permute-start(bf16[512,2048]{1,0:T(8,128)(2,1)S(1)} %collective-permute-done.19.h0_ref), channel_id=1, source_target_pairs={{0,1},{1,0},{2,3},{3,2},{4,5},{5,4},{6,7},{7,6}} | collective-permute-start | bytes 6291464 | tf_op jit(solution)/shard_map/ppermute | solution.py:313
  280.1 68.4 %collective-permute-start.20 = (bf16[512,2048]{1,0:T(8,128)(2,1)}, bf16[512,2048]{1,0:T(8,128)(2,1)}, u32[]{:S(2)}, u32[]{:S(2)}) collective-permute-start(bf16[512,2048]{1,0:T(8,128)(2,1)} %get-tuple-element.112.h1_ref), channel_id=1, source_target_pairs={{0,2},{1,3},{2,0},{3,1},{4,6},{5,7},{6,4},{7,5}} | collective-permute-start | bytes 6291464 | tf_op jit(solution)/shard_map/ppermute | solution.py:313
  348.6 48.9 %collective-permute-start.18 = (bf16[512,2048]{1,0:T(8,128)(2,1)}, bf16[512,2048]{1,0:T(8,128)(2,1)}, u32[]{:S(2)}, u32[]{:S(2)}) collective-permute-start(bf16[512,2048]{1,0:T(8,128)(2,1)} %get-tuple-element.110.h0_ref), channel_id=1, source_target_pairs={{0,2},{1,3},{2,0},{3,1},{4,6},{5,7},{6,4},{7,5}} | collective-permute-start | bytes 6291464 | tf_op jit(solution)/shard_map/ppermute | solution.py:313
  397.5 69.3 %collective-permute-start.28 = (bf16[512,2048]{1,0:T(8,128)(2,1)}, bf16[512,2048]{1,0:T(8,128)(2,1)}, u32[]{:S(2)}, u32[]{:S(2)}) collective-permute-start(bf16[512,2048]{1,0:T(8,128)(2,1)} %collective-permute-done.18.h0_ref), channel_id=1, source_target_pairs={{0,1},{1,0},{2,3},{3,2},{4,5},{5,4},{6,7},{7,6}} | collective-permute-start | bytes 6291464 | tf_op jit(solution)/shard_map/ppermute | solution.py:313
  398.0 68.8 %collective-permute-start.25 = (bf16[512,2048]{1,0:T(8,128)(2,1)S(1)}, bf16[512,2048]{1,0:T(8,128)(2,1)}, u32[]{:S(2)}, u32[]{:S(2)}) collective-permute-start(bf16[512,2048]{1,0:T(8,128)(2,1)S(1)} %copy-done.4), channel_id=1, source_target_pairs={{0,2},{1,3},{2,0},{3,1},{4,6},{5,7},{6,4},{7,5}} | collective-permute-start | bytes 6291464 | tf_op jit(solution)/shard_map/ppermute | solution.py:313
  501.4 71.3 %collective-permute-start.44 = (bf16[1024,512]{1,0:T(8,128)(2,1)}, bf16[1024,512]{1,0:T(8,128)(2,1)S(1)}, u32[]{:S(2)}, u32[]{:S(2)}) collective-permute-start(bf16[1024,512]{1,0:T(8,128)(2,1)} %get-tuple-element.178), channel_id=1, source_target_pairs={{0,1},{1,0},{2,3},{3,2},{4,5},{5,4},{6,7},{7,6}} | collective-permute-start | bytes 3145736 | tf_op jit(solution)/shard_map/ppermute | solution.py:313
  502.3 68.6 %collective-permute-start.36 = (bf16[512,2048]{1,0:T(8,128)(2,1)S(1)}, bf16[512,2048]{1,0:T(8,128)(2,1)}, u32[]{:S(2)}, u32[]{:S(2)}) collective-permute-start(bf16[512,2048]{1,0:T(8,128)(2,1)S(1)} %copy-done.1), channel_id=1, source_target_pairs={{0,2},{1,3},{2,0},{3,1},{4,6},{5,7},{6,4},{7,5}} | collective-permute-start | bytes 6291464 | tf_op jit(solution)/shard_map/ppermute | solution.py:313
  503.2 122.1 %collective-permute-start.35 = (bf16[512,2048]{1,0:T(8,128)(2,1)S(1)}, bf16[512,2048]{1,0:T(8,128)(2,1)}, u32[]{:S(2)}, u32[]{:S(2)}) collective-permute-start(bf16[512,2048]{1,0:T(8,128)(2,1)S(1)} %copy-done.1), channel_id=1, source_target_pairs={{0,1},{1,0},{2,3},{3,2},{4,5},{5,4},{6,7},{7,6}} | collective-permute-start | bytes 6291464 | tf_op jit(solution)/shard_map/ppermute | solution.py:313
  570.9 55.4 %collective-permute-start.37 = (bf16[512,2048]{1,0:T(8,128)(2,1)}, bf16[512,2048]{1,0:T(8,128)(2,1)}, u32[]{:S(2)}, u32[]{:S(2)}) collective-permute-start(bf16[512,2048]{1,0:T(8,128)(2,1)} %collective-permute-done.36.w2), channel_id=1, source_target_pairs={{0,1},{1,0},{2,3},{3,2},{4,5},{5,4},{6,7},{7,6}} | collective-permute-start | bytes 6291464 | tf_op jit(solution)/shard_map/ppermute | solution.py:313
  572.5 46.3 %collective-permute-start.46 = (bf16[1024,512]{1,0:T(8,128)(2,1)}, bf16[1024,512]{1,0:T(8,128)(2,1)S(1)}, u32[]{:S(2)}, u32[]{:S(2)}) collective-permute-start(bf16[1024,512]{1,0:T(8,128)(2,1)} %constant_dynamic-slice_fusion.15), channel_id=1, source_target_pairs={{0,3},{1,2},{2,1},{3,0},{4,7},{5,6},{6,5},{7,4}} | collective-permute-start | bytes 3145736 | tf_op jit(solution)/shard_map/ppermute | solution.py:313
  573.7 46.9 %collective-permute-start.41 = (bf16[1024,512]{1,0:T(8,128)(2,1)}, bf16[1024,512]{1,0:T(8,128)(2,1)S(1)}, u32[]{:S(2)}, u32[]{:S(2)}) collective-permute-start(bf16[1024,512]{1,0:T(8,128)(2,1)} %get-tuple-element.182), channel_id=1, source_target_pairs={{0,1},{1,0},{2,3},{3,2},{4,5},{5,4},{6,7},{7,6}} | collective-permute-start | bytes 3145736 | tf_op jit(solution)/shard_map/ppermute | solution.py:313
  625.3 62.2 %collective-permute-start.39 = (bf16[1024,512]{1,0:T(8,128)(2,1)}, bf16[1024,512]{1,0:T(8,128)(2,1)S(1)}, u32[]{:S(2)}, u32[]{:S(2)}) collective-permute-start(bf16[1024,512]{1,0:T(8,128)(2,1)} %get-tuple-element.185), channel_id=1, source_target_pairs={{0,2},{1,3},{2,0},{3,1},{4,6},{5,7},{6,4},{7,5}} | collective-permute-start | bytes 3145736 | tf_op jit(solution)/shard_map/ppermute | solution.py:313
  626.3 82.4 %collective-permute-start.40 = (bf16[1024,512]{1,0:T(8,128)(2,1)}, bf16[1024,512]{1,0:T(8,128)(2,1)S(1)}, u32[]{:S(2)}, u32[]{:S(2)}) collective-permute-start(bf16[1024,512]{1,0:T(8,128)(2,1)} %get-tuple-element.184), channel_id=1, source_target_pairs={{0,3},{1,2},{2,1},{3,0},{4,7},{5,6},{6,5},{7,4}} | collective-permute-start | bytes 3145736 | tf_op jit(solution)/shard_map/ppermute | solution.py:313
  642.6 81.0 %collective-permute-start.32 = (bf16[1024,512]{1,0:T(8,128)(2,1)}, bf16[1024,512]{1,0:T(8,128)(2,1)S(1)}, u32[]{:S(2)}, u32[]{:S(2)}) collective-permute-start(bf16[1024,512]{1,0:T(8,128)(2,1)} %get-tuple-element.190), channel_id=1, source_target_pairs={{0,1},{1,0},{2,3},{3,2},{4,5},{5,4},{6,7},{7,6}} | collective-permute-start | bytes 3145736 | tf_op jit(solution)/shard_map/ppermute | solution.py:313
  663.8 68.7 %collective-permute-start.33 = (bf16[1024,512]{1,0:T(8,128)(2,1)}, bf16[1024,512]{1,0:T(8,128)(2,1)}, u32[]{:S(2)}, u32[]{:S(2)}) collective-permute-start(bf16[1024,512]{1,0:T(8,128)(2,1)} %get-tuple-element.189), channel_id=1, source_target_pairs={{0,2},{1,3},{2,0},{3,1},{4,6},{5,7},{6,4},{7,5}} | collective-permute-start | bytes 3145736 | tf_op jit(solution)/shard_map/ppermute | solution.py:313
  664.7 88.4 %collective-permute-start.34 = (bf16[1024,512]{1,0:T(8,128)(2,1)}, bf16[1024,512]{1,0:T(8,128)(2,1)}, u32[]{:S(2)}, u32[]{:S(2)}) collective-permute-start(bf16[1024,512]{1,0:T(8,128)(2,1)} %get-tuple-element.188), channel_id=1, source_target_pairs={{0,3},{1,2},{2,1},{3,0},{4,7},{5,6},{6,5},{7,4}} | collective-permute-start | bytes 3145736 | tf_op jit(solution)/shard_map/ppermute | solution.py:313
  (42 other events, 680.2 us)

commit v4 on v3

--- a/solution.py
+++ b/solution.py
@@ -26,11 +26,15 @@
 
 
 def rope_tables(seq_len):
-    half_dim = HD // 2
-    inv_freq = 10000.0 ** (-jnp.arange(half_dim, dtype=F32) * (2.0 / HD))
-    angles = jnp.arange(seq_len, dtype=F32)[:, None] * inv_freq[None, :]
-    c, s = jnp.cos(angles), jnp.sin(angles)
-    return jnp.concatenate([c, c], axis=1), jnp.concatenate([-s, s], axis=1)
+    fine = 64
+    lane = jnp.arange(HD)
+    inv_freq = 10000.0 ** (-(lane % (HD // 2)).astype(F32) * (2.0 / HD))
+    low = jnp.arange(fine, dtype=F32)[:, None] * inv_freq[None, :]
+    high = (jnp.arange(seq_len // fine) * fine).astype(F32)[:, None] * inv_freq[None, :]
+    cl, sl, ch, sh = lax.optimization_barrier((jnp.cos(low)[None], jnp.sin(low)[None], jnp.cos(high)[:, None], jnp.sin(high)[:, None]))
+    c = (ch * cl - sh * sl).reshape(seq_len, HD)
+    s = (sh * cl + ch * sl).reshape(seq_len, HD)
+    return c, jnp.where(lane < HD // 2, -s, s)
 
 
 def sq_sum(a):
@@ -47,6 +51,38 @@
     for g, t in enumerate(blocks):
         scr[pl.ds(g, rows, stride=n), :] = t
     return scr[...].astype(BF16)
+
+
+def norm_kernel(x_ref, g_ref, a_ref, b_ref):
+    x = x_ref[0].astype(F32)
+    mean = jnp.sum(x * x, axis=1, keepdims=True) * (1.0 / x.shape[1])
+    h = (x * lax.rsqrt(mean + 1e-5) * g_ref[...]).astype(BF16)
+    lower = pl.program_id(0) < pl.num_programs(0) // 2
+
+    @pl.when(lower)
+    def _():
+        a_ref[...] = h
+
+    @pl.when(jnp.logical_not(lower))
+    def _():
+        b_ref[...] = h
+
+
+def norm_call(x, gain, b):
+    rows, width = x.shape[1:]
+    br = 256
+    n = rows // br
+    half = jax.ShapeDtypeStruct((rows // 2, width), BF16)
+    return pl.pallas_call(
+        norm_kernel,
+        grid=(n,),
+        in_specs=[pl.BlockSpec((1, br, width), lambda s: (b, s, 0)), pl.BlockSpec((1, width), lambda s: (0, 0))],
+        out_specs=[pl.BlockSpec((br, width), lambda s: (jnp.minimum(s, n // 2 - 1), 0)), pl.BlockSpec((br, width), lambda s: (jnp.maximum(s - n // 2, 0), 0))],
+        out_shape=[half, half],
+        compiler_params=params("arbitrary"),
+        cost_estimate=cost(8 * rows * width, 4 * rows * width),
+        name="norm",
+    )(x, gain)
 
 
 def qkv_kernel(n_sub, me_ref, h0_ref, h1_ref, h2_ref, h3_ref, wq_ref, wk_ref, wv_ref, *refs):
@@ -255,38 +291,58 @@
     )(q, k, vt)
 
 
-def out_kernel(o0, o1, o2, o3, w0, w1, w2, w3, x_ref, *refs):
-    out_ref = refs[-1]
-    acc = jnp.dot(o0[...], w0[...], preferred_element_type=F32)
-    for o, w in ((o1, w1), (o2, w2), (o3, w3)):
-        acc += jnp.dot(o[...], w[...], preferred_element_type=F32)
+def out_kernel(n_items, *refs):
+    pieces, (w0, w1, w2, w3, x_ref) = refs[:4 * n_items], refs[4 * n_items:4 * n_items + 5]
+    out_ref, o_buf, sems = refs[-3:]
+    item, n = pl.program_id(0), pl.program_id(1)
+
+    def loads(t):
+        return [pltpu.make_async_copy(pieces[4 * t + r], o_buf.at[t % 2, r], sems.at[t % 2, r]) for r in range(4)]
+
+    for t in range(n_items):
+        @pl.when((item == max(t - 1, 0)) & (n == (1 if t else 0)))
+        def _(t=t):
+            for load in loads(t):
+                load.start()
+
+        @pl.when((item == t) & (n == 0))
+        def _(t=t):
+            for load in loads(t):
+                load.wait()
+
+    slot = item % 2
+    acc = jnp.dot(o_buf[slot, 0], w0[...], preferred_element_type=F32)
+    for r, w in ((1, w1), (2, w2), (3, w3)):
+        acc += jnp.dot(o_buf[slot, r], w[...], preferred_element_type=F32)
     y = acc.astype(BF16).astype(F32)
     out_ref[0] = (x_ref[0].astype(F32) + y).astype(BF16)
 
 
-def out_call(os, ws, x, prev, b):
-    _, rows, width = x.shape
-    cols = os[0].shape[1]
+def out_call(items, ws, x, prev, b, part):
+    width = x.shape[2]
+    n_items = len(items)
+    rows, cols = items[0][0].shape
     bn = 512
-    ospec = pl.BlockSpec((rows, cols), lambda n: (0, 0))
-    wspec = pl.BlockSpec((cols, bn), lambda n: (0, n))
-    xspec = pl.BlockSpec((1, rows, bn), lambda n: (b, 0, n))
-    in_specs = [ospec] * 4 + [wspec] * 4 + [xspec]
-    args = [*os, *ws, x]
+    hbm = pl.BlockSpec(memory_space=pl.ANY)
+    wspec = pl.BlockSpec((cols, bn), lambda t, n: (0, n))
+    xspec = pl.BlockSpec((1, rows, bn), lambda t, n: (b + t, part, n))
+    in_specs = [hbm] * (4 * n_items) + [wspec] * 4 + [xspec]
+    args = [*sum(items, []), *ws, x]
     aliases = {}
     if prev is not None:
-        in_specs.append(pl.BlockSpec(memory_space=pl.ANY))
+        aliases = {len(args): 0}
+        in_specs.append(hbm)
         args.append(prev)
-        aliases = {9: 0}
     return pl.pallas_call(
-        out_kernel,
-        grid=(width // bn,),
+        functools.partial(out_kernel, n_items),
+        grid=(n_items, width // bn),
         in_specs=in_specs,
         out_specs=xspec,
         out_shape=jax.ShapeDtypeStruct(x.shape, BF16),
+        scratch_shapes=[pltpu.VMEM((2, 4, rows, cols), BF16), pltpu.SemaphoreType.DMA((2, 4))],
         input_output_aliases=aliases,
-        compiler_params=params("arbitrary"),
-        cost_estimate=cost(2 * rows * width * width, 2 * (width * width + 3 * rows * width)),
+        compiler_params=params("arbitrary", "arbitrary"),
+        cost_estimate=cost(2 * n_items * rows * width * width, n_items * (2 * width * width + 6 * rows * width)),
         name="outproj",
     )(*args)
 
@@ -312,16 +368,10 @@
         def send(val, hop):
             return lax.ppermute(val, 'tp', pairs[hop])
 
-        half = rows // 2
+        gain = attn_gain.reshape(1, width)
         own = []
         for b in range(n_batch):
-            xs = x_local if b == 0 else after(x_local, own[0][0])
-            parts = []
-            for p in range(2):
-                xf = xs[b, p * half:(p + 1) * half].astype(F32)
-                inv_rms = lax.rsqrt(jnp.mean(xf * xf, axis=-1, keepdims=True) + 1e-5)
-                parts.append((xf * inv_rms * attn_gain).astype(BF16))
-            own.append(parts)
+            own.append(norm_call(x_local, after(gain, own[-1][0]) if own else gain, b))
         far = [[None, None] for _ in own]
 
         def push(b, p, *deps):
@@ -357,13 +407,11 @@
             o = attn_call(qr, kr, vt)
             return o, kc
 
-        def cut(o, r):
-            return lax.dynamic_slice_in_dim(o, (me ^ r) * rows, rows, axis=0)
-
-        def exchange(o, dep):
+        def exchange(o, dep, n_parts=1):
             o = after(o, dep)
-            pieces = [cut(o, r) for r in range(n_tp)]
-            return [pieces[0]] + [send(pieces[r], r) for r in range(1, n_tp)]
+            size = rows // n_parts
+            pieces = [[lax.dynamic_slice_in_dim(o, (me ^ r) * rows + p * size, size, axis=0) for r in range(n_tp)] for p in range(n_parts)]
+            return [[cut[0]] + [send(cut[r], r) for r in range(1, n_tp)] for cut in pieces]
 
         vc = early(0, None)
         vc = early(1, vc, vc, ct, st)
@@ -373,33 +421,38 @@
         push(1, 1, done)
         push(2, 0, done)
         vc = early(3, vc, done)
+        w_cut = [0, cols // 2, 3 * cols // 4, cols]
+
+        def push_w(n, dep):
+            return send(after(wo_rows, dep)[w_cut[n]:w_cut[n + 1]], 2)
+
+        w2 = [push_w(0, done)]
         o0, kc = attend(0, kc, vc)
-        pos0 = [cut(o0, r) for r in range(3)]
-        pos0 = [pos0[0], send(pos0[1], 1), send(pos0[2], 2)]
         vc = project(1, vc, o0)
         done = late[1][3]
         push(2, 1, done)
         push(3, 0, done)
-        piece = cut(after(o0, done), 3)
-        ex.append(pos0 + [send(piece, 3)])
-        o1, kc = attend(1, kc, piece)
+        w2.append(push_w(1, done))
+        ex.append(exchange(o0, done))
+        o1, kc = attend(1, kc, ex[0][0][0])
         vc = project(2, vc, o1)
         done = late[2][3]
         push(3, 1, done)
+        w2.append(push_w(2, done))
         ex.append(exchange(o1, done))
-        o2, kc = attend(2, kc, ex[1][0])
+        o2, kc = attend(2, kc, ex[1][0][0])
         vc = project(3, vc, o2)
         done = late[3][3]
-        wo_late = after(wo_rows, done)
-        w2 = send(wo_late, 2)
-        ws = [wo_rows, send(wo_late, 1), w2]
         ex.append(exchange(o2, done))
-        o3, kc = attend(3, kc, ex[2][0])
-        ws.append(send(after(w2, o3), 1))
-        ex.append(exchange(o3, o3))
-        for b, pos in enumerate(ex):
-            pos = [after(pos[0], o3), *pos[1:]]
-            out = out_call(pos, ws, x_local, out, b)
+        o3, kc = attend(3, kc, ex[2][0][0])
+        ex.append(exchange(o3, o3, 2))
+        w2 = jnp.concatenate([after(w2[0], ex[3][0][0]), *w2[1:]], axis=0)
+        ws = [wo_rows, send(after(wo_rows, done), 1), w2, send(w2, 1)]
+        first = [list(parts[0]) for parts in ex[:-1]]
+        first[0][0] = after(first[0][0], ex[3][0][0])
+        out = out_call(first, ws, x_local, None, 0, 0)
+        for p, pos in enumerate(ex[-1]):
+            out = out_call([pos], ws, x_local, out, n_batch - 1, p)
         shape = (n_batch, seq, cols // HD, HD)
         return (out, kc.reshape(shape), vc.reshape(shape))
 

time: 777 us -> 752 us (0.968)
  other arithmetic: 37.6 us -> 6.4 us
  waiting for transfers between devices: 178 us -> 152 us
  Pallas kernels: 498 us -> 521 us
  local copies, waits for them, and re-layouts: 22.3 us -> 30.1 us
    ppermute x47 -> x52, waiting for transfers between devices: 178 us -> 152 us  [send(): return lax.ppermute(val, 'tp', pairs[hop])]
    pallas_call x4 -> x7, Pallas kernels: 55.4 us -> 78 us  [the longest x3 54.6 us: out_call(): pl.pallas_call(functools.partial(out_kernel, n_items), grid=(n_items, wid...]
    convert_element_type x2 -> x1, other arithmetic: 10.5 us -> 0.01 us  [rope_tables(): (jnp.arange(seq_len // fine) * fine).astype(F32)[:, None]]
    reduce_sum x2 -> x0, other arithmetic: 9.01 us -> none  [block(): inv_rms = lax.rsqrt(jnp.mean(xf * xf, axis=-1, keepdims=True) + 1e-05)]
    neg x1 -> x0, other arithmetic: 8.78 us -> none  [rope_tables(): return (jnp.concatenate([c, c], axis=1), jnp.concatenate([-s, s], axis=1))]
    ppermute x47 -> x52, starting transfers between devices: 29.5 us -> 32.1 us  [send(): return lax.ppermute(val, 'tp', pairs[hop])]
    dynamic_slice x5 -> x4, local copies, waits for them, and re-layouts: 17.2 us -> 16.4 us  [exchange(): lax.dynamic_slice_in_dim(o, (me ^ r) * rows + p * size, size, axis=0)]
  transfers between devices with their start and end apart: 47 -> 52, of which waited for: 16 -> 12; matrix products, arithmetic and copies ran while one was open for 6% -> 4% of each run, Pallas kernels for 60% -> 65%
where the time goes in v4:
time: 752 us; the launch traced here: 743 us
  Pallas kernels  521 us (69%)
  waiting for transfers between devices  152 us (20%)
  starting transfers between devices  32.1 us (4%)
  local copies, waits for them, and re-layouts  30.1 us (4%)
    pallas_call x4, Pallas kernels, attn_call(): pl.pallas_call(functools.partial(attn_kernel, n_h, bq, ch), grid=(cols //...  215 us
    pallas_call x8, Pallas kernels, qkv_call(): pl.pallas_call(functools.partial(qkv_kernel, n_sub), grid_spec=pltpu.Pref...  175 us
    ppermute x52, waiting for transfers between devices, send(): return lax.ppermute(val, 'tp', pairs[hop])  152 us
    pallas_call x3, Pallas kernels, out_call(): pl.pallas_call(functools.partial(out_kernel, n_items), grid=(n_items, wid...  54.6 us
    pallas_call x4, Pallas kernels, rope_call(): pl.pallas_call(functools.partial(rope_kernel, width), grid=(nq,), in_spec...  53 us
    ppermute x52, starting transfers between devices, send(): return lax.ppermute(val, 'tp', pairs[hop])  32.1 us
    pallas_call x4, Pallas kernels, norm_call(): pl.pallas_call(norm_kernel, grid=(n,), in_specs=[pl.BlockSpec((1, br, wid...  23.4 us
    dynamic_slice x4, local copies, waits for them, and re-layouts, exchange(): lax.dynamic_slice_in_dim(o, (me ^ r) * rows + p * size, size, axis=0)  16.4 us
  transfers between devices with their start and end apart: 52, of which 12 were waited for; matrix products, arithmetic and copies ran while one was open for 4% of the time, Pallas kernels for 65%

profile of v4, /device:TPU:0, one launch (start us, length us, event | category | flops | bytes accessed | tf_op | source)
XLA Modules:
  0.0 742.8 jit_solution(15376611160408195132)
XLA Ops:
  27.1 21.8 %qkv.8 = (bf16[4096,512]{1,0:T(8,128)(2,1)}, bf16[4096,512]{1,0:T(8,128)(2,1)}, bf16[512,4096]{1,0:T(8,128)(2,1)}, bf16[65536,128]{1,0:T(8,128)(2,1)}, f32[2,4096]{1,0:T(2,128)}) custom-call(s32[1]{0:T(128)} %bitcast.me_ref, bf16[512,2048]{1,0:T(8,128)(2,1)} %get-tuple-element.95.h0_ref, bf16[512,2048]{1,0:T(8,128)(2,1)} %get-tuple-element.103.h1_ref, ...), custom_call_target="tpu_custom_call" | custom-call | flops 12884901888 | bytes 23068672 | tf_op jit(solution)/shard_map/qkv/pallas_call | solution.py:132
  48.9 21.9 %qkv.9 = (bf16[4096,512]{1,0:T(8,128)(2,1)}, bf16[4096,512]{1,0:T(8,128)(2,1)}, bf16[512,4096]{1,0:T(8,128)(2,1)}, bf16[65536,128]{1,0:T(8,128)(2,1)}, f32[2,4096]{1,0:T(2,128)}) custom-call(s32[1]{0:T(128)} %bitcast.me_ref, bf16[512,2048]{1,0:T(8,128)(2,1)} %get-tuple-element.97.h0_ref, ...), custom_call_target="tpu_custom_call", output_to_operand_aliasing={{3}: (8, {})} | custom-call | flops 12884901888 | bytes 23068672 | tf_op jit(solution)/shard_map/qkv/pallas_call | solution.py:132
  70.9 21.9 %qkv.10 = (bf16[4096,512]{1,0:T(8,128)(2,1)}, bf16[4096,512]{1,0:T(8,128)(2,1)}, bf16[512,4096]{1,0:T(8,128)(2,1)}, bf16[65536,128]{1,0:T(8,128)(2,1)}, f32[2,4096]{1,0:T(2,128)}) custom-call(s32[1]{0:T(128)} %bitcast.me_ref, bf16[512,2048]{1,0:T(8,128)(2,1)} %get-tuple-element.138.h0_ref, ...), custom_call_target="tpu_custom_call", output_to_operand_aliasing={{3}: (8, {})} | custom-call | flops 12884901888 | bytes 23068672 | tf_op jit(solution)/shard_map/qkv/pallas_call | solution.py:132
  109.5 21.8 %qkv.11 = (bf16[4096,512]{1,0:T(8,128)(2,1)}, bf16[4096,512]{1,0:T(8,128)(2,1)}, bf16[512,4096]{1,0:T(8,128)(2,1)}, bf16[65536,128]{1,0:T(8,128)(2,1)}, f32[2,4096]{1,0:T(2,128)}) custom-call(s32[1]{0:T(128)} %bitcast.me_ref, ...), custom_call_target="tpu_custom_call", output_to_operand_aliasing={{0}: (8, {}), {1}: (9, {}), {2}: (10, {}), {3}: (11, {}), {... | custom-call | flops 12884901888 | bytes 23068672 | tf_op jit(solution)/shard_map/qkv/pallas_call | solution.py:132
  132.9 22.4 %qkv.12 = (bf16[4096,512]{1,0:T(8,128)(2,1)}, bf16[4096,512]{1,0:T(8,128)(2,1)}, bf16[512,4096]{1,0:T(8,128)(2,1)}, bf16[65536,128]{1,0:T(8,128)(2,1)}, f32[2,4096]{1,0:T(2,128)}) custom-call(s32[1]{0:T(128)} %bitcast.me_ref, bf16[512,2048]{1,0:T(8,128)(2,1)} %get-tuple-element.137.h0_ref, ...), custom_call_target="tpu_custom_call", output_to_operand_aliasing={{3}: (8, {})} | custom-call | flops 12884901888 | bytes 23068672 | tf_op jit(solution)/shard_map/qkv/pallas_call | solution.py:132
  159.6 13.3 %rope.4 = (bf16[4096,512]{1,0:T(8,128)(2,1)}, bf16[4096,512]{1,0:T(8,128)(2,1)}, bf16[65536,128]{1,0:T(8,128)(2,1)}) custom-call(bf16[4096,512]{1,0:T(8,128)(2,1)} %get-tuple-element.121.q_ref, bf16[4096,512]{1,0:T(8,128)(2,1)} %get-tuple-element.122.k_ref, f32[2,4096]{1,0:T(2,128)} %add.107.ss_ref, f32[1,512]{1,0:T(1,128)} %bitcast.26, f32[1,512]{1,0:T(1,128)} %bitcast.30, ...), custom_call_target="tpu_custom_call" | custom-call | flops 7000000000 | bytes 20971520 | tf_op jit(solution)/shard_map/rope/pallas_call | solution.py:198
  173.0 53.6 %attn.4 = bf16[4096,512]{1,0:T(8,128)(2,1)} custom-call(bf16[4096,512]{1,0:T(8,128)(2,1)} %get-tuple-element.128.q_ref, bf16[4096,512]{1,0:T(8,128)(2,1)} %get-tuple-element.129.k_ref, bf16[512,4096]{1,0:T(8,128)(2,1)} %get-tuple-element.130.vt_ref), custom_call_target="tpu_custom_call" | custom-call | flops 34359738368 | bytes 16777216 | tf_op jit(solution)/shard_map/attn/pallas_call | solution.py:280
  232.2 21.8 %qkv.13 = (bf16[4096,512]{1,0:T(8,128)(2,1)}, bf16[4096,512]{1,0:T(8,128)(2,1)}, bf16[512,4096]{1,0:T(8,128)(2,1)}, bf16[65536,128]{1,0:T(8,128)(2,1)}, f32[2,4096]{1,0:T(2,128)}) custom-call(s32[1]{0:T(128)} %bitcast.me_ref, ...), custom_call_target="tpu_custom_call", output_to_operand_aliasing={{0}: (8, {}), {1}: (9, {}), {2}: (10, {}), {3}: (11, {}), {... | custom-call | flops 12884901888 | bytes 23068672 | tf_op jit(solution)/shard_map/qkv/pallas_call | solution.py:132
  258.7 16.9 %collective-permute-done.21 = f32[2,4096]{1,0:T(2,128)S(1)} collective-permute-done((f32[2,4096]{1,0:T(2,128)}, f32[2,4096]{1,0:T(2,128)S(1)}, u32[]{:S(2)}, u32[]{:S(2)}) %collective-permute-start.21) | collective-permute-done | bytes 32800 | tf_op jit(solution)/shard_map/ppermute | solution.py:369
  277.4 13.2 %rope.5 = (bf16[4096,512]{1,0:T(8,128)(2,1)}, bf16[4096,512]{1,0:T(8,128)(2,1)}, bf16[65536,128]{1,0:T(8,128)(2,1)}) custom-call(bf16[4096,512]{1,0:T(8,128)(2,1)} %get-tuple-element.140.q_ref, bf16[4096,512]{1,0:T(8,128)(2,1)} %get-tuple-element.141.k_ref, f32[2,4096]{1,0:T(2,128)} %add.110.ss_ref, ...), custom_call_target="tpu_custom_call", output_to_operand_aliasing={{2}: (7, {})} | custom-call | flops 7000000000 | bytes 20971520 | tf_op jit(solution)/shard_map/rope/pallas_call | solution.py:198
  290.6 53.6 %attn.5 = bf16[4096,512]{1,0:T(8,128)(2,1)} custom-call(bf16[4096,512]{1,0:T(8,128)(2,1)} %get-tuple-element.145.q_ref, bf16[4096,512]{1,0:T(8,128)(2,1)} %get-tuple-element.146.k_ref, bf16[512,4096]{1,0:T(8,128)(2,1)} %get-tuple-element.147.vt_ref), custom_call_target="tpu_custom_call" | custom-call | flops 34359738368 | bytes 16777216 | tf_op jit(solution)/shard_map/attn/pallas_call | solution.py:280
  349.9 22.0 %qkv.14 = (bf16[4096,512]{1,0:T(8,128)(2,1)}, bf16[4096,512]{1,0:T(8,128)(2,1)}, bf16[512,4096]{1,0:T(8,128)(2,1)}, bf16[65536,128]{1,0:T(8,128)(2,1)}, f32[2,4096]{1,0:T(2,128)}) custom-call(s32[1]{0:T(128)} %bitcast.me_ref, ...), custom_call_target="tpu_custom_call", output_to_operand_aliasing={{0}: (8, {}), {1}: (9, {}), {2}: (10, {}), {3}: (11, {}), {... | custom-call | flops 12884901888 | bytes 23068672 | tf_op jit(solution)/shard_map/qkv/pallas_call | solution.py:132
  377.5 15.7 %collective-permute-done.26 = f32[2,4096]{1,0:T(2,128)S(1)} collective-permute-done((f32[2,4096]{1,0:T(2,128)}, f32[2,4096]{1,0:T(2,128)S(1)}, u32[]{:S(2)}, u32[]{:S(2)}) %collective-permute-start.26) | collective-permute-done | bytes 32800 | tf_op jit(solution)/shard_map/ppermute | solution.py:369
  395.7 13.3 %rope.6 = (bf16[4096,512]{1,0:T(8,128)(2,1)}, bf16[4096,512]{1,0:T(8,128)(2,1)}, bf16[65536,128]{1,0:T(8,128)(2,1)}) custom-call(bf16[4096,512]{1,0:T(8,128)(2,1)} %get-tuple-element.156.q_ref, bf16[4096,512]{1,0:T(8,128)(2,1)} %get-tuple-element.157.k_ref, f32[2,4096]{1,0:T(2,128)} %add.112.ss_ref, ...), custom_call_target="tpu_custom_call", output_to_operand_aliasing={{2}: (7, {})} | custom-call | flops 7000000000 | bytes 20971520 | tf_op jit(solution)/shard_map/rope/pallas_call | solution.py:198
  409.0 53.6 %attn.6 = bf16[4096,512]{1,0:T(8,128)(2,1)} custom-call(bf16[4096,512]{1,0:T(8,128)(2,1)} %get-tuple-element.161.q_ref, bf16[4096,512]{1,0:T(8,128)(2,1)} %get-tuple-element.162.k_ref, bf16[512,4096]{1,0:T(8,128)(2,1)} %get-tuple-element.163.vt_ref), custom_call_target="tpu_custom_call" | custom-call | flops 34359738368 | bytes 16777216 | tf_op jit(solution)/shard_map/attn/pallas_call | solution.py:280
  468.3 21.8 %qkv.15 = (bf16[4096,512]{1,0:T(8,128)(2,1)}, bf16[4096,512]{1,0:T(8,128)(2,1)}, bf16[512,4096]{1,0:T(8,128)(2,1)}, bf16[65536,128]{1,0:T(8,128)(2,1)}, f32[2,4096]{1,0:T(2,128)}) custom-call(s32[1]{0:T(128)} %bitcast.me_ref, ...), custom_call_target="tpu_custom_call", output_to_operand_aliasing={{0}: (8, {}), {1}: (9, {}), {2}: (10, {}), {3}: (11, {}), {... | custom-call | flops 12884901888 | bytes 23068672 | tf_op jit(solution)/shard_map/qkv/pallas_call | solution.py:132
  501.6 13.2 %rope.7 = (bf16[4096,512]{1,0:T(8,128)(2,1)}, bf16[4096,512]{1,0:T(8,128)(2,1)}, bf16[65536,128]{1,0:T(8,128)(2,1)}) custom-call(bf16[4096,512]{1,0:T(8,128)(2,1)} %get-tuple-element.170.q_ref, bf16[4096,512]{1,0:T(8,128)(2,1)} %get-tuple-element.171.k_ref, f32[2,4096]{1,0:T(2,128)} %add.114.ss_ref, ...), custom_call_target="tpu_custom_call", output_to_operand_aliasing={{2}: (7, {})} | custom-call | flops 7000000000 | bytes 20971520 | tf_op jit(solution)/shard_map/rope/pallas_call | solution.py:198
  514.9 53.8 %attn.7 = bf16[4096,512]{1,0:T(8,128)(2,1)} custom-call(bf16[4096,512]{1,0:T(8,128)(2,1)} %get-tuple-element.176.q_ref, bf16[4096,512]{1,0:T(8,128)(2,1)} %get-tuple-element.177.k_ref, bf16[512,4096]{1,0:T(8,128)(2,1)} %get-tuple-element.178.vt_ref), custom_call_target="tpu_custom_call" | custom-call | flops 34359738368 | bytes 16777216 | tf_op jit(solution)/shard_map/attn/pallas_call | solution.py:280
  578.7 11.1 %collective-permute-done.38 = bf16[128,2048]{1,0:T(8,128)(2,1)S(1)} collective-permute-done((bf16[128,2048]{1,0:T(8,128)(2,1)S(1)}, bf16[128,2048]{1,0:T(8,128)(2,1)S(1)}, u32[]{:S(2)}, u32[]{:S(2)}) %collective-permute-start.38) | collective-permute-done | bytes 524320 | tf_op jit(solution)/shard_map/ppermute | solution.py:369
  590.5 21.8 %collective-permute-done.47.refs_6_ = bf16[1024,512]{1,0:T(8,128)(2,1)S(1)} collective-permute-done((bf16[1024,512]{1,0:T(8,128)(2,1)S(1)}, bf16[1024,512]{1,0:T(8,128)(2,1)S(1)}, u32[]{:S(2)}, u32[]{:S(2)}) %collective-permute-start.47) | collective-permute-done | bytes 1048608 | tf_op jit(solution)/shard_map/ppermute | solution.py:369
  612.4 21.3 %collective-permute-done.48.refs_7_ = bf16[1024,512]{1,0:T(8,128)(2,1)S(1)} collective-permute-done((bf16[1024,512]{1,0:T(8,128)(2,1)S(1)}, bf16[1024,512]{1,0:T(8,128)(2,1)S(1)}, u32[]{:S(2)}, u32[]{:S(2)}) %collective-permute-start.48) | collective-permute-done | bytes 1048608 | tf_op jit(solution)/shard_map/ppermute | solution.py:369
  636.9 22.9 %collective-permute-done.50.refs_10_ = bf16[1024,512]{1,0:T(8,128)(2,1)S(1)} collective-permute-done((bf16[1024,512]{1,0:T(8,128)(2,1)S(1)}, bf16[1024,512]{1,0:T(8,128)(2,1)S(1)}, u32[]{:S(2)}, u32[]{:S(2)}) %collective-permute-start.50) | collective-permute-done | bytes 1048608 | tf_op jit(solution)/shard_map/ppermute | solution.py:369
  659.7 21.4 %collective-permute-done.51.refs_11_ = bf16[1024,512]{1,0:T(8,128)(2,1)S(1)} collective-permute-done((bf16[1024,512]{1,0:T(8,128)(2,1)S(1)}, bf16[1024,512]{1,0:T(8,128)(2,1)S(1)}, u32[]{:S(2)}, u32[]{:S(2)}) %collective-permute-start.51) | collective-permute-done | bytes 1048608 | tf_op jit(solution)/shard_map/ppermute | solution.py:369
  685.8 34.4 %outproj.3.refs_9_ = bf16[4,1024,2048]{2,1,0:T(8,128)(2,1)} custom-call(bf16[1024,512]{1,0:T(8,128)(2,1)} %get-tuple-element.184.refs_0_, bf16[1024,512]{1,0:T(8,128)(2,1)} %collective-permute-done.43.refs_1_, bf16[1024,512]{1,0:T(8,128)(2,1)} %collective-permute-done.44.refs_2_, bf16[1024,512]{1,0:T(8,128)(2,1)} %collective-permute-done.45.refs_3_, ...), custom_call_target="tpu_custom_call" | custom-call | flops 25769803776 | bytes 62914560 | tf_op jit(solution)/shard_map/outproj/pallas_call | solution.py:336
  (194 shorter events, 132.8 us)
Async XLA Ops:
  7.3 85.5 %collective-permute-start.2 = (bf16[512,2048]{1,0:T(8,128)(2,1)}, bf16[512,2048]{1,0:T(8,128)(2,1)}, u32[]{:S(2)}, u32[]{:S(2)}) collective-permute-start(bf16[512,2048]{1,0:T(8,128)(2,1)} %get-tuple-element.103.h1_ref), channel_id=1, source_target_pairs={{0,2},{1,3},{2,0},{3,1},{4,6},{5,7},{6,4},{7,5}} | collective-permute-start | bytes 6291464 | tf_op jit(solution)/shard_map/ppermute | solution.py:369
  48.8 52.5 %collective-permute-start.1 = (bf16[512,2048]{1,0:T(8,128)(2,1)}, bf16[512,2048]{1,0:T(8,128)(2,1)}, u32[]{:S(2)}, u32[]{:S(2)}) collective-permute-start(bf16[512,2048]{1,0:T(8,128)(2,1)} %get-tuple-element.95.h0_ref), channel_id=1, source_target_pairs={{0,2},{1,3},{2,0},{3,1},{4,6},{5,7},{6,4},{7,5}} | collective-permute-start | bytes 6291464 | tf_op jit(solution)/shard_map/ppermute | solution.py:369
  107.8 49.0 %collective-permute-start = (bf16[512,2048]{1,0:T(8,128)(2,1)}, bf16[512,2048]{1,0:T(8,128)(2,1)}, u32[]{:S(2)}, u32[]{:S(2)}) collective-permute-start(bf16[512,2048]{1,0:T(8,128)(2,1)} %get-tuple-element.97.h0_ref), channel_id=1, source_target_pairs={{0,2},{1,3},{2,0},{3,1},{4,6},{5,7},{6,4},{7,5}} | collective-permute-start | bytes 6291464 | tf_op jit(solution)/shard_map/ppermute | solution.py:369
  156.8 70.6 %collective-permute-start.16 = (bf16[512,2048]{1,0:T(8,128)(2,1)}, bf16[512,2048]{1,0:T(8,128)(2,1)}, u32[]{:S(2)}, u32[]{:S(2)}) collective-permute-start(bf16[512,2048]{1,0:T(8,128)(2,1)} %collective-permute-done.h0_ref), channel_id=1, source_target_pairs={{0,1},{1,0},{2,3},{3,2},{4,5},{5,4},{6,7},{7,6}} | collective-permute-start | bytes 6291464 | tf_op jit(solution)/shard_map/ppermute | solution.py:369
  157.3 69.3 %collective-permute-start.11 = (bf16[512,2048]{1,0:T(8,128)(2,1)S(1)}, bf16[512,2048]{1,0:T(8,128)(2,1)}, u32[]{:S(2)}, u32[]{:S(2)}) collective-permute-start(bf16[512,2048]{1,0:T(8,128)(2,1)S(1)} %copy-done.22), channel_id=1, source_target_pairs={{0,2},{1,3},{2,0},{3,1},{4,6},{5,7},{6,4},{7,5}} | collective-permute-start | bytes 6291464 | tf_op jit(solution)/shard_map/ppermute | solution.py:369
  226.6 49.0 %collective-permute-start.19 = (bf16[512,2048]{1,0:T(8,128)(2,1)}, bf16[512,2048]{1,0:T(8,128)(2,1)}, u32[]{:S(2)}, u32[]{:S(2)}) collective-permute-start(bf16[512,2048]{1,0:T(8,128)(2,1)} %get-tuple-element.138.h0_ref), channel_id=1, source_target_pairs={{0,2},{1,3},{2,0},{3,1},{4,6},{5,7},{6,4},{7,5}} | collective-permute-start | bytes 6291464 | tf_op jit(solution)/shard_map/ppermute | solution.py:369
  275.6 70.0 %collective-permute-start.23 = (bf16[512,2048]{1,0:T(8,128)(2,1)}, bf16[512,2048]{1,0:T(8,128)(2,1)}, u32[]{:S(2)}, u32[]{:S(2)}) collective-permute-start(bf16[512,2048]{1,0:T(8,128)(2,1)} %collective-permute-done.19.h0_ref), channel_id=1, source_target_pairs={{0,1},{1,0},{2,3},{3,2},{4,5},{5,4},{6,7},{7,6}} | collective-permute-start | bytes 6291464 | tf_op jit(solution)/shard_map/ppermute | solution.py:369
  276.1 68.1 %collective-permute-start.20 = (bf16[512,2048]{1,0:T(8,128)(2,1)S(1)}, bf16[512,2048]{1,0:T(8,128)(2,1)}, u32[]{:S(2)}, u32[]{:S(2)}) collective-permute-start(bf16[512,2048]{1,0:T(8,128)(2,1)S(1)} %copy-done.20), channel_id=1, source_target_pairs={{0,2},{1,3},{2,0},{3,1},{4,6},{5,7},{6,4},{7,5}} | collective-permute-start | bytes 6291464 | tf_op jit(solution)/shard_map/ppermute | solution.py:369
  344.4 48.8 %collective-permute-start.18 = (bf16[512,2048]{1,0:T(8,128)(2,1)}, bf16[512,2048]{1,0:T(8,128)(2,1)}, u32[]{:S(2)}, u32[]{:S(2)}) collective-permute-start(bf16[512,2048]{1,0:T(8,128)(2,1)} %get-tuple-element.137.h0_ref), channel_id=1, source_target_pairs={{0,2},{1,3},{2,0},{3,1},{4,6},{5,7},{6,4},{7,5}} | collective-permute-start | bytes 6291464 | tf_op jit(solution)/shard_map/ppermute | solution.py:369
  393.2 69.4 %collective-permute-start.28 = (bf16[512,2048]{1,0:T(8,128)(2,1)}, bf16[512,2048]{1,0:T(8,128)(2,1)}, u32[]{:S(2)}, u32[]{:S(2)}) collective-permute-start(bf16[512,2048]{1,0:T(8,128)(2,1)} %collective-permute-done.18.h0_ref), channel_id=1, source_target_pairs={{0,1},{1,0},{2,3},{3,2},{4,5},{5,4},{6,7},{7,6}} | collective-permute-start | bytes 6291464 | tf_op jit(solution)/shard_map/ppermute | solution.py:369
  393.7 68.9 %collective-permute-start.25 = (bf16[512,2048]{1,0:T(8,128)(2,1)S(1)}, bf16[512,2048]{1,0:T(8,128)(2,1)}, u32[]{:S(2)}, u32[]{:S(2)}) collective-permute-start(bf16[512,2048]{1,0:T(8,128)(2,1)S(1)} %copy-done.21), channel_id=1, source_target_pairs={{0,2},{1,3},{2,0},{3,1},{4,6},{5,7},{6,4},{7,5}} | collective-permute-start | bytes 6291464 | tf_op jit(solution)/shard_map/ppermute | solution.py:369
  496.2 72.5 %collective-permute-start.36 = (bf16[256,2048]{1,0:T(8,128)(2,1)}, bf16[256,2048]{1,0:T(8,128)(2,1)}, u32[]{:S(2)}, u32[]{:S(2)}) collective-permute-start(bf16[256,2048]{1,0:T(8,128)(2,1)} %slice.9), channel_id=1, source_target_pairs={{0,2},{1,3},{2,0},{3,1},{4,6},{5,7},{6,4},{7,5}} | collective-permute-start | bytes 3145736 | tf_op jit(solution)/shard_map/ppermute | solution.py:369
  498.4 75.8 %collective-permute-start.37 = (bf16[128,2048]{1,0:T(8,128)(2,1)}, bf16[128,2048]{1,0:T(8,128)(2,1)}, u32[]{:S(2)}, u32[]{:S(2)}) collective-permute-start(bf16[128,2048]{1,0:T(8,128)(2,1)} %slice.10), channel_id=1, source_target_pairs={{0,2},{1,3},{2,0},{3,1},{4,6},{5,7},{6,4},{7,5}} | collective-permute-start | bytes 1572872 | tf_op jit(solution)/shard_map/ppermute | solution.py:369
  499.1 77.7 %collective-permute-start.43 = (bf16[1024,512]{1,0:T(8,128)(2,1)}, bf16[1024,512]{1,0:T(8,128)(2,1)}, u32[]{:S(2)}, u32[]{:S(2)}) collective-permute-start(bf16[1024,512]{1,0:T(8,128)(2,1)} %get-tuple-element.197), channel_id=1, source_target_pairs={{0,1},{1,0},{2,3},{3,2},{4,5},{5,4},{6,7},{7,6}} | collective-permute-start | bytes 3145736 | tf_op jit(solution)/shard_map/ppermute | solution.py:369
  499.1 78.5 %collective-permute-start.44 = (bf16[1024,512]{1,0:T(8,128)(2,1)}, bf16[1024,512]{1,0:T(8,128)(2,1)}, u32[]{:S(2)}, u32[]{:S(2)}) collective-permute-start(bf16[1024,512]{1,0:T(8,128)(2,1)} %get-tuple-element.196), channel_id=1, source_target_pairs={{0,2},{1,3},{2,0},{3,1},{4,6},{5,7},{6,4},{7,5}} | collective-permute-start | bytes 3145736 | tf_op jit(solution)/shard_map/ppermute | solution.py:369
  500.5 89.5 %collective-permute-start.45 = (bf16[1024,512]{1,0:T(8,128)(2,1)S(1)}, bf16[1024,512]{1,0:T(8,128)(2,1)}, u32[]{:S(2)}, u32[]{:S(2)}) collective-permute-start(bf16[1024,512]{1,0:T(8,128)(2,1)S(1)} %get-tuple-element.195), channel_id=1, source_target_pairs={{0,3},{1,2},{2,1},{3,0},{4,7},{5,6},{6,5},{7,4}} | collective-permute-start | bytes 3145736 | tf_op jit(solution)/shard_map/ppermute | solution.py:369
  577.6 56.1 %collective-permute-start.48 = (bf16[1024,512]{1,0:T(8,128)(2,1)S(1)}, bf16[1024,512]{1,0:T(8,128)(2,1)S(1)}, u32[]{:S(2)}, u32[]{:S(2)}) collective-permute-start(bf16[1024,512]{1,0:T(8,128)(2,1)S(1)} %copy-done.4), channel_id=1, source_target_pairs={{0,3},{1,2},{2,1},{3,0},{4,7},{5,6},{6,5},{7,4}} | collective-permute-start | bytes 3145736 | tf_op jit(solution)/shard_map/ppermute | solution.py:369
  589.9 92.2 %collective-permute-start.35 = (bf16[512,2048]{1,0:T(8,128)(2,1)S(1)}, bf16[512,2048]{1,0:T(8,128)(2,1)S(1)}, u32[]{:S(2)}, u32[]{:S(2)}) collective-permute-start(bf16[512,2048]{1,0:T(8,128)(2,1)S(1)} %copy-done), channel_id=1, source_target_pairs={{0,1},{1,0},{2,3},{3,2},{4,5},{5,4},{6,7},{7,6}} | collective-permute-start | bytes 6291464 | tf_op jit(solution)/shard_map/ppermute | solution.py:369
  589.9 93.6 %collective-permute-start.39 = (bf16[512,2048]{1,0:T(8,128)(2,1)S(1)}, bf16[512,2048]{1,0:T(8,128)(2,1)S(1)}, u32[]{:S(2)}, u32[]{:S(2)}) collective-permute-start(bf16[512,2048]{1,0:T(8,128)(2,1)S(1)} %constant_dynamic-update-slice_fusion.refs_14_.refs_6_), channel_id=1, source_target_pairs={{0,1},{1,0},{2,3},{3,2},{4,5},{5,4},{6,7},{7,6}} | collective-permute-start | bytes 6291464 | tf_op jit(solution)/shard_map/ppermute | solution.py:369
  635.5 84.7 %collective-permute-start.41 = (bf16[512,512]{1,0:T(8,128)(2,1)}, bf16[512,512]{1,0:T(8,128)(2,1)S(1)}, u32[]{:S(2)}, u32[]{:S(2)}) collective-permute-start(bf16[512,512]{1,0:T(8,128)(2,1)} %get-tuple-element.200), channel_id=1, source_target_pairs={{0,2},{1,3},{2,0},{3,1},{4,6},{5,7},{6,4},{7,5}} | collective-permute-start | bytes 1572872 | tf_op jit(solution)/shard_map/ppermute | solution.py:369
  659.7 60.5 %collective-permute-start.42 = (bf16[512,512]{1,0:T(8,128)(2,1)}, bf16[512,512]{1,0:T(8,128)(2,1)}, u32[]{:S(2)}, u32[]{:S(2)}) collective-permute-start(bf16[512,512]{1,0:T(8,128)(2,1)} %get-tuple-element.199), channel_id=1, source_target_pairs={{0,3},{1,2},{2,1},{3,0},{4,7},{5,6},{6,5},{7,4}} | collective-permute-start | bytes 1572872 | tf_op jit(solution)/shard_map/ppermute | solution.py:369
  681.2 50.0 %collective-permute-start.32 = (bf16[512,512]{1,0:T(8,128)(2,1)}, bf16[512,512]{1,0:T(8,128)(2,1)S(1)}, u32[]{:S(2)}, u32[]{:S(2)}) collective-permute-start(bf16[512,512]{1,0:T(8,128)(2,1)} %get-tuple-element.205), channel_id=1, source_target_pairs={{0,1},{1,0},{2,3},{3,2},{4,5},{5,4},{6,7},{7,6}} | collective-permute-start | bytes 1572872 | tf_op jit(solution)/shard_map/ppermute | solution.py:369
  682.0 49.2 %collective-permute-start.33 = (bf16[512,512]{1,0:T(8,128)(2,1)}, bf16[512,512]{1,0:T(8,128)(2,1)S(1)}, u32[]{:S(2)}, u32[]{:S(2)}) collective-permute-start(bf16[512,512]{1,0:T(8,128)(2,1)} %get-tuple-element.204), channel_id=1, source_target_pairs={{0,2},{1,3},{2,0},{3,1},{4,6},{5,7},{6,4},{7,5}} | collective-permute-start | bytes 1572872 | tf_op jit(solution)/shard_map/ppermute | solution.py:369
  684.8 46.4 %collective-permute-start.34 = (bf16[512,512]{1,0:T(8,128)(2,1)}, bf16[512,512]{1,0:T(8,128)(2,1)S(1)}, u32[]{:S(2)}, u32[]{:S(2)}) collective-permute-start(bf16[512,512]{1,0:T(8,128)(2,1)} %get-tuple-element.203), channel_id=1, source_target_pairs={{0,3},{1,2},{2,1},{3,0},{4,7},{5,6},{6,5},{7,4}} | collective-permute-start | bytes 1572872 | tf_op jit(solution)/shard_map/ppermute | solution.py:369
  (61 other events, 1372.6 us)

commit v5 on v4

--- a/solution.py
+++ b/solution.py
@@ -54,18 +54,17 @@
 
 
 def norm_kernel(x_ref, g_ref, a_ref, b_ref):
-    x = x_ref[0].astype(F32)
-    mean = jnp.sum(x * x, axis=1, keepdims=True) * (1.0 / x.shape[1])
-    h = (x * lax.rsqrt(mean + 1e-5) * g_ref[...]).astype(BF16)
+    rows, width = a_ref.shape
     lower = pl.program_id(0) < pl.num_programs(0) // 2
-
-    @pl.when(lower)
-    def _():
-        a_ref[...] = h
-
-    @pl.when(jnp.logical_not(lower))
-    def _():
-        b_ref[...] = h
+    for first, dst in ((True, a_ref), (False, b_ref)):
+        @pl.when(lower == first)
+        def _(dst=dst):
+            @pl.loop(0, rows // 64)
+            def _(t):
+                part = pl.ds(pl.multiple_of(t * 64, 64), 64)
+                x = x_ref[0, part, :].astype(F32)
+                mean = jnp.sum(x * x, axis=1, keepdims=True) * (1.0 / width)
+                dst[part, :] = (x * lax.rsqrt(mean + 1e-5) * g_ref[...]).astype(BF16)
 
 
 def norm_call(x, gain, b):
@@ -91,7 +90,10 @@
     for n, src in enumerate((h0_ref, h1_ref, h2_ref, h3_ref)):
         @pl.when(step // n_sub == n)
         def _(src=src):
-            h_ref[...] = src[...]
+            @pl.loop(0, src.shape[0] // 64)
+            def _(t):
+                part = pl.ds(pl.multiple_of(t * 64, 64), 64)
+                h_ref[part, :] = src[part, :]
     h = h_ref[...]
     cols = wq_ref.shape[1]
     q = jnp.dot(h, wq_ref[...], preferred_element_type=F32).astype(BF16)
@@ -209,9 +211,14 @@
     )(*args)
 
 
-def attn_kernel(n_h, bq, ch, q_ref, k_ref, vt_ref, o_ref, l_s, acc_s, m_s, *stage_refs):
+def attn_kernel(n_tp, n_parts, n_h, bq, ch, q_ref, k_ref, vt_ref, *refs):
+    outs = refs[:n_tp * n_parts]
+    l_s, acc_s, m_s, o_s, sem, *stage_refs = refs[n_tp * n_parts:]
+    me = lax.axis_index('tp')
+    n_q = pl.num_programs(0)
+    per = n_q // n_tp
     s_s, mx_s = stage_refs[:n_h], stage_refs[n_h:]
-    i = pl.program_id(1)
+    i = pl.program_id(0)
     c = HD ** -0.5 * LOG2E
     n_c = bq // ch
 
@@ -268,24 +275,48 @@
         return carry
 
     lax.fori_loop(0, i, body, 0)
+
+    def moves(t, act):
+        for n, out in enumerate(outs):
+            r, p = n % n_tp, n // n_tp
+            hit = ((t // per) ^ me) == r
+            if n_parts == 1:
+                dst = out.at[pl.ds(pl.multiple_of((t % per) * bq, bq), bq), :]
+            else:
+                dst = out
+                hit = hit & (t % per == p)
+
+            @pl.when(hit)
+            def _(dst=dst):
+                act(pltpu.make_async_copy(o_s, dst, sem))
+
+    @pl.when(i > 0)
+    def _():
+        moves(i - 1, lambda copy: copy.wait())
+
     for g in range(n_h):
         l = jnp.sum(l_s[g], axis=0, keepdims=True)
-        o_ref[:, heads(g)] = (acc_s[g] / l).T.astype(BF16)
-
-
-def attn_call(q, k, vt):
+        o_s[:, heads(g)] = (acc_s[g] / l).T.astype(BF16)
+    moves(i, lambda copy: copy.start())
+
+    @pl.when(i == n_q - 1)
+    def _():
+        moves(i, lambda copy: copy.wait())
+
+
+def attn_call(q, k, vt, n_tp, n_parts):
     seq, cols = q.shape
-    bq, ch, n_h = 512, 256, min(4, cols // HD)
-    qspec = pl.BlockSpec((bq, n_h * HD), lambda h, i: (i, h))
+    bq, ch, n_h = 512, 256, cols // HD
+    size = seq // n_tp // n_parts
     return pl.pallas_call(
-        functools.partial(attn_kernel, n_h, bq, ch),
-        grid=(cols // (n_h * HD), seq // bq),
-        in_specs=[qspec, pl.BlockSpec((seq, n_h * HD), lambda h, i: (0, h)), pl.BlockSpec((n_h * HD, seq), lambda h, i: (h, 0))],
-        out_specs=qspec,
-        out_shape=jax.ShapeDtypeStruct((seq, cols), BF16),
-        scratch_shapes=[pltpu.VMEM((n_h, 8, bq), F32), pltpu.VMEM((n_h, HD, bq), F32), pltpu.VMEM((n_h, 1, bq), F32)]
+        functools.partial(attn_kernel, n_tp, n_parts, n_h, bq, ch),
+        grid=(seq // bq,),
+        in_specs=[pl.BlockSpec((bq, cols), lambda i: (i, 0)), pl.BlockSpec((seq, cols), lambda i: (0, 0)), pl.BlockSpec((cols, seq), lambda i: (0, 0))],
+        out_specs=[pl.BlockSpec(memory_space=pl.ANY)] * (n_tp * n_parts),
+        out_shape=[jax.ShapeDtypeStruct((size, cols), BF16)] * (n_tp * n_parts),
+        scratch_shapes=[pltpu.VMEM((n_h, 8, bq), F32), pltpu.VMEM((n_h, HD, bq), F32), pltpu.VMEM((n_h, 1, bq), F32), pltpu.VMEM((bq, cols), BF16), pltpu.SemaphoreType.DMA]
         + [pltpu.VMEM((bq, bq), F32)] * n_h + [pltpu.VMEM((8, bq), F32)] * n_h,
-        compiler_params=params("arbitrary", "arbitrary"),
+        compiler_params=params("arbitrary"),
         cost_estimate=cost(4 * seq * seq * cols, 8 * seq * cols, seq * seq * cols // HD // 2),
         name="attn",
     )(q, k, vt)
@@ -377,6 +408,14 @@
         def push(b, p, *deps):
             far[b][p] = send(after(own[b][p], *deps) if deps else own[b][p], 2)
 
+        w_cut = [n * cols // 8 for n in (0, 4, 6, 8)]
+        w2 = []
+
+        def push_w(n, *deps):
+            piece = (after(wo_rows, *deps) if deps else wo_rows)[w_cut[n]:w_cut[n + 1]]
+            w2.append(send(piece, 2))
+            return piece
+
         push(0, 0)
         push(0, 1)
         push(1, 0)
@@ -399,19 +438,20 @@
             stats.append(send(buf[3], 2))
             return vc
 
-        def attend(b, kc, *deps):
+        def attend(b, kc, dep, n_parts=1):
             q, k, vt, ss = late[b]
-            pair_ss = after(stats[b], *deps) + ss
+            pair_ss = after(stats[b], dep) + ss
             tot = pair_ss + send(pair_ss, 1)
             qr, kr, kc = rope_call(q, k, tot, qg, kg, ct, st, kc, b, n_batch, width)
-            o = attn_call(qr, kr, vt)
-            return o, kc
-
-        def exchange(o, dep, n_parts=1):
-            o = after(o, dep)
-            size = rows // n_parts
-            pieces = [[lax.dynamic_slice_in_dim(o, (me ^ r) * rows + p * size, size, axis=0) for r in range(n_tp)] for p in range(n_parts)]
-            return [[cut[0]] + [send(cut[r], r) for r in range(1, n_tp)] for cut in pieces]
+            o = attn_call(qr, kr, vt, n_tp, n_parts)
+            return [o[p * n_tp:(p + 1) * n_tp] for p in range(n_parts)], kc
+
+        def exchange(parts, dep=None):
+            res = []
+            for piece in parts:
+                moved = [after(t, dep) if dep is not None else t for t in piece[1:]]
+                res.append([piece[0]] + [send(t, r + 1) for r, t in enumerate(moved)])
+            return res
 
         vc = early(0, None)
         vc = early(1, vc, vc, ct, st)
@@ -421,32 +461,27 @@
         push(1, 1, done)
         push(2, 0, done)
         vc = early(3, vc, done)
-        w_cut = [0, cols // 2, 3 * cols // 4, cols]
-
-        def push_w(n, dep):
-            return send(after(wo_rows, dep)[w_cut[n]:w_cut[n + 1]], 2)
-
-        w2 = [push_w(0, done)]
+        push_w(0, done)
         o0, kc = attend(0, kc, vc)
-        vc = project(1, vc, o0)
+        vc = project(1, vc, o0[0][0])
         done = late[1][3]
         push(2, 1, done)
         push(3, 0, done)
-        w2.append(push_w(1, done))
+        mark = push_w(1, done)
         ex.append(exchange(o0, done))
-        o1, kc = attend(1, kc, ex[0][0][0])
-        vc = project(2, vc, o1)
+        o1, kc = attend(1, kc, mark)
+        vc = project(2, vc, o1[0][0])
         done = late[2][3]
         push(3, 1, done)
-        w2.append(push_w(2, done))
+        mark = push_w(2, done)
         ex.append(exchange(o1, done))
-        o2, kc = attend(2, kc, ex[1][0][0])
-        vc = project(3, vc, o2)
+        o2, kc = attend(2, kc, mark)
+        vc = project(3, vc, o2[0][0])
         done = late[3][3]
         ex.append(exchange(o2, done))
-        o3, kc = attend(3, kc, ex[2][0][0])
-        ex.append(exchange(o3, o3, 2))
-        w2 = jnp.concatenate([after(w2[0], ex[3][0][0]), *w2[1:]], axis=0)
+        o3, kc = attend(3, kc, done, 2)
+        ex.append(exchange(o3))
+        w2 = jnp.concatenate([after(w2[0], o3[0][0]), *w2[1:]], axis=0)
         ws = [wo_rows, send(after(wo_rows, done), 1), w2, send(w2, 1)]
         first = [list(parts[0]) for parts in ex[:-1]]
         first[0][0] = after(first[0][0], ex[3][0][0])

time: 752 us -> 728 us (0.968); the launches traced: 743 us -> 726 us
  local copies, waits for them, and re-layouts: 30.1 us -> 11.2 us
    dynamic_slice x4 -> x0, local copies, waits for them, and re-layouts: 16.4 us -> none  [exchange(): lax.dynamic_slice_in_dim(o, (me ^ r) * rows + p * size, size, axis=0)]
  transfers between devices with their start and end apart: 52 -> 52, of which waited for: 12 -> 12; matrix products, arithmetic and copies ran while one was open for 4% -> 2% of each run, Pallas kernels for 65% -> 70%
where the time goes in v5:
time: 728 us; the launch traced here: 726 us
  Pallas kernels  523 us (72%)
  waiting for transfers between devices  150 us (21%)
  starting transfers between devices  31.3 us (4%)
  local copies, waits for them, and re-layouts  11.2 us (2%)
  other arithmetic  8.74 us (1%)
    pallas_call x4, Pallas kernels, attn_call(): pl.pallas_call(functools.partial(attn_kernel, n_tp, n_parts, n_h, bq, ch)...  216 us
    pallas_call x8, Pallas kernels, qkv_call(): pl.pallas_call(functools.partial(qkv_kernel, n_sub), grid_spec=pltpu.Pref...  176 us
    ppermute x52, waiting for transfers between devices, send(): return lax.ppermute(val, 'tp', pairs[hop])  150 us
    pallas_call x3, Pallas kernels, out_call(): pl.pallas_call(functools.partial(out_kernel, n_items), grid=(n_items, wid...  54.6 us
    pallas_call x4, Pallas kernels, rope_call(): pl.pallas_call(functools.partial(rope_kernel, width), grid=(nq,), in_spec...  53 us
    ppermute x52, starting transfers between devices, send(): return lax.ppermute(val, 'tp', pairs[hop])  31.3 us
    pallas_call x4, Pallas kernels, norm_call(): pl.pallas_call(norm_kernel, grid=(n,), in_specs=[pl.BlockSpec((1, br, wid...  24.7 us
  transfers between devices with their start and end apart: 52, of which 12 were waited for; matrix products, arithmetic and copies ran while one was open for 2% of the time, Pallas kernels for 70%

profile of v5, /device:TPU:0, one launch (start us, length us, event | category | flops | bytes accessed | tf_op | source)
XLA Modules:
  0.0 726.4 jit_solution(17557427739062513724)
XLA Ops:
  28.2 21.9 %qkv.8 = (bf16[4096,512]{1,0:T(8,128)(2,1)}, bf16[4096,512]{1,0:T(8,128)(2,1)}, bf16[512,4096]{1,0:T(8,128)(2,1)}, bf16[65536,128]{1,0:T(8,128)(2,1)}, f32[2,4096]{1,0:T(2,128)}) custom-call(s32[1]{0:T(128)} %bitcast.me_ref, bf16[512,2048]{1,0:T(8,128)(2,1)} %get-tuple-element.121.h0_ref, bf16[512,2048]{1,0:T(8,128)(2,1)} %get-tuple-element.129.h1_ref, ...), custom_call_target="tpu_custom_call" | custom-call | flops 12884901888 | bytes 23068672 | tf_op jit(solution)/shard_map/qkv/pallas_call | solution.py:134
  50.2 22.0 %qkv.9 = (bf16[4096,512]{1,0:T(8,128)(2,1)}, bf16[4096,512]{1,0:T(8,128)(2,1)}, bf16[512,4096]{1,0:T(8,128)(2,1)}, bf16[65536,128]{1,0:T(8,128)(2,1)}, f32[2,4096]{1,0:T(2,128)}) custom-call(s32[1]{0:T(128)} %bitcast.me_ref, bf16[512,2048]{1,0:T(8,128)(2,1)} %get-tuple-element.123.h0_ref, ...), custom_call_target="tpu_custom_call", output_to_operand_aliasing={{3}: (8, {})} | custom-call | flops 12884901888 | bytes 23068672 | tf_op jit(solution)/shard_map/qkv/pallas_call | solution.py:134
  72.2 22.0 %qkv.10 = (bf16[4096,512]{1,0:T(8,128)(2,1)}, bf16[4096,512]{1,0:T(8,128)(2,1)}, bf16[512,4096]{1,0:T(8,128)(2,1)}, bf16[65536,128]{1,0:T(8,128)(2,1)}, f32[2,4096]{1,0:T(2,128)}) custom-call(s32[1]{0:T(128)} %bitcast.me_ref, bf16[512,2048]{1,0:T(8,128)(2,1)} %get-tuple-element.165.h0_ref, ...), custom_call_target="tpu_custom_call", output_to_operand_aliasing={{3}: (8, {})} | custom-call | flops 12884901888 | bytes 23068672 | tf_op jit(solution)/shard_map/qkv/pallas_call | solution.py:134
  110.1 21.9 %qkv.11 = (bf16[4096,512]{1,0:T(8,128)(2,1)}, bf16[4096,512]{1,0:T(8,128)(2,1)}, bf16[512,4096]{1,0:T(8,128)(2,1)}, bf16[65536,128]{1,0:T(8,128)(2,1)}, f32[2,4096]{1,0:T(2,128)}) custom-call(s32[1]{0:T(128)} %bitcast.me_ref, ...), custom_call_target="tpu_custom_call", output_to_operand_aliasing={{0}: (8, {}), {1}: (9, {}), {2}: (10, {}), {3}: (11, {}), {... | custom-call | flops 12884901888 | bytes 23068672 | tf_op jit(solution)/shard_map/qkv/pallas_call | solution.py:134
  133.6 22.1 %qkv.12 = (bf16[4096,512]{1,0:T(8,128)(2,1)}, bf16[4096,512]{1,0:T(8,128)(2,1)}, bf16[512,4096]{1,0:T(8,128)(2,1)}, bf16[65536,128]{1,0:T(8,128)(2,1)}, f32[2,4096]{1,0:T(2,128)}) custom-call(s32[1]{0:T(128)} %bitcast.me_ref, bf16[512,2048]{1,0:T(8,128)(2,1)} %get-tuple-element.164.h0_ref, ...), custom_call_target="tpu_custom_call", output_to_operand_aliasing={{3}: (8, {})} | custom-call | flops 12884901888 | bytes 23068672 | tf_op jit(solution)/shard_map/qkv/pallas_call | solution.py:134
  160.2 13.3 %rope.4 = (bf16[4096,512]{1,0:T(8,128)(2,1)}, bf16[4096,512]{1,0:T(8,128)(2,1)}, bf16[65536,128]{1,0:T(8,128)(2,1)}) custom-call(bf16[4096,512]{1,0:T(8,128)(2,1)} %get-tuple-element.147.q_ref, bf16[4096,512]{1,0:T(8,128)(2,1)} %get-tuple-element.148.k_ref, f32[2,4096]{1,0:T(2,128)} %add.51.ss_ref, f32[1,512]{1,0:T(1,128)} %bitcast.26, f32[1,512]{1,0:T(1,128)} %bitcast.30, ...), custom_call_target="tpu_custom_call" | custom-call | flops 7000000000 | bytes 20971520 | tf_op jit(solution)/shard_map/rope/pallas_call | solution.py:200
  173.5 53.9 %attn.4 = (bf16[1024,512]{1,0:T(8,128)(2,1)}, bf16[1024,512]{1,0:T(8,128)(2,1)}, bf16[1024,512]{1,0:T(8,128)(2,1)}, bf16[1024,512]{1,0:T(8,128)(2,1)}) custom-call(bf16[4096,512]{1,0:T(8,128)(2,1)} %get-tuple-element.154.q_ref, bf16[4096,512]{1,0:T(8,128)(2,1)} %get-tuple-element.155.k_ref, bf16[512,4096]{1,0:T(8,128)(2,1)} %get-tuple-element.156.vt_ref), custom_call_target="tpu_custom_call" | custom-call | flops 34359738368 | bytes 16777216 | tf_op jit(solution)/shard_map/attn/pallas_call | solution.py:311
  233.2 22.0 %qkv.13 = (bf16[4096,512]{1,0:T(8,128)(2,1)}, bf16[4096,512]{1,0:T(8,128)(2,1)}, bf16[512,4096]{1,0:T(8,128)(2,1)}, bf16[65536,128]{1,0:T(8,128)(2,1)}, f32[2,4096]{1,0:T(2,128)}) custom-call(s32[1]{0:T(128)} %bitcast.me_ref, ...), custom_call_target="tpu_custom_call", output_to_operand_aliasing={{0}: (8, {}), {1}: (9, {}), {2}: (10, {}), {3}: (11, {}), {... | custom-call | flops 12884901888 | bytes 23068672 | tf_op jit(solution)/shard_map/qkv/pallas_call | solution.py:134
  255.9 20.5 %collective-permute-done.21 = f32[2,4096]{1,0:T(2,128)S(1)} collective-permute-done((f32[2,4096]{1,0:T(2,128)}, f32[2,4096]{1,0:T(2,128)S(1)}, u32[]{:S(2)}, u32[]{:S(2)}) %collective-permute-start.21) | collective-permute-done | bytes 32800 | tf_op jit(solution)/shard_map/ppermute | solution.py:400
  279.1 13.2 %rope.5 = (bf16[4096,512]{1,0:T(8,128)(2,1)}, bf16[4096,512]{1,0:T(8,128)(2,1)}, bf16[65536,128]{1,0:T(8,128)(2,1)}) custom-call(bf16[4096,512]{1,0:T(8,128)(2,1)} %get-tuple-element.167.q_ref, bf16[4096,512]{1,0:T(8,128)(2,1)} %get-tuple-element.168.k_ref, f32[2,4096]{1,0:T(2,128)} %add.53.ss_ref, ...), custom_call_target="tpu_custom_call", output_to_operand_aliasing={{2}: (7, {})} | custom-call | flops 7000000000 | bytes 20971520 | tf_op jit(solution)/shard_map/rope/pallas_call | solution.py:200
  292.3 53.7 %attn.5 = (bf16[1024,512]{1,0:T(8,128)(2,1)}, bf16[1024,512]{1,0:T(8,128)(2,1)}, bf16[1024,512]{1,0:T(8,128)(2,1)}, bf16[1024,512]{1,0:T(8,128)(2,1)}) custom-call(bf16[4096,512]{1,0:T(8,128)(2,1)} %get-tuple-element.172.q_ref, bf16[4096,512]{1,0:T(8,128)(2,1)} %get-tuple-element.173.k_ref, bf16[512,4096]{1,0:T(8,128)(2,1)} %get-tuple-element.174.vt_ref), custom_call_target="tpu_custom_call" | custom-call | flops 34359738368 | bytes 16777216 | tf_op jit(solution)/shard_map/attn/pallas_call | solution.py:311
  350.6 21.9 %qkv.14 = (bf16[4096,512]{1,0:T(8,128)(2,1)}, bf16[4096,512]{1,0:T(8,128)(2,1)}, bf16[512,4096]{1,0:T(8,128)(2,1)}, bf16[65536,128]{1,0:T(8,128)(2,1)}, f32[2,4096]{1,0:T(2,128)}) custom-call(s32[1]{0:T(128)} %bitcast.me_ref, ...), custom_call_target="tpu_custom_call", output_to_operand_aliasing={{0}: (8, {}), {1}: (9, {}), {2}: (10, {}), {3}: (11, {}), {... | custom-call | flops 12884901888 | bytes 23068672 | tf_op jit(solution)/shard_map/qkv/pallas_call | solution.py:134
  374.7 20.3 %collective-permute-done.26 = f32[2,4096]{1,0:T(2,128)S(1)} collective-permute-done((f32[2,4096]{1,0:T(2,128)}, f32[2,4096]{1,0:T(2,128)S(1)}, u32[]{:S(2)}, u32[]{:S(2)}) %collective-permute-start.26) | collective-permute-done | bytes 32800 | tf_op jit(solution)/shard_map/ppermute | solution.py:400
  398.3 13.2 %rope.6 = (bf16[4096,512]{1,0:T(8,128)(2,1)}, bf16[4096,512]{1,0:T(8,128)(2,1)}, bf16[65536,128]{1,0:T(8,128)(2,1)}) custom-call(bf16[4096,512]{1,0:T(8,128)(2,1)} %get-tuple-element.184.q_ref, bf16[4096,512]{1,0:T(8,128)(2,1)} %get-tuple-element.185.k_ref, f32[2,4096]{1,0:T(2,128)} %add.55.ss_ref, ...), custom_call_target="tpu_custom_call", output_to_operand_aliasing={{2}: (7, {})} | custom-call | flops 7000000000 | bytes 20971520 | tf_op jit(solution)/shard_map/rope/pallas_call | solution.py:200
  411.5 53.9 %attn.6 = (bf16[1024,512]{1,0:T(8,128)(2,1)}, bf16[1024,512]{1,0:T(8,128)(2,1)}, bf16[1024,512]{1,0:T(8,128)(2,1)}, bf16[1024,512]{1,0:T(8,128)(2,1)}) custom-call(bf16[4096,512]{1,0:T(8,128)(2,1)} %get-tuple-element.189.q_ref, bf16[4096,512]{1,0:T(8,128)(2,1)} %get-tuple-element.190.k_ref, bf16[512,4096]{1,0:T(8,128)(2,1)} %get-tuple-element.191.vt_ref), custom_call_target="tpu_custom_call" | custom-call | flops 34359738368 | bytes 16777216 | tf_op jit(solution)/shard_map/attn/pallas_call | solution.py:311
  470.0 21.9 %qkv.15 = (bf16[4096,512]{1,0:T(8,128)(2,1)}, bf16[4096,512]{1,0:T(8,128)(2,1)}, bf16[512,4096]{1,0:T(8,128)(2,1)}, bf16[65536,128]{1,0:T(8,128)(2,1)}, f32[2,4096]{1,0:T(2,128)}) custom-call(s32[1]{0:T(128)} %bitcast.me_ref, ...), custom_call_target="tpu_custom_call", output_to_operand_aliasing={{0}: (8, {}), {1}: (9, {}), {2}: (10, {}), {3}: (11, {}), {... | custom-call | flops 12884901888 | bytes 23068672 | tf_op jit(solution)/shard_map/qkv/pallas_call | solution.py:134
  500.1 13.2 %rope.7 = (bf16[4096,512]{1,0:T(8,128)(2,1)}, bf16[4096,512]{1,0:T(8,128)(2,1)}, bf16[65536,128]{1,0:T(8,128)(2,1)}) custom-call(bf16[4096,512]{1,0:T(8,128)(2,1)} %get-tuple-element.199.q_ref, bf16[4096,512]{1,0:T(8,128)(2,1)} %get-tuple-element.200.k_ref, f32[2,4096]{1,0:T(2,128)} %add.57.ss_ref, ...), custom_call_target="tpu_custom_call", output_to_operand_aliasing={{2}: (7, {})} | custom-call | flops 7000000000 | bytes 20971520 | tf_op jit(solution)/shard_map/rope/pallas_call | solution.py:200
  514.7 54.0 %attn.7 = (bf16[512,512]{1,0:T(8,128)(2,1)}, bf16[512,512]{1,0:T(8,128)(2,1)}, bf16[512,512]{1,0:T(8,128)(2,1)}, bf16[512,512]{1,0:T(8,128)(2,1)}, bf16[512,512]...) custom-call(bf16[4096,512]{1,0:T(8,128)(2,1)} %get-tuple-element.204.q_ref, ...), custom_call_target="tpu_custom_call" | custom-call | flops 34359738368 | bytes 16777216 | tf_op jit(solution)/shard_map/attn/pallas_call | solution.py:311
  573.5 20.5 %collective-permute-done.48.refs_7_ = bf16[1024,512]{1,0:T(8,128)(2,1)S(1)} collective-permute-done((bf16[1024,512]{1,0:T(8,128)(2,1)}, bf16[1024,512]{1,0:T(8,128)(2,1)S(1)}, u32[]{:S(2)}, u32[]{:S(2)}) %collective-permute-start.48) | collective-permute-done | bytes 1048608 | tf_op jit(solution)/shard_map/ppermute | solution.py:400
  594.6 22.2 %collective-permute-done.47.refs_6_ = bf16[1024,512]{1,0:T(8,128)(2,1)S(1)} collective-permute-done((bf16[1024,512]{1,0:T(8,128)(2,1)S(1)}, bf16[1024,512]{1,0:T(8,128)(2,1)S(1)}, u32[]{:S(2)}, u32[]{:S(2)}) %collective-permute-start.47) | collective-permute-done | bytes 1048608 | tf_op jit(solution)/shard_map/ppermute | solution.py:400
  618.8 23.8 %collective-permute-done.51.refs_11_ = bf16[1024,512]{1,0:T(8,128)(2,1)S(1)} collective-permute-done((bf16[1024,512]{1,0:T(8,128)(2,1)}, bf16[1024,512]{1,0:T(8,128)(2,1)S(1)}, u32[]{:S(2)}, u32[]{:S(2)}) %collective-permute-start.51) | collective-permute-done | bytes 1048608 | tf_op jit(solution)/shard_map/ppermute | solution.py:400
  643.3 21.5 %collective-permute-done.50.refs_10_ = bf16[1024,512]{1,0:T(8,128)(2,1)S(1)} collective-permute-done((bf16[1024,512]{1,0:T(8,128)(2,1)S(1)}, bf16[1024,512]{1,0:T(8,128)(2,1)S(1)}, u32[]{:S(2)}, u32[]{:S(2)}) %collective-permute-start.50) | collective-permute-done | bytes 1048608 | tf_op jit(solution)/shard_map/ppermute | solution.py:400
  669.5 34.4 %outproj.3.refs_9_ = bf16[4,1024,2048]{2,1,0:T(8,128)(2,1)} custom-call(bf16[1024,512]{1,0:T(8,128)(2,1)} %get-tuple-element.218.refs_0_, bf16[1024,512]{1,0:T(8,128)(2,1)} %collective-permute-done.43.refs_1_, bf16[1024,512]{1,0:T(8,128)(2,1)} %collective-permute-done.44.refs_2_, bf16[1024,512]{1,0:T(8,128)(2,1)} %collective-permute-done.45.refs_3_, ...), custom_call_target="tpu_custom_call" | custom-call | flops 25769803776 | bytes 62914560 | tf_op jit(solution)/shard_map/outproj/pallas_call | solution.py:367
  704.8 10.1 %outproj.4.refs_9_ = bf16[4,1024,2048]{2,1,0:T(8,128)(2,1)} custom-call(bf16[512,512]{1,0:T(8,128)(2,1)} %get-tuple-element.213.refs_0_, bf16[512,512]{1,0:T(8,128)(2,1)} %copy-done.4, bf16[512,512]{1,0:T(8,128)(2,1)} %copy-done.6, bf16[512,512]{1,0:T(8,128)(2,1)} %collective-permute-done.42.refs_3_, ...), custom_call_target="tpu_custom_call", output_to_operand_aliasing={{}: (9, {})} | custom-call | flops 4294967296 | bytes 14680064 | tf_op jit(solution)/shard_map/outproj/pallas_call | solution.py:367
  (172 shorter events, 107.7 us)
Async XLA Ops:
  7.7 86.5 %collective-permute-start.2 = (bf16[512,2048]{1,0:T(8,128)(2,1)}, bf16[512,2048]{1,0:T(8,128)(2,1)}, u32[]{:S(2)}, u32[]{:S(2)}) collective-permute-start(bf16[512,2048]{1,0:T(8,128)(2,1)} %get-tuple-element.129.h1_ref), channel_id=1, source_target_pairs={{0,2},{1,3},{2,0},{3,1},{4,6},{5,7},{6,4},{7,5}} | collective-permute-start | bytes 6291464 | tf_op jit(solution)/shard_map/ppermute | solution.py:400
  50.1 51.6 %collective-permute-start.1 = (bf16[512,2048]{1,0:T(8,128)(2,1)}, bf16[512,2048]{1,0:T(8,128)(2,1)}, u32[]{:S(2)}, u32[]{:S(2)}) collective-permute-start(bf16[512,2048]{1,0:T(8,128)(2,1)} %get-tuple-element.121.h0_ref), channel_id=1, source_target_pairs={{0,2},{1,3},{2,0},{3,1},{4,6},{5,7},{6,4},{7,5}} | collective-permute-start | bytes 6291464 | tf_op jit(solution)/shard_map/ppermute | solution.py:400
  108.3 49.0 %collective-permute-start = (bf16[512,2048]{1,0:T(8,128)(2,1)}, bf16[512,2048]{1,0:T(8,128)(2,1)}, u32[]{:S(2)}, u32[]{:S(2)}) collective-permute-start(bf16[512,2048]{1,0:T(8,128)(2,1)} %get-tuple-element.123.h0_ref), channel_id=1, source_target_pairs={{0,2},{1,3},{2,0},{3,1},{4,6},{5,7},{6,4},{7,5}} | collective-permute-start | bytes 6291464 | tf_op jit(solution)/shard_map/ppermute | solution.py:400
  157.4 71.0 %collective-permute-start.16 = (bf16[512,2048]{1,0:T(8,128)(2,1)}, bf16[512,2048]{1,0:T(8,128)(2,1)}, u32[]{:S(2)}, u32[]{:S(2)}) collective-permute-start(bf16[512,2048]{1,0:T(8,128)(2,1)} %collective-permute-done.h0_ref), channel_id=1, source_target_pairs={{0,1},{1,0},{2,3},{3,2},{4,5},{5,4},{6,7},{7,6}} | collective-permute-start | bytes 6291464 | tf_op jit(solution)/shard_map/ppermute | solution.py:400
  157.8 69.6 %collective-permute-start.11 = (bf16[512,2048]{1,0:T(8,128)(2,1)S(1)}, bf16[512,2048]{1,0:T(8,128)(2,1)}, u32[]{:S(2)}, u32[]{:S(2)}) collective-permute-start(bf16[512,2048]{1,0:T(8,128)(2,1)S(1)} %copy-done.11), channel_id=1, source_target_pairs={{0,2},{1,3},{2,0},{3,1},{4,6},{5,7},{6,4},{7,5}} | collective-permute-start | bytes 6291464 | tf_op jit(solution)/shard_map/ppermute | solution.py:400
  227.5 49.8 %collective-permute-start.19 = (bf16[512,2048]{1,0:T(8,128)(2,1)}, bf16[512,2048]{1,0:T(8,128)(2,1)}, u32[]{:S(2)}, u32[]{:S(2)}) collective-permute-start(bf16[512,2048]{1,0:T(8,128)(2,1)} %get-tuple-element.165.h0_ref), channel_id=1, source_target_pairs={{0,2},{1,3},{2,0},{3,1},{4,6},{5,7},{6,4},{7,5}} | collective-permute-start | bytes 6291464 | tf_op jit(solution)/shard_map/ppermute | solution.py:400
  277.3 70.2 %collective-permute-start.23 = (bf16[512,2048]{1,0:T(8,128)(2,1)}, bf16[512,2048]{1,0:T(8,128)(2,1)}, u32[]{:S(2)}, u32[]{:S(2)}) collective-permute-start(bf16[512,2048]{1,0:T(8,128)(2,1)} %collective-permute-done.19.h0_ref), channel_id=1, source_target_pairs={{0,1},{1,0},{2,3},{3,2},{4,5},{5,4},{6,7},{7,6}} | collective-permute-start | bytes 6291464 | tf_op jit(solution)/shard_map/ppermute | solution.py:400
  277.7 68.3 %collective-permute-start.20 = (bf16[512,2048]{1,0:T(8,128)(2,1)}, bf16[512,2048]{1,0:T(8,128)(2,1)}, u32[]{:S(2)}, u32[]{:S(2)}) collective-permute-start(bf16[512,2048]{1,0:T(8,128)(2,1)} %get-tuple-element.166.h1_ref), channel_id=1, source_target_pairs={{0,2},{1,3},{2,0},{3,1},{4,6},{5,7},{6,4},{7,5}} | collective-permute-start | bytes 6291464 | tf_op jit(solution)/shard_map/ppermute | solution.py:400
  346.2 49.6 %collective-permute-start.18 = (bf16[512,2048]{1,0:T(8,128)(2,1)}, bf16[512,2048]{1,0:T(8,128)(2,1)}, u32[]{:S(2)}, u32[]{:S(2)}) collective-permute-start(bf16[512,2048]{1,0:T(8,128)(2,1)} %get-tuple-element.164.h0_ref), channel_id=1, source_target_pairs={{0,2},{1,3},{2,0},{3,1},{4,6},{5,7},{6,4},{7,5}} | collective-permute-start | bytes 6291464 | tf_op jit(solution)/shard_map/ppermute | solution.py:400
  395.8 71.6 %collective-permute-start.28 = (bf16[512,2048]{1,0:T(8,128)(2,1)}, bf16[512,2048]{1,0:T(8,128)(2,1)}, u32[]{:S(2)}, u32[]{:S(2)}) collective-permute-start(bf16[512,2048]{1,0:T(8,128)(2,1)} %collective-permute-done.18.h0_ref), channel_id=1, source_target_pairs={{0,1},{1,0},{2,3},{3,2},{4,5},{5,4},{6,7},{7,6}} | collective-permute-start | bytes 6291464 | tf_op jit(solution)/shard_map/ppermute | solution.py:400
  396.3 69.2 %collective-permute-start.25 = (bf16[512,2048]{1,0:T(8,128)(2,1)}, bf16[512,2048]{1,0:T(8,128)(2,1)}, u32[]{:S(2)}, u32[]{:S(2)}) collective-permute-start(bf16[512,2048]{1,0:T(8,128)(2,1)} %get-tuple-element.183.h1_ref), channel_id=1, source_target_pairs={{0,2},{1,3},{2,0},{3,1},{4,6},{5,7},{6,4},{7,5}} | collective-permute-start | bytes 6291464 | tf_op jit(solution)/shard_map/ppermute | solution.py:400
  466.6 46.7 %collective-permute-start.36 = (bf16[256,2048]{1,0:T(8,128)(2,1)}, bf16[256,2048]{1,0:T(8,128)(2,1)S(1)}, u32[]{:S(2)}, u32[]{:S(2)}) collective-permute-start(bf16[256,2048]{1,0:T(8,128)(2,1)} %slice.11), channel_id=1, source_target_pairs={{0,2},{1,3},{2,0},{3,1},{4,6},{5,7},{6,4},{7,5}} | collective-permute-start | bytes 3145736 | tf_op jit(solution)/shard_map/ppermute | solution.py:400
  496.9 71.8 %collective-permute-start.37 = (bf16[128,2048]{1,0:T(8,128)(2,1)S(1)}, bf16[128,2048]{1,0:T(8,128)(2,1)}, u32[]{:S(2)}, u32[]{:S(2)}) collective-permute-start(bf16[128,2048]{1,0:T(8,128)(2,1)S(1)} %slice.9), channel_id=1, source_target_pairs={{0,2},{1,3},{2,0},{3,1},{4,6},{5,7},{6,4},{7,5}} | collective-permute-start | bytes 1572872 | tf_op jit(solution)/shard_map/ppermute | solution.py:400
  497.6 73.0 %collective-permute-start.45 = (bf16[1024,512]{1,0:T(8,128)(2,1)}, bf16[1024,512]{1,0:T(8,128)(2,1)}, u32[]{:S(2)}, u32[]{:S(2)}) collective-permute-start(bf16[1024,512]{1,0:T(8,128)(2,1)} %get-tuple-element.224), channel_id=1, source_target_pairs={{0,3},{1,2},{2,1},{3,0},{4,7},{5,6},{6,5},{7,4}} | collective-permute-start | bytes 3145736 | tf_op jit(solution)/shard_map/ppermute | solution.py:400
  498.7 73.1 %collective-permute-start.44 = (bf16[1024,512]{1,0:T(8,128)(2,1)}, bf16[1024,512]{1,0:T(8,128)(2,1)}, u32[]{:S(2)}, u32[]{:S(2)}) collective-permute-start(bf16[1024,512]{1,0:T(8,128)(2,1)} %get-tuple-element.222), channel_id=1, source_target_pairs={{0,2},{1,3},{2,0},{3,1},{4,6},{5,7},{6,4},{7,5}} | collective-permute-start | bytes 3145736 | tf_op jit(solution)/shard_map/ppermute | solution.py:400
  499.4 74.0 %collective-permute-start.43 = (bf16[1024,512]{1,0:T(8,128)(2,1)}, bf16[1024,512]{1,0:T(8,128)(2,1)}, u32[]{:S(2)}, u32[]{:S(2)}) collective-permute-start(bf16[1024,512]{1,0:T(8,128)(2,1)} %get-tuple-element.220), channel_id=1, source_target_pairs={{0,1},{1,0},{2,3},{3,2},{4,5},{5,4},{6,7},{7,6}} | collective-permute-start | bytes 3145736 | tf_op jit(solution)/shard_map/ppermute | solution.py:400
  513.3 58.5 %collective-permute-start.38 = (bf16[128,2048]{1,0:T(8,128)(2,1)}, bf16[128,2048]{1,0:T(8,128)(2,1)}, u32[]{:S(2)}, u32[]{:S(2)}) collective-permute-start(bf16[128,2048]{1,0:T(8,128)(2,1)} %slice.10), channel_id=1, source_target_pairs={{0,2},{1,3},{2,0},{3,1},{4,6},{5,7},{6,4},{7,5}} | collective-permute-start | bytes 1572872 | tf_op jit(solution)/shard_map/ppermute | solution.py:400
  571.8 94.1 %collective-permute-start.35 = (bf16[512,2048]{1,0:T(8,128)(2,1)S(1)}, bf16[512,2048]{1,0:T(8,128)(2,1)S(1)}, u32[]{:S(2)}, u32[]{:S(2)}) collective-permute-start(bf16[512,2048]{1,0:T(8,128)(2,1)S(1)} %copy-done), channel_id=1, source_target_pairs={{0,1},{1,0},{2,3},{3,2},{4,5},{5,4},{6,7},{7,6}} | collective-permute-start | bytes 6291464 | tf_op jit(solution)/shard_map/ppermute | solution.py:400
  573.4 93.5 %collective-permute-start.39 = (bf16[512,2048]{1,0:T(8,128)(2,1)S(1)}, bf16[512,2048]{1,0:T(8,128)(2,1)S(1)}, u32[]{:S(2)}, u32[]{:S(2)}) collective-permute-start(bf16[512,2048]{1,0:T(8,128)(2,1)S(1)} %constant_dynamic-update-slice_fusion.refs_14_.refs_6_), channel_id=1, source_target_pairs={{0,1},{1,0},{2,3},{3,2},{4,5},{5,4},{6,7},{7,6}} | collective-permute-start | bytes 6291464 | tf_op jit(solution)/shard_map/ppermute | solution.py:400
  617.1 47.7 %collective-permute-start.50 = (bf16[1024,512]{1,0:T(8,128)(2,1)S(1)}, bf16[1024,512]{1,0:T(8,128)(2,1)S(1)}, u32[]{:S(2)}, u32[]{:S(2)}) collective-permute-start(bf16[1024,512]{1,0:T(8,128)(2,1)S(1)} %copy-done.17), channel_id=1, source_target_pairs={{0,2},{1,3},{2,0},{3,1},{4,6},{5,7},{6,4},{7,5}} | collective-permute-start | bytes 3145736 | tf_op jit(solution)/shard_map/ppermute | solution.py:400
  618.2 47.2 %collective-permute-start.49 = (bf16[1024,512]{1,0:T(8,128)(2,1)S(1)}, bf16[1024,512]{1,0:T(8,128)(2,1)S(1)}, u32[]{:S(2)}, u32[]{:S(2)}) collective-permute-start(bf16[1024,512]{1,0:T(8,128)(2,1)S(1)} %copy-done.16), channel_id=1, source_target_pairs={{0,1},{1,0},{2,3},{3,2},{4,5},{5,4},{6,7},{7,6}} | collective-permute-start | bytes 3145736 | tf_op jit(solution)/shard_map/ppermute | solution.py:400
  642.5 61.4 %collective-permute-start.41 = (bf16[512,512]{1,0:T(8,128)(2,1)}, bf16[512,512]{1,0:T(8,128)(2,1)S(1)}, u32[]{:S(2)}, u32[]{:S(2)}) collective-permute-start(bf16[512,512]{1,0:T(8,128)(2,1)} %get-tuple-element.216), channel_id=1, source_target_pairs={{0,2},{1,3},{2,0},{3,1},{4,6},{5,7},{6,4},{7,5}} | collective-permute-start | bytes 1572872 | tf_op jit(solution)/shard_map/ppermute | solution.py:400
  665.5 49.4 %collective-permute-start.32 = (bf16[512,512]{1,0:T(8,128)(2,1)}, bf16[512,512]{1,0:T(8,128)(2,1)S(1)}, u32[]{:S(2)}, u32[]{:S(2)}) collective-permute-start(bf16[512,512]{1,0:T(8,128)(2,1)} %get-tuple-element.208), channel_id=1, source_target_pairs={{0,1},{1,0},{2,3},{3,2},{4,5},{5,4},{6,7},{7,6}} | collective-permute-start | bytes 1572872 | tf_op jit(solution)/shard_map/ppermute | solution.py:400
  665.9 49.0 %collective-permute-start.33 = (bf16[512,512]{1,0:T(8,128)(2,1)}, bf16[512,512]{1,0:T(8,128)(2,1)S(1)}, u32[]{:S(2)}, u32[]{:S(2)}) collective-permute-start(bf16[512,512]{1,0:T(8,128)(2,1)} %get-tuple-element.209), channel_id=1, source_target_pairs={{0,2},{1,3},{2,0},{3,1},{4,6},{5,7},{6,4},{7,5}} | collective-permute-start | bytes 1572872 | tf_op jit(solution)/shard_map/ppermute | solution.py:400
  (52 other events, 1180.1 us)

commit v6 on v5

--- a/solution.py
+++ b/solution.py
@@ -80,6 +80,31 @@
         out_shape=[half, half],
         compiler_params=params("arbitrary"),
         cost_estimate=cost(8 * rows * width, 4 * rows * width),
+        name="norm",
+    )(x, gain)
+
+
+def norm_half_kernel(x_ref, g_ref, h_ref):
+    @pl.loop(0, h_ref.shape[0] // 64)
+    def _(t):
+        part = pl.ds(pl.multiple_of(t * 64, 64), 64)
+        x = x_ref[0, part, :].astype(F32)
+        mean = jnp.sum(x * x, axis=1, keepdims=True) * (1.0 / x.shape[1])
+        h_ref[part, :] = (x * lax.rsqrt(mean + 1e-5) * g_ref[...]).astype(BF16)
+
+
+def norm_half_call(x, gain, b, p):
+    rows, width = x.shape[1:]
+    br = 256
+    n = rows // 2 // br
+    return pl.pallas_call(
+        norm_half_kernel,
+        grid=(n,),
+        in_specs=[pl.BlockSpec((1, br, width), lambda s: (b, p * n + s, 0)), pl.BlockSpec((1, width), lambda s: (0, 0))],
+        out_specs=pl.BlockSpec((br, width), lambda s: (s, 0)),
+        out_shape=jax.ShapeDtypeStruct((rows // 2, width), BF16),
+        compiler_params=params("arbitrary"),
+        cost_estimate=cost(4 * rows * width, 2 * rows * width),
         name="norm",
     )(x, gain)
 
@@ -378,6 +403,46 @@
     )(*args)
 
 
+def near_kernel(o0_ref, o1_ref, w0_ref, w1_ref, acc_ref):
+    acc = jnp.dot(o0_ref[...], w0_ref[...], preferred_element_type=F32)
+    acc_ref[...] = acc + jnp.dot(o1_ref[...], w1_ref[...], preferred_element_type=F32)
+
+
+def final_kernel(o2_ref, o3_ref, w2_ref, w3_ref, acc_ref, x_ref, *refs):
+    acc = acc_ref[...] + jnp.dot(o2_ref[...], w2_ref[...], preferred_element_type=F32)
+    acc += jnp.dot(o3_ref[...], w3_ref[...], preferred_element_type=F32)
+    y = acc.astype(BF16).astype(F32)
+    refs[-1][0] = (x_ref[0].astype(F32) + y).astype(BF16)
+
+
+def half_out_call(pieces, ws, x=None, prev=None, acc=None, b=0, part=0):
+    rows, cols = pieces[0].shape
+    width = ws[0].shape[1]
+    bn = 512
+    ospec = pl.BlockSpec((rows, cols), lambda n: (0, 0))
+    wspec = pl.BlockSpec((cols, bn), lambda n: (0, n))
+    aspec = pl.BlockSpec((rows, bn), lambda n: (0, n))
+    in_specs, args, aliases = [ospec] * 2 + [wspec] * 2, [*pieces, *ws], {}
+    kernel, out_spec, out_shape = near_kernel, aspec, jax.ShapeDtypeStruct((rows, width), F32)
+    if acc is not None:
+        out_spec = pl.BlockSpec((1, rows, bn), lambda n: (b, part, n))
+        in_specs += [aspec, out_spec, pl.BlockSpec(memory_space=pl.ANY)]
+        args += [acc, x, prev]
+        aliases = {6: 0}
+        kernel, out_shape = final_kernel, jax.ShapeDtypeStruct(x.shape, BF16)
+    return pl.pallas_call(
+        kernel,
+        grid=(width // bn,),
+        in_specs=in_specs,
+        out_specs=out_spec,
+        out_shape=out_shape,
+        input_output_aliases=aliases,
+        compiler_params=params("arbitrary"),
+        cost_estimate=cost(4 * rows * cols * width, 4 * cols * width + 8 * rows * width),
+        name="outhalf",
+    )(*args)
+
+
 def solution(mesh):
     n_tp = mesh.shape['tp']
     pairs = {r: [(d, d ^ r) for d in range(n_tp)] for r in range(1, n_tp)}
@@ -400,9 +465,10 @@
             return lax.ppermute(val, 'tp', pairs[hop])
 
         gain = attn_gain.reshape(1, width)
-        own = []
-        for b in range(n_batch):
-            own.append(norm_call(x_local, after(gain, own[-1][0]) if own else gain, b))
+        own = [[norm_half_call(x_local, gain, 0, 0)]]
+        own[0].append(norm_half_call(x_local, after(gain, own[0][0]), 0, 1))
+        for b in range(1, n_batch):
+            own.append(norm_call(x_local, after(gain, own[-1][1]), b))
         far = [[None, None] for _ in own]
 
         def push(b, p, *deps):
@@ -452,6 +518,10 @@
                 moved = [after(t, dep) if dep is not None else t for t in piece[1:]]
                 res.append([piece[0]] + [send(t, r + 1) for r, t in enumerate(moved)])
             return res
+
+        def fill_w(n, buf, *deps):
+            piece = after(w2[n], *deps)
+            return lax.dynamic_update_slice(buf, piece, (w_cut[n], 0))
 
         vc = early(0, None)
         vc = early(1, vc, vc, ct, st)
@@ -470,24 +540,28 @@
         mark = push_w(1, done)
         ex.append(exchange(o0, done))
         o1, kc = attend(1, kc, mark)
+        w_buf = fill_w(0, jnp.zeros((cols, width), BF16), o1[0][0])
         vc = project(2, vc, o1[0][0])
         done = late[2][3]
         push(3, 1, done)
         mark = push_w(2, done)
         ex.append(exchange(o1, done))
         o2, kc = attend(2, kc, mark)
+        w_buf = fill_w(1, after(w_buf, o2[0][0]), o2[0][0])
         vc = project(3, vc, o2[0][0])
         done = late[3][3]
         ex.append(exchange(o2, done))
         o3, kc = attend(3, kc, done, 2)
         ex.append(exchange(o3))
-        w2 = jnp.concatenate([after(w2[0], o3[0][0]), *w2[1:]], axis=0)
+        w2 = fill_w(2, w_buf, o3[0][0])
         ws = [wo_rows, send(after(wo_rows, done), 1), w2, send(w2, 1)]
+        head, tail = ex[3]
+        acc = half_out_call(tail[:2], ws[:2])
         first = [list(parts[0]) for parts in ex[:-1]]
-        first[0][0] = after(first[0][0], ex[3][0][0])
+        first[0][0] = after(first[0][0], acc)
         out = out_call(first, ws, x_local, None, 0, 0)
-        for p, pos in enumerate(ex[-1]):
-            out = out_call([pos], ws, x_local, out, n_batch - 1, p)
+        out = out_call([head], ws, x_local, out, n_batch - 1, 0)
+        out = half_out_call(tail[2:], ws[2:], x_local, out, acc, n_batch - 1, 1)
         shape = (n_batch, seq, cols // HD, HD)
         return (out, kc.reshape(shape), vc.reshape(shape))
 

time: 728 us -> 731 us (level)
    pallas_call x0 -> x4, Pallas kernels: none -> 21.1 us  [the longest x2 14 us: half_out_call(): pl.pallas_call(kernel, grid=(width // bn,), in_specs=in_specs, out_specs=...]
    pallas_call x3 -> x2, Pallas kernels: 54.6 us -> 44.5 us  [out_call(): pl.pallas_call(functools.partial(out_kernel, n_items), grid=(n_items, wid...]
    pallas_call x4 -> x3, Pallas kernels: 24.7 us -> 18.5 us  [norm_call(): pl.pallas_call(norm_kernel, grid=(n,), in_specs=[pl.BlockSpec((1, br, wid...]
  transfers between devices with their start and end apart: 52 -> 52, of which waited for: 12 -> 13; matrix products, arithmetic and copies ran while one was open for 2% -> 2% of each run, Pallas kernels for 70% -> 71%
where the time goes in v6:
time: 731 us; the launch traced here: 730 us
  Pallas kernels  529 us (72%)
  waiting for transfers between devices  148 us (20%)
  starting transfers between devices  32.6 us (4%)
  local copies, waits for them, and re-layouts  11.8 us (2%)
  other arithmetic  7.82 us (1%)
    pallas_call x4, Pallas kernels, attn_call(): pl.pallas_call(functools.partial(attn_kernel, n_tp, n_parts, n_h, bq, ch)...  216 us
    pallas_call x8, Pallas kernels, qkv_call(): pl.pallas_call(functools.partial(qkv_kernel, n_sub), grid_spec=pltpu.Pref...  176 us
    ppermute x52, waiting for transfers between devices, send(): return lax.ppermute(val, 'tp', pairs[hop])  148 us
    pallas_call x4, Pallas kernels, rope_call(): pl.pallas_call(functools.partial(rope_kernel, width), grid=(nq,), in_spec...  53 us
    pallas_call x2, Pallas kernels, out_call(): pl.pallas_call(functools.partial(out_kernel, n_items), grid=(n_items, wid...  44.5 us
    ppermute x52, starting transfers between devices, send(): return lax.ppermute(val, 'tp', pairs[hop])  32.6 us
    pallas_call x3, Pallas kernels, norm_call(): pl.pallas_call(norm_kernel, grid=(n,), in_specs=[pl.BlockSpec((1, br, wid...  18.5 us
  transfers between devices with their start and end apart: 52, of which 13 were waited for; matrix products, arithmetic and copies ran while one was open for 2% of the time, Pallas kernels for 71%

profile of v6, /device:TPU:0, one launch (start us, length us, event | category | flops | bytes accessed | tf_op | source)
XLA Modules:
  0.0 729.6 jit_solution(7212049083802267438)
XLA Ops:
  29.6 22.1 %qkv.8 = (bf16[4096,512]{1,0:T(8,128)(2,1)}, bf16[4096,512]{1,0:T(8,128)(2,1)}, bf16[512,4096]{1,0:T(8,128)(2,1)}, bf16[65536,128]{1,0:T(8,128)(2,1)}, f32[2,4096]{1,0:T(2,128)}) custom-call(s32[1]{0:T(128)} %bitcast.me_ref, bf16[512,2048]{1,0:T(8,128)(2,1)} %norm.5.h0_ref, bf16[512,2048]{1,0:T(8,128)(2,1)} %norm.6.h1_ref, bf16[512,2048]{1,0:T(8,128)(2,1)} %copy-done.12, ...), custom_call_target="tpu_custom_call" | custom-call | flops 12884901888 | bytes 23068672 | tf_op jit(solution)/shard_map/qkv/pallas_call | solution.py:159
  51.7 22.0 %qkv.9 = (bf16[4096,512]{1,0:T(8,128)(2,1)}, bf16[4096,512]{1,0:T(8,128)(2,1)}, bf16[512,4096]{1,0:T(8,128)(2,1)}, bf16[65536,128]{1,0:T(8,128)(2,1)}, f32[2,4096]{1,0:T(2,128)}) custom-call(s32[1]{0:T(128)} %bitcast.me_ref, bf16[512,2048]{1,0:T(8,128)(2,1)} %get-tuple-element.130.h0_ref, ...), custom_call_target="tpu_custom_call", output_to_operand_aliasing={{3}: (8, {})} | custom-call | flops 12884901888 | bytes 23068672 | tf_op jit(solution)/shard_map/qkv/pallas_call | solution.py:159
  73.8 22.0 %qkv.10 = (bf16[4096,512]{1,0:T(8,128)(2,1)}, bf16[4096,512]{1,0:T(8,128)(2,1)}, bf16[512,4096]{1,0:T(8,128)(2,1)}, bf16[65536,128]{1,0:T(8,128)(2,1)}, f32[2,4096]{1,0:T(2,128)}) custom-call(s32[1]{0:T(128)} %bitcast.me_ref, bf16[512,2048]{1,0:T(8,128)(2,1)} %get-tuple-element.166.h0_ref, ...), custom_call_target="tpu_custom_call", output_to_operand_aliasing={{3}: (8, {})} | custom-call | flops 12884901888 | bytes 23068672 | tf_op jit(solution)/shard_map/qkv/pallas_call | solution.py:159
  111.0 21.9 %qkv.11 = (bf16[4096,512]{1,0:T(8,128)(2,1)}, bf16[4096,512]{1,0:T(8,128)(2,1)}, bf16[512,4096]{1,0:T(8,128)(2,1)}, bf16[65536,128]{1,0:T(8,128)(2,1)}, f32[2,4096]{1,0:T(2,128)}) custom-call(s32[1]{0:T(128)} %bitcast.me_ref, ...), custom_call_target="tpu_custom_call", output_to_operand_aliasing={{0}: (8, {}), {1}: (9, {}), {2}: (10, {}), {3}: (11, {}), {... | custom-call | flops 12884901888 | bytes 23068672 | tf_op jit(solution)/shard_map/qkv/pallas_call | solution.py:159
  134.6 22.1 %qkv.12 = (bf16[4096,512]{1,0:T(8,128)(2,1)}, bf16[4096,512]{1,0:T(8,128)(2,1)}, bf16[512,4096]{1,0:T(8,128)(2,1)}, bf16[65536,128]{1,0:T(8,128)(2,1)}, f32[2,4096]{1,0:T(2,128)}) custom-call(s32[1]{0:T(128)} %bitcast.me_ref, bf16[512,2048]{1,0:T(8,128)(2,1)} %get-tuple-element.165.h0_ref, ...), custom_call_target="tpu_custom_call", output_to_operand_aliasing={{3}: (8, {})} | custom-call | flops 12884901888 | bytes 23068672 | tf_op jit(solution)/shard_map/qkv/pallas_call | solution.py:159
  161.2 13.3 %rope.4 = (bf16[4096,512]{1,0:T(8,128)(2,1)}, bf16[4096,512]{1,0:T(8,128)(2,1)}, bf16[65536,128]{1,0:T(8,128)(2,1)}) custom-call(bf16[4096,512]{1,0:T(8,128)(2,1)} %get-tuple-element.148.q_ref, bf16[4096,512]{1,0:T(8,128)(2,1)} %get-tuple-element.149.k_ref, f32[2,4096]{1,0:T(2,128)} %add.53.ss_ref, f32[1,512]{1,0:T(1,128)} %bitcast.27, f32[1,512]{1,0:T(1,128)} %bitcast.31, ...), custom_call_target="tpu_custom_call" | custom-call | flops 7000000000 | bytes 20971520 | tf_op jit(solution)/shard_map/rope/pallas_call | solution.py:225
  174.5 53.9 %attn.4 = (bf16[1024,512]{1,0:T(8,128)(2,1)}, bf16[1024,512]{1,0:T(8,128)(2,1)}, bf16[1024,512]{1,0:T(8,128)(2,1)}, bf16[1024,512]{1,0:T(8,128)(2,1)}) custom-call(bf16[4096,512]{1,0:T(8,128)(2,1)} %get-tuple-element.155.q_ref, bf16[4096,512]{1,0:T(8,128)(2,1)} %get-tuple-element.156.k_ref, bf16[512,4096]{1,0:T(8,128)(2,1)} %get-tuple-element.157.vt_ref), custom_call_target="tpu_custom_call" | custom-call | flops 34359738368 | bytes 16777216 | tf_op jit(solution)/shard_map/attn/pallas_call | solution.py:336
  233.0 21.9 %qkv.13 = (bf16[4096,512]{1,0:T(8,128)(2,1)}, bf16[4096,512]{1,0:T(8,128)(2,1)}, bf16[512,4096]{1,0:T(8,128)(2,1)}, bf16[65536,128]{1,0:T(8,128)(2,1)}, f32[2,4096]{1,0:T(2,128)}) custom-call(s32[1]{0:T(128)} %bitcast.me_ref, ...), custom_call_target="tpu_custom_call", output_to_operand_aliasing={{0}: (8, {}), {1}: (9, {}), {2}: (10, {}), {3}: (11, {}), {... | custom-call | flops 12884901888 | bytes 23068672 | tf_op jit(solution)/shard_map/qkv/pallas_call | solution.py:159
  256.7 20.8 %collective-permute-done.21 = f32[2,4096]{1,0:T(2,128)S(1)} collective-permute-done((f32[2,4096]{1,0:T(2,128)}, f32[2,4096]{1,0:T(2,128)S(1)}, u32[]{:S(2)}, u32[]{:S(2)}) %collective-permute-start.21) | collective-permute-done | bytes 32800 | tf_op jit(solution)/shard_map/ppermute | solution.py:465
  280.1 13.2 %rope.5 = (bf16[4096,512]{1,0:T(8,128)(2,1)}, bf16[4096,512]{1,0:T(8,128)(2,1)}, bf16[65536,128]{1,0:T(8,128)(2,1)}) custom-call(bf16[4096,512]{1,0:T(8,128)(2,1)} %get-tuple-element.168.q_ref, bf16[4096,512]{1,0:T(8,128)(2,1)} %get-tuple-element.169.k_ref, f32[2,4096]{1,0:T(2,128)} %add.55.ss_ref, ...), custom_call_target="tpu_custom_call", output_to_operand_aliasing={{2}: (7, {})} | custom-call | flops 7000000000 | bytes 20971520 | tf_op jit(solution)/shard_map/rope/pallas_call | solution.py:225
  293.3 53.7 %attn.5 = (bf16[1024,512]{1,0:T(8,128)(2,1)}, bf16[1024,512]{1,0:T(8,128)(2,1)}, bf16[1024,512]{1,0:T(8,128)(2,1)}, bf16[1024,512]{1,0:T(8,128)(2,1)}) custom-call(bf16[4096,512]{1,0:T(8,128)(2,1)} %get-tuple-element.173.q_ref, bf16[4096,512]{1,0:T(8,128)(2,1)} %get-tuple-element.174.k_ref, bf16[512,4096]{1,0:T(8,128)(2,1)} %get-tuple-element.175.vt_ref), custom_call_target="tpu_custom_call" | custom-call | flops 34359738368 | bytes 16777216 | tf_op jit(solution)/shard_map/attn/pallas_call | solution.py:336
  352.8 22.0 %qkv.14 = (bf16[4096,512]{1,0:T(8,128)(2,1)}, bf16[4096,512]{1,0:T(8,128)(2,1)}, bf16[512,4096]{1,0:T(8,128)(2,1)}, bf16[65536,128]{1,0:T(8,128)(2,1)}, f32[2,4096]{1,0:T(2,128)}) custom-call(s32[1]{0:T(128)} %bitcast.me_ref, bf16[512,2048]{1,0:T(8,128)(2,1)} %copy-done.11, ...), custom_call_target="tpu_custom_call", output_to_operand_aliasing={{0}: (8, {}), {1}: (9, {}), {2}: (10, {}), {3}: (11, {}), {... | custom-call | flops 12884901888 | bytes 23068672 | tf_op jit(solution)/shard_map/qkv/pallas_call | solution.py:159
  378.1 18.0 %collective-permute-done.26 = f32[2,4096]{1,0:T(2,128)S(1)} collective-permute-done((f32[2,4096]{1,0:T(2,128)}, f32[2,4096]{1,0:T(2,128)S(1)}, u32[]{:S(2)}, u32[]{:S(2)}) %collective-permute-start.26) | collective-permute-done | bytes 32800 | tf_op jit(solution)/shard_map/ppermute | solution.py:465
  399.3 13.2 %rope.6 = (bf16[4096,512]{1,0:T(8,128)(2,1)}, bf16[4096,512]{1,0:T(8,128)(2,1)}, bf16[65536,128]{1,0:T(8,128)(2,1)}) custom-call(bf16[4096,512]{1,0:T(8,128)(2,1)} %get-tuple-element.185.q_ref, bf16[4096,512]{1,0:T(8,128)(2,1)} %get-tuple-element.186.k_ref, f32[2,4096]{1,0:T(2,128)} %add.57.ss_ref, ...), custom_call_target="tpu_custom_call", output_to_operand_aliasing={{2}: (7, {})} | custom-call | flops 7000000000 | bytes 20971520 | tf_op jit(solution)/shard_map/rope/pallas_call | solution.py:225
  412.6 53.9 %attn.6 = (bf16[1024,512]{1,0:T(8,128)(2,1)}, bf16[1024,512]{1,0:T(8,128)(2,1)}, bf16[1024,512]{1,0:T(8,128)(2,1)}, bf16[1024,512]{1,0:T(8,128)(2,1)}) custom-call(bf16[4096,512]{1,0:T(8,128)(2,1)} %get-tuple-element.190.q_ref, bf16[4096,512]{1,0:T(8,128)(2,1)} %get-tuple-element.191.k_ref, bf16[512,4096]{1,0:T(8,128)(2,1)} %get-tuple-element.192.vt_ref), custom_call_target="tpu_custom_call" | custom-call | flops 34359738368 | bytes 16777216 | tf_op jit(solution)/shard_map/attn/pallas_call | solution.py:336
  471.1 21.9 %qkv.15 = (bf16[4096,512]{1,0:T(8,128)(2,1)}, bf16[4096,512]{1,0:T(8,128)(2,1)}, bf16[512,4096]{1,0:T(8,128)(2,1)}, bf16[65536,128]{1,0:T(8,128)(2,1)}, f32[2,4096]{1,0:T(2,128)}) custom-call(s32[1]{0:T(128)} %bitcast.me_ref, ...), custom_call_target="tpu_custom_call", output_to_operand_aliasing={{0}: (8, {}), {1}: (9, {}), {2}: (10, {}), {3}: (11, {}), {... | custom-call | flops 12884901888 | bytes 23068672 | tf_op jit(solution)/shard_map/qkv/pallas_call | solution.py:159
  508.4 13.2 %rope.7 = (bf16[4096,512]{1,0:T(8,128)(2,1)}, bf16[4096,512]{1,0:T(8,128)(2,1)}, bf16[65536,128]{1,0:T(8,128)(2,1)}) custom-call(bf16[4096,512]{1,0:T(8,128)(2,1)} %get-tuple-element.200.q_ref, bf16[4096,512]{1,0:T(8,128)(2,1)} %get-tuple-element.201.k_ref, f32[2,4096]{1,0:T(2,128)} %add.59.ss_ref, ...), custom_call_target="tpu_custom_call", output_to_operand_aliasing={{2}: (7, {})} | custom-call | flops 7000000000 | bytes 20971520 | tf_op jit(solution)/shard_map/rope/pallas_call | solution.py:225
  521.6 54.0 %attn.7 = (bf16[512,512]{1,0:T(8,128)(2,1)}, bf16[512,512]{1,0:T(8,128)(2,1)}, bf16[512,512]{1,0:T(8,128)(2,1)}, bf16[512,512]{1,0:T(8,128)(2,1)}, bf16[512,512]...) custom-call(bf16[4096,512]{1,0:T(8,128)(2,1)} %get-tuple-element.205.q_ref, ...), custom_call_target="tpu_custom_call" | custom-call | flops 34359738368 | bytes 16777216 | tf_op jit(solution)/shard_map/attn/pallas_call | solution.py:336
  578.0 23.0 %collective-permute-done.48.refs_7_ = bf16[1024,512]{1,0:T(8,128)(2,1)S(1)} collective-permute-done((bf16[1024,512]{1,0:T(8,128)(2,1)}, bf16[1024,512]{1,0:T(8,128)(2,1)S(1)}, u32[]{:S(2)}, u32[]{:S(2)}) %collective-permute-start.48) | collective-permute-done | bytes 1048608 | tf_op jit(solution)/shard_map/ppermute | solution.py:465
  601.5 22.3 %collective-permute-done.47.refs_6_ = bf16[1024,512]{1,0:T(8,128)(2,1)S(1)} collective-permute-done((bf16[1024,512]{1,0:T(8,128)(2,1)}, bf16[1024,512]{1,0:T(8,128)(2,1)S(1)}, u32[]{:S(2)}, u32[]{:S(2)}) %collective-permute-start.47) | collective-permute-done | bytes 1048608 | tf_op jit(solution)/shard_map/ppermute | solution.py:465
  632.4 17.2 %collective-permute-done.51.refs_11_ = bf16[1024,512]{1,0:T(8,128)(2,1)} collective-permute-done((bf16[1024,512]{1,0:T(8,128)(2,1)}, bf16[1024,512]{1,0:T(8,128)(2,1)}, u32[]{:S(2)}, u32[]{:S(2)}) %collective-permute-start.51) | collective-permute-done | bytes 1048608 | tf_op jit(solution)/shard_map/ppermute | solution.py:465
  650.8 21.2 %collective-permute-done.50.refs_10_ = bf16[1024,512]{1,0:T(8,128)(2,1)} collective-permute-done((bf16[1024,512]{1,0:T(8,128)(2,1)}, bf16[1024,512]{1,0:T(8,128)(2,1)}, u32[]{:S(2)}, u32[]{:S(2)}) %collective-permute-start.50) | collective-permute-done | bytes 1048608 | tf_op jit(solution)/shard_map/ppermute | solution.py:465
  674.8 34.4 %outproj.2.refs_9_ = bf16[4,1024,2048]{2,1,0:T(8,128)(2,1)} custom-call(bf16[1024,512]{1,0:T(8,128)(2,1)} %get-tuple-element.222.refs_0_, bf16[1024,512]{1,0:T(8,128)(2,1)} %collective-permute-done.43.refs_1_, bf16[1024,512]{1,0:T(8,128)(2,1)} %collective-permute-done.44.refs_2_, bf16[1024,512]{1,0:T(8,128)(2,1)} %collective-permute-done.45.refs_3_, ...), custom_call_target="tpu_custom_call" | custom-call | flops 25769803776 | bytes 62914560 | tf_op jit(solution)/shard_map/outproj/pallas_call | solution.py:392
  710.2 10.1 %outproj.3.refs_0_ = bf16[4,1024,2048]{2,1,0:T(8,128)(2,1)} custom-call(bf16[512,512]{1,0:T(8,128)(2,1)} %get-tuple-element.214.refs_0_, bf16[512,512]{1,0:T(8,128)(2,1)} %copy-done.5, bf16[512,512]{1,0:T(8,128)(2,1)} %copy-done.6, bf16[512,512]{1,0:T(8,128)(2,1)} %collective-permute-done.42.refs_3_, ...), custom_call_target="tpu_custom_call", output_to_operand_aliasing={{}: (9, {})} | custom-call | flops 4294967296 | bytes 14680064 | tf_op jit(solution)/shard_map/outproj/pallas_call | solution.py:392
  (162 shorter events, 117.2 us)
Async XLA Ops:
  8.6 87.2 %collective-permute-start.2 = (bf16[512,2048]{1,0:T(8,128)(2,1)}, bf16[512,2048]{1,0:T(8,128)(2,1)}, u32[]{:S(2)}, u32[]{:S(2)}) collective-permute-start(bf16[512,2048]{1,0:T(8,128)(2,1)} %norm.6.h1_ref), channel_id=1, source_target_pairs={{0,2},{1,3},{2,0},{3,1},{4,6},{5,7},{6,4},{7,5}} | collective-permute-start | bytes 6291464 | tf_op jit(solution)/shard_map/ppermute | solution.py:465
  51.7 50.9 %collective-permute-start.1 = (bf16[512,2048]{1,0:T(8,128)(2,1)S(1)}, bf16[512,2048]{1,0:T(8,128)(2,1)}, u32[]{:S(2)}, u32[]{:S(2)}) collective-permute-start(bf16[512,2048]{1,0:T(8,128)(2,1)S(1)} %copy-done.1), channel_id=1, source_target_pairs={{0,2},{1,3},{2,0},{3,1},{4,6},{5,7},{6,4},{7,5}} | collective-permute-start | bytes 6291464 | tf_op jit(solution)/shard_map/ppermute | solution.py:465
  109.3 49.0 %collective-permute-start = (bf16[512,2048]{1,0:T(8,128)(2,1)}, bf16[512,2048]{1,0:T(8,128)(2,1)}, u32[]{:S(2)}, u32[]{:S(2)}) collective-permute-start(bf16[512,2048]{1,0:T(8,128)(2,1)} %get-tuple-element.130.h0_ref), channel_id=1, source_target_pairs={{0,2},{1,3},{2,0},{3,1},{4,6},{5,7},{6,4},{7,5}} | collective-permute-start | bytes 6291464 | tf_op jit(solution)/shard_map/ppermute | solution.py:465
  158.3 71.0 %collective-permute-start.16 = (bf16[512,2048]{1,0:T(8,128)(2,1)}, bf16[512,2048]{1,0:T(8,128)(2,1)}, u32[]{:S(2)}, u32[]{:S(2)}) collective-permute-start(bf16[512,2048]{1,0:T(8,128)(2,1)} %collective-permute-done.h0_ref), channel_id=1, source_target_pairs={{0,1},{1,0},{2,3},{3,2},{4,5},{5,4},{6,7},{7,6}} | collective-permute-start | bytes 6291464 | tf_op jit(solution)/shard_map/ppermute | solution.py:465
  158.8 69.6 %collective-permute-start.11 = (bf16[512,2048]{1,0:T(8,128)(2,1)S(1)}, bf16[512,2048]{1,0:T(8,128)(2,1)}, u32[]{:S(2)}, u32[]{:S(2)}) collective-permute-start(bf16[512,2048]{1,0:T(8,128)(2,1)S(1)} %copy-done.10), channel_id=1, source_target_pairs={{0,2},{1,3},{2,0},{3,1},{4,6},{5,7},{6,4},{7,5}} | collective-permute-start | bytes 6291464 | tf_op jit(solution)/shard_map/ppermute | solution.py:465
  228.5 49.8 %collective-permute-start.19 = (bf16[512,2048]{1,0:T(8,128)(2,1)}, bf16[512,2048]{1,0:T(8,128)(2,1)S(1)}, u32[]{:S(2)}, u32[]{:S(2)}) collective-permute-start(bf16[512,2048]{1,0:T(8,128)(2,1)} %get-tuple-element.166.h0_ref), channel_id=1, source_target_pairs={{0,2},{1,3},{2,0},{3,1},{4,6},{5,7},{6,4},{7,5}} | collective-permute-start | bytes 6291464 | tf_op jit(solution)/shard_map/ppermute | solution.py:465
  278.3 70.2 %collective-permute-start.23 = (bf16[512,2048]{1,0:T(8,128)(2,1)S(1)}, bf16[512,2048]{1,0:T(8,128)(2,1)}, u32[]{:S(2)}, u32[]{:S(2)}) collective-permute-start(bf16[512,2048]{1,0:T(8,128)(2,1)S(1)} %collective-permute-done.19.h0_ref), channel_id=1, source_target_pairs={{0,1},{1,0},{2,3},{3,2},{4,5},{5,4},{6,7},{7,6}} | collective-permute-start | bytes 6291464 | tf_op jit(solution)/shard_map/ppermute | solution.py:465
  278.8 68.3 %collective-permute-start.20 = (bf16[512,2048]{1,0:T(8,128)(2,1)}, bf16[512,2048]{1,0:T(8,128)(2,1)}, u32[]{:S(2)}, u32[]{:S(2)}) collective-permute-start(bf16[512,2048]{1,0:T(8,128)(2,1)} %get-tuple-element.167.h1_ref), channel_id=1, source_target_pairs={{0,2},{1,3},{2,0},{3,1},{4,6},{5,7},{6,4},{7,5}} | collective-permute-start | bytes 6291464 | tf_op jit(solution)/shard_map/ppermute | solution.py:465
  347.3 49.6 %collective-permute-start.18 = (bf16[512,2048]{1,0:T(8,128)(2,1)}, bf16[512,2048]{1,0:T(8,128)(2,1)}, u32[]{:S(2)}, u32[]{:S(2)}) collective-permute-start(bf16[512,2048]{1,0:T(8,128)(2,1)} %get-tuple-element.165.h0_ref), channel_id=1, source_target_pairs={{0,2},{1,3},{2,0},{3,1},{4,6},{5,7},{6,4},{7,5}} | collective-permute-start | bytes 6291464 | tf_op jit(solution)/shard_map/ppermute | solution.py:465
  396.9 73.1 %collective-permute-start.28 = (bf16[512,2048]{1,0:T(8,128)(2,1)}, bf16[512,2048]{1,0:T(8,128)(2,1)}, u32[]{:S(2)}, u32[]{:S(2)}) collective-permute-start(bf16[512,2048]{1,0:T(8,128)(2,1)} %collective-permute-done.18.h0_ref), channel_id=1, source_target_pairs={{0,1},{1,0},{2,3},{3,2},{4,5},{5,4},{6,7},{7,6}} | collective-permute-start | bytes 6291464 | tf_op jit(solution)/shard_map/ppermute | solution.py:465
  397.4 69.2 %collective-permute-start.25 = (bf16[512,2048]{1,0:T(8,128)(2,1)S(1)}, bf16[512,2048]{1,0:T(8,128)(2,1)}, u32[]{:S(2)}, u32[]{:S(2)}) collective-permute-start(bf16[512,2048]{1,0:T(8,128)(2,1)S(1)} %copy-done.9), channel_id=1, source_target_pairs={{0,2},{1,3},{2,0},{3,1},{4,6},{5,7},{6,4},{7,5}} | collective-permute-start | bytes 6291464 | tf_op jit(solution)/shard_map/ppermute | solution.py:465
  493.7 82.9 %collective-permute-start.45 = (bf16[1024,512]{1,0:T(8,128)(2,1)}, bf16[1024,512]{1,0:T(8,128)(2,1)}, u32[]{:S(2)}, u32[]{:S(2)}) collective-permute-start(bf16[1024,512]{1,0:T(8,128)(2,1)} %get-tuple-element.228), channel_id=1, source_target_pairs={{0,3},{1,2},{2,1},{3,0},{4,7},{5,6},{6,5},{7,4}} | collective-permute-start | bytes 3145736 | tf_op jit(solution)/shard_map/ppermute | solution.py:465
  494.4 83.1 %collective-permute-start.44 = (bf16[1024,512]{1,0:T(8,128)(2,1)}, bf16[1024,512]{1,0:T(8,128)(2,1)}, u32[]{:S(2)}, u32[]{:S(2)}) collective-permute-start(bf16[1024,512]{1,0:T(8,128)(2,1)} %get-tuple-element.226), channel_id=1, source_target_pairs={{0,2},{1,3},{2,0},{3,1},{4,6},{5,7},{6,4},{7,5}} | collective-permute-start | bytes 3145736 | tf_op jit(solution)/shard_map/ppermute | solution.py:465
  495.2 82.4 %collective-permute-start.43 = (bf16[1024,512]{1,0:T(8,128)(2,1)}, bf16[1024,512]{1,0:T(8,128)(2,1)}, u32[]{:S(2)}, u32[]{:S(2)}) collective-permute-start(bf16[1024,512]{1,0:T(8,128)(2,1)} %get-tuple-element.224), channel_id=1, source_target_pairs={{0,1},{1,0},{2,3},{3,2},{4,5},{5,4},{6,7},{7,6}} | collective-permute-start | bytes 3145736 | tf_op jit(solution)/shard_map/ppermute | solution.py:465
  505.3 70.3 %collective-permute-start.36 = (bf16[128,2048]{1,0:T(8,128)(2,1)}, bf16[128,2048]{1,0:T(8,128)(2,1)S(1)}, u32[]{:S(2)}, u32[]{:S(2)}) collective-permute-start(bf16[128,2048]{1,0:T(8,128)(2,1)} %slice.10), channel_id=1, source_target_pairs={{0,2},{1,3},{2,0},{3,1},{4,6},{5,7},{6,4},{7,5}} | collective-permute-start | bytes 1572872 | tf_op jit(solution)/shard_map/ppermute | solution.py:465
  507.4 117.9 %collective-permute-start.39 = (bf16[512,2048]{1,0:T(8,128)(2,1)}, bf16[512,2048]{1,0:T(8,128)(2,1)}, u32[]{:S(2)}, u32[]{:S(2)}) collective-permute-start(bf16[512,2048]{1,0:T(8,128)(2,1)} %refs_4_.1), channel_id=1, source_target_pairs={{0,1},{1,0},{2,3},{3,2},{4,5},{5,4},{6,7},{7,6}} | collective-permute-start | bytes 6291464 | tf_op jit(solution)/shard_map/ppermute | solution.py:465
  576.6 47.2 %collective-permute-start.47 = (bf16[1024,512]{1,0:T(8,128)(2,1)}, bf16[1024,512]{1,0:T(8,128)(2,1)S(1)}, u32[]{:S(2)}, u32[]{:S(2)}) collective-permute-start(bf16[1024,512]{1,0:T(8,128)(2,1)} %get-tuple-element.232), channel_id=1, source_target_pairs={{0,2},{1,3},{2,0},{3,1},{4,6},{5,7},{6,4},{7,5}} | collective-permute-start | bytes 3145736 | tf_op jit(solution)/shard_map/ppermute | solution.py:465
  577.5 96.3 %collective-permute-start.37 = (bf16[512,2048]{1,0:T(8,128)(2,1)S(1)}, bf16[512,2048]{1,0:T(8,128)(2,1)}, u32[]{:S(2)}, u32[]{:S(2)}) collective-permute-start(bf16[512,2048]{1,0:T(8,128)(2,1)S(1)} %constant_dynamic-update-slice_fusion.refs_14_.refs_6_.w2_ref), channel_id=1, source_target_pairs={{0,1},{1,0},{2,3},{3,2},{4,5},{5,4},{6,7},{7,6}} | collective-permute-start | bytes 6291464 | tf_op jit(solution)/shard_map/ppermute | solution.py:465
  577.6 46.9 %collective-permute-start.38 = (bf16[512,512]{1,0:T(8,128)(2,1)}, bf16[512,512]{1,0:T(8,128)(2,1)S(1)}, u32[]{:S(2)}, u32[]{:S(2)}) collective-permute-start(bf16[512,512]{1,0:T(8,128)(2,1)} %get-tuple-element.217), channel_id=1, source_target_pairs={{0,1},{1,0},{2,3},{3,2},{4,5},{5,4},{6,7},{7,6}} | collective-permute-start | bytes 1572872 | tf_op jit(solution)/shard_map/ppermute | solution.py:465
  624.5 47.5 %collective-permute-start.50 = (bf16[1024,512]{1,0:T(8,128)(2,1)}, bf16[1024,512]{1,0:T(8,128)(2,1)}, u32[]{:S(2)}, u32[]{:S(2)}) collective-permute-start(bf16[1024,512]{1,0:T(8,128)(2,1)} %get-tuple-element.238), channel_id=1, source_target_pairs={{0,2},{1,3},{2,0},{3,1},{4,6},{5,7},{6,4},{7,5}} | collective-permute-start | bytes 3145736 | tf_op jit(solution)/shard_map/ppermute | solution.py:465
  625.3 47.8 %collective-permute-start.49 = (bf16[1024,512]{1,0:T(8,128)(2,1)}, bf16[1024,512]{1,0:T(8,128)(2,1)}, u32[]{:S(2)}, u32[]{:S(2)}) collective-permute-start(bf16[1024,512]{1,0:T(8,128)(2,1)} %get-tuple-element.236), channel_id=1, source_target_pairs={{0,1},{1,0},{2,3},{3,2},{4,5},{5,4},{6,7},{7,6}} | collective-permute-start | bytes 3145736 | tf_op jit(solution)/shard_map/ppermute | solution.py:465
  632.1 77.2 %collective-permute-start.40 = (bf16[512,512]{1,0:T(8,128)(2,1)}, bf16[512,512]{1,0:T(8,128)(2,1)S(1)}, u32[]{:S(2)}, u32[]{:S(2)}) collective-permute-start(bf16[512,512]{1,0:T(8,128)(2,1)} %get-tuple-element.219), channel_id=1, source_target_pairs={{0,1},{1,0},{2,3},{3,2},{4,5},{5,4},{6,7},{7,6}} | collective-permute-start | bytes 1572872 | tf_op jit(solution)/shard_map/ppermute | solution.py:465
  649.6 59.7 %collective-permute-start.41 = (bf16[512,512]{1,0:T(8,128)(2,1)}, bf16[512,512]{1,0:T(8,128)(2,1)S(1)}, u32[]{:S(2)}, u32[]{:S(2)}) collective-permute-start(bf16[512,512]{1,0:T(8,128)(2,1)} %get-tuple-element.220), channel_id=1, source_target_pairs={{0,2},{1,3},{2,0},{3,1},{4,6},{5,7},{6,4},{7,5}} | collective-permute-start | bytes 1572872 | tf_op jit(solution)/shard_map/ppermute | solution.py:465
  673.0 47.3 %collective-permute-start.32 = (bf16[512,512]{1,0:T(8,128)(2,1)}, bf16[512,512]{1,0:T(8,128)(2,1)S(1)}, u32[]{:S(2)}, u32[]{:S(2)}) collective-permute-start(bf16[512,512]{1,0:T(8,128)(2,1)} %get-tuple-element.208), channel_id=1, source_target_pairs={{0,2},{1,3},{2,0},{3,1},{4,6},{5,7},{6,4},{7,5}} | collective-permute-start | bytes 1572872 | tf_op jit(solution)/shard_map/ppermute | solution.py:465
  (46 other events, 917.6 us)

commit v7 on v6

--- a/solution.py
+++ b/solution.py
@@ -14,11 +14,12 @@
 F32 = jnp.float32
 BF16 = jnp.bfloat16
 QKV_ROWS = 256
+OUT_LIMIT = 48 * 1024 * 1024
 VMEM_LIMIT = 60 * 1024 * 1024
 
 
-def params(*sem):
-    return pltpu.CompilerParams(dimension_semantics=sem, vmem_limit_bytes=VMEM_LIMIT)
+def params(*sem, limit=VMEM_LIMIT):
+    return pltpu.CompilerParams(dimension_semantics=sem, vmem_limit_bytes=limit)
 
 
 def cost(flops, nbytes, trans=0):
@@ -397,7 +398,7 @@
         out_shape=jax.ShapeDtypeStruct(x.shape, BF16),
         scratch_shapes=[pltpu.VMEM((2, 4, rows, cols), BF16), pltpu.SemaphoreType.DMA((2, 4))],
         input_output_aliases=aliases,
-        compiler_params=params("arbitrary", "arbitrary"),
+        compiler_params=params("arbitrary", "arbitrary", limit=OUT_LIMIT),
         cost_estimate=cost(2 * n_items * rows * width * width, n_items * (2 * width * width + 6 * rows * width)),
         name="outproj",
     )(*args)
@@ -437,7 +438,7 @@
         out_specs=out_spec,
         out_shape=out_shape,
         input_output_aliases=aliases,
-        compiler_params=params("arbitrary"),
+        compiler_params=params("arbitrary", limit=OUT_LIMIT),
         cost_estimate=cost(4 * rows * cols * width, 4 * cols * width + 8 * rows * width),
         name="outhalf",
     )(*args)

time: 731 us -> 727 us (level)
  no operation moved by 1% of the time
where the time goes in v7:
time: 727 us; the launch traced here: 725 us
  Pallas kernels  525 us (72%)
  waiting for transfers between devices  145 us (20%)
  starting transfers between devices  32.2 us (4%)
  local copies, waits for them, and re-layouts  14 us (2%)
  other arithmetic  7.96 us (1%)
    pallas_call x4, Pallas kernels, attn_call(): pl.pallas_call(functools.partial(attn_kernel, n_tp, n_parts, n_h, bq, ch)...  216 us
    pallas_call x8, Pallas kernels, qkv_call(): pl.pallas_call(functools.partial(qkv_kernel, n_sub), grid_spec=pltpu.Pref...  176 us
    ppermute x52, waiting for transfers between devices, send(): return lax.ppermute(val, 'tp', pairs[hop])  145 us
    pallas_call x4, Pallas kernels, rope_call(): pl.pallas_call(functools.partial(rope_kernel, width), grid=(nq,), in_spec...  53 us
    pallas_call x2, Pallas kernels, out_call(): pl.pallas_call(functools.partial(out_kernel, n_items), grid=(n_items, wid...  42.4 us
    ppermute x52, starting transfers between devices, send(): return lax.ppermute(val, 'tp', pairs[hop])  32.2 us
    pallas_call x3, Pallas kernels, norm_call(): pl.pallas_call(norm_kernel, grid=(n,), in_specs=[pl.BlockSpec((1, br, wid...  18.5 us
  transfers between devices with their start and end apart: 52, of which 13 were waited for; matrix products, arithmetic and copies ran while one was open for 2% of the time, Pallas kernels for 71%

profile of v7, /device:TPU:0, one launch (start us, length us, event | category | flops | bytes accessed | tf_op | source)
XLA Modules:
  0.0 725.1 jit_solution(14038446320282288254)
XLA Ops:
  29.6 22.1 %qkv.8 = (bf16[4096,512]{1,0:T(8,128)(2,1)}, bf16[4096,512]{1,0:T(8,128)(2,1)}, bf16[512,4096]{1,0:T(8,128)(2,1)}, bf16[65536,128]{1,0:T(8,128)(2,1)}, f32[2,4096]{1,0:T(2,128)}) custom-call(s32[1]{0:T(128)} %bitcast.me_ref, bf16[512,2048]{1,0:T(8,128)(2,1)} %norm.5.h0_ref, bf16[512,2048]{1,0:T(8,128)(2,1)} %norm.6.h1_ref, bf16[512,2048]{1,0:T(8,128)(2,1)} %copy-done.15, ...), custom_call_target="tpu_custom_call" | custom-call | flops 12884901888 | bytes 23068672 | tf_op jit(solution)/shard_map/qkv/pallas_call | solution.py:160
  51.7 22.0 %qkv.9 = (bf16[4096,512]{1,0:T(8,128)(2,1)}, bf16[4096,512]{1,0:T(8,128)(2,1)}, bf16[512,4096]{1,0:T(8,128)(2,1)}, bf16[65536,128]{1,0:T(8,128)(2,1)}, f32[2,4096]{1,0:T(2,128)}) custom-call(s32[1]{0:T(128)} %bitcast.me_ref, bf16[512,2048]{1,0:T(8,128)(2,1)} %get-tuple-element.130.h0_ref, ...), custom_call_target="tpu_custom_call", output_to_operand_aliasing={{3}: (8, {})} | custom-call | flops 12884901888 | bytes 23068672 | tf_op jit(solution)/shard_map/qkv/pallas_call | solution.py:160
  73.7 22.0 %qkv.10 = (bf16[4096,512]{1,0:T(8,128)(2,1)}, bf16[4096,512]{1,0:T(8,128)(2,1)}, bf16[512,4096]{1,0:T(8,128)(2,1)}, bf16[65536,128]{1,0:T(8,128)(2,1)}, f32[2,4096]{1,0:T(2,128)}) custom-call(s32[1]{0:T(128)} %bitcast.me_ref, bf16[512,2048]{1,0:T(8,128)(2,1)} %get-tuple-element.166.h0_ref, ...), custom_call_target="tpu_custom_call", output_to_operand_aliasing={{3}: (8, {})} | custom-call | flops 12884901888 | bytes 23068672 | tf_op jit(solution)/shard_map/qkv/pallas_call | solution.py:160
  111.0 21.9 %qkv.11 = (bf16[4096,512]{1,0:T(8,128)(2,1)}, bf16[4096,512]{1,0:T(8,128)(2,1)}, bf16[512,4096]{1,0:T(8,128)(2,1)}, bf16[65536,128]{1,0:T(8,128)(2,1)}, f32[2,4096]{1,0:T(2,128)}) custom-call(s32[1]{0:T(128)} %bitcast.me_ref, ...), custom_call_target="tpu_custom_call", output_to_operand_aliasing={{0}: (8, {}), {1}: (9, {}), {2}: (10, {}), {3}: (11, {}), {... | custom-call | flops 12884901888 | bytes 23068672 | tf_op jit(solution)/shard_map/qkv/pallas_call | solution.py:160
  134.5 22.1 %qkv.12 = (bf16[4096,512]{1,0:T(8,128)(2,1)}, bf16[4096,512]{1,0:T(8,128)(2,1)}, bf16[512,4096]{1,0:T(8,128)(2,1)}, bf16[65536,128]{1,0:T(8,128)(2,1)}, f32[2,4096]{1,0:T(2,128)}) custom-call(s32[1]{0:T(128)} %bitcast.me_ref, bf16[512,2048]{1,0:T(8,128)(2,1)} %get-tuple-element.165.h0_ref, ...), custom_call_target="tpu_custom_call", output_to_operand_aliasing={{3}: (8, {})} | custom-call | flops 12884901888 | bytes 23068672 | tf_op jit(solution)/shard_map/qkv/pallas_call | solution.py:160
  161.1 13.3 %rope.4 = (bf16[4096,512]{1,0:T(8,128)(2,1)}, bf16[4096,512]{1,0:T(8,128)(2,1)}, bf16[65536,128]{1,0:T(8,128)(2,1)}) custom-call(bf16[4096,512]{1,0:T(8,128)(2,1)} %get-tuple-element.148.q_ref, bf16[4096,512]{1,0:T(8,128)(2,1)} %get-tuple-element.149.k_ref, f32[2,4096]{1,0:T(2,128)} %add.53.ss_ref, f32[1,512]{1,0:T(1,128)} %bitcast.27, f32[1,512]{1,0:T(1,128)} %bitcast.31, ...), custom_call_target="tpu_custom_call" | custom-call | flops 7000000000 | bytes 20971520 | tf_op jit(solution)/shard_map/rope/pallas_call | solution.py:226
  174.4 53.9 %attn.4 = (bf16[1024,512]{1,0:T(8,128)(2,1)}, bf16[1024,512]{1,0:T(8,128)(2,1)}, bf16[1024,512]{1,0:T(8,128)(2,1)}, bf16[1024,512]{1,0:T(8,128)(2,1)}) custom-call(bf16[4096,512]{1,0:T(8,128)(2,1)} %get-tuple-element.155.q_ref, bf16[4096,512]{1,0:T(8,128)(2,1)} %get-tuple-element.156.k_ref, bf16[512,4096]{1,0:T(8,128)(2,1)} %get-tuple-element.157.vt_ref), custom_call_target="tpu_custom_call" | custom-call | flops 34359738368 | bytes 16777216 | tf_op jit(solution)/shard_map/attn/pallas_call | solution.py:337
  232.9 21.9 %qkv.13 = (bf16[4096,512]{1,0:T(8,128)(2,1)}, bf16[4096,512]{1,0:T(8,128)(2,1)}, bf16[512,4096]{1,0:T(8,128)(2,1)}, bf16[65536,128]{1,0:T(8,128)(2,1)}, f32[2,4096]{1,0:T(2,128)}) custom-call(s32[1]{0:T(128)} %bitcast.me_ref, ...), custom_call_target="tpu_custom_call", output_to_operand_aliasing={{0}: (8, {}), {1}: (9, {}), {2}: (10, {}), {3}: (11, {}), {... | custom-call | flops 12884901888 | bytes 23068672 | tf_op jit(solution)/shard_map/qkv/pallas_call | solution.py:160
  256.6 20.8 %collective-permute-done.21 = f32[2,4096]{1,0:T(2,128)S(1)} collective-permute-done((f32[2,4096]{1,0:T(2,128)}, f32[2,4096]{1,0:T(2,128)S(1)}, u32[]{:S(2)}, u32[]{:S(2)}) %collective-permute-start.21) | collective-permute-done | bytes 32800 | tf_op jit(solution)/shard_map/ppermute | solution.py:466
  280.0 13.2 %rope.5 = (bf16[4096,512]{1,0:T(8,128)(2,1)}, bf16[4096,512]{1,0:T(8,128)(2,1)}, bf16[65536,128]{1,0:T(8,128)(2,1)}) custom-call(bf16[4096,512]{1,0:T(8,128)(2,1)} %get-tuple-element.168.q_ref, bf16[4096,512]{1,0:T(8,128)(2,1)} %get-tuple-element.169.k_ref, f32[2,4096]{1,0:T(2,128)} %add.55.ss_ref, ...), custom_call_target="tpu_custom_call", output_to_operand_aliasing={{2}: (7, {})} | custom-call | flops 7000000000 | bytes 20971520 | tf_op jit(solution)/shard_map/rope/pallas_call | solution.py:226
  293.2 53.7 %attn.5 = (bf16[1024,512]{1,0:T(8,128)(2,1)}, bf16[1024,512]{1,0:T(8,128)(2,1)}, bf16[1024,512]{1,0:T(8,128)(2,1)}, bf16[1024,512]{1,0:T(8,128)(2,1)}) custom-call(bf16[4096,512]{1,0:T(8,128)(2,1)} %get-tuple-element.173.q_ref, bf16[4096,512]{1,0:T(8,128)(2,1)} %get-tuple-element.174.k_ref, bf16[512,4096]{1,0:T(8,128)(2,1)} %get-tuple-element.175.vt_ref), custom_call_target="tpu_custom_call" | custom-call | flops 34359738368 | bytes 16777216 | tf_op jit(solution)/shard_map/attn/pallas_call | solution.py:337
  352.7 22.0 %qkv.14 = (bf16[4096,512]{1,0:T(8,128)(2,1)}, bf16[4096,512]{1,0:T(8,128)(2,1)}, bf16[512,4096]{1,0:T(8,128)(2,1)}, bf16[65536,128]{1,0:T(8,128)(2,1)}, f32[2,4096]{1,0:T(2,128)}) custom-call(s32[1]{0:T(128)} %bitcast.me_ref, bf16[512,2048]{1,0:T(8,128)(2,1)} %copy-done.14, ...), custom_call_target="tpu_custom_call", output_to_operand_aliasing={{0}: (8, {}), {1}: (9, {}), {2}: (10, {}), {3}: (11, {}), {... | custom-call | flops 12884901888 | bytes 23068672 | tf_op jit(solution)/shard_map/qkv/pallas_call | solution.py:160
  377.9 18.1 %collective-permute-done.26 = f32[2,4096]{1,0:T(2,128)S(1)} collective-permute-done((f32[2,4096]{1,0:T(2,128)}, f32[2,4096]{1,0:T(2,128)S(1)}, u32[]{:S(2)}, u32[]{:S(2)}) %collective-permute-start.26) | collective-permute-done | bytes 32800 | tf_op jit(solution)/shard_map/ppermute | solution.py:466
  399.2 13.2 %rope.6 = (bf16[4096,512]{1,0:T(8,128)(2,1)}, bf16[4096,512]{1,0:T(8,128)(2,1)}, bf16[65536,128]{1,0:T(8,128)(2,1)}) custom-call(bf16[4096,512]{1,0:T(8,128)(2,1)} %get-tuple-element.185.q_ref, bf16[4096,512]{1,0:T(8,128)(2,1)} %get-tuple-element.186.k_ref, f32[2,4096]{1,0:T(2,128)} %add.57.ss_ref, ...), custom_call_target="tpu_custom_call", output_to_operand_aliasing={{2}: (7, {})} | custom-call | flops 7000000000 | bytes 20971520 | tf_op jit(solution)/shard_map/rope/pallas_call | solution.py:226
  412.5 54.0 %attn.6 = (bf16[1024,512]{1,0:T(8,128)(2,1)}, bf16[1024,512]{1,0:T(8,128)(2,1)}, bf16[1024,512]{1,0:T(8,128)(2,1)}, bf16[1024,512]{1,0:T(8,128)(2,1)}) custom-call(bf16[4096,512]{1,0:T(8,128)(2,1)} %get-tuple-element.190.q_ref, bf16[4096,512]{1,0:T(8,128)(2,1)} %get-tuple-element.191.k_ref, bf16[512,4096]{1,0:T(8,128)(2,1)} %get-tuple-element.192.vt_ref), custom_call_target="tpu_custom_call" | custom-call | flops 34359738368 | bytes 16777216 | tf_op jit(solution)/shard_map/attn/pallas_call | solution.py:337
  470.9 21.9 %qkv.15 = (bf16[4096,512]{1,0:T(8,128)(2,1)}, bf16[4096,512]{1,0:T(8,128)(2,1)}, bf16[512,4096]{1,0:T(8,128)(2,1)}, bf16[65536,128]{1,0:T(8,128)(2,1)}, f32[2,4096]{1,0:T(2,128)}) custom-call(s32[1]{0:T(128)} %bitcast.me_ref, ...), custom_call_target="tpu_custom_call", output_to_operand_aliasing={{0}: (8, {}), {1}: (9, {}), {2}: (10, {}), {3}: (11, {}), {... | custom-call | flops 12884901888 | bytes 23068672 | tf_op jit(solution)/shard_map/qkv/pallas_call | solution.py:160
  508.3 13.2 %rope.7 = (bf16[4096,512]{1,0:T(8,128)(2,1)}, bf16[4096,512]{1,0:T(8,128)(2,1)}, bf16[65536,128]{1,0:T(8,128)(2,1)}) custom-call(bf16[4096,512]{1,0:T(8,128)(2,1)} %get-tuple-element.200.q_ref, bf16[4096,512]{1,0:T(8,128)(2,1)} %get-tuple-element.201.k_ref, f32[2,4096]{1,0:T(2,128)} %add.59.ss_ref, ...), custom_call_target="tpu_custom_call", output_to_operand_aliasing={{2}: (7, {})} | custom-call | flops 7000000000 | bytes 20971520 | tf_op jit(solution)/shard_map/rope/pallas_call | solution.py:226
  521.5 54.0 %attn.7 = (bf16[512,512]{1,0:T(8,128)(2,1)}, bf16[512,512]{1,0:T(8,128)(2,1)}, bf16[512,512]{1,0:T(8,128)(2,1)}, bf16[512,512]{1,0:T(8,128)(2,1)}, bf16[512,512]...) custom-call(bf16[4096,512]{1,0:T(8,128)(2,1)} %get-tuple-element.205.q_ref, ...), custom_call_target="tpu_custom_call" | custom-call | flops 34359738368 | bytes 16777216 | tf_op jit(solution)/shard_map/attn/pallas_call | solution.py:337
  577.9 23.1 %collective-permute-done.48.refs_7_ = bf16[1024,512]{1,0:T(8,128)(2,1)S(1)} collective-permute-done((bf16[1024,512]{1,0:T(8,128)(2,1)}, bf16[1024,512]{1,0:T(8,128)(2,1)S(1)}, u32[]{:S(2)}, u32[]{:S(2)}) %collective-permute-start.48) | collective-permute-done | bytes 1048608 | tf_op jit(solution)/shard_map/ppermute | solution.py:466
  601.3 22.4 %collective-permute-done.47.refs_6_ = bf16[1024,512]{1,0:T(8,128)(2,1)S(1)} collective-permute-done((bf16[1024,512]{1,0:T(8,128)(2,1)}, bf16[1024,512]{1,0:T(8,128)(2,1)S(1)}, u32[]{:S(2)}, u32[]{:S(2)}) %collective-permute-start.47) | collective-permute-done | bytes 1048608 | tf_op jit(solution)/shard_map/ppermute | solution.py:466
  633.0 16.4 %collective-permute-done.51.refs_11_ = bf16[1024,512]{1,0:T(8,128)(2,1)S(1)} collective-permute-done((bf16[1024,512]{1,0:T(8,128)(2,1)}, bf16[1024,512]{1,0:T(8,128)(2,1)S(1)}, u32[]{:S(2)}, u32[]{:S(2)}) %collective-permute-start.51) | collective-permute-done | bytes 1048608 | tf_op jit(solution)/shard_map/ppermute | solution.py:466
  650.6 21.4 %collective-permute-done.50.refs_10_ = bf16[1024,512]{1,0:T(8,128)(2,1)} collective-permute-done((bf16[1024,512]{1,0:T(8,128)(2,1)}, bf16[1024,512]{1,0:T(8,128)(2,1)}, u32[]{:S(2)}, u32[]{:S(2)}) %collective-permute-start.50) | collective-permute-done | bytes 1048608 | tf_op jit(solution)/shard_map/ppermute | solution.py:466
  676.3 33.7 %outproj.2.refs_9_ = bf16[4,1024,2048]{2,1,0:T(8,128)(2,1)} custom-call(bf16[1024,512]{1,0:T(8,128)(2,1)S(1)} %copy-done.6, bf16[1024,512]{1,0:T(8,128)(2,1)} %collective-permute-done.43.refs_1_, bf16[1024,512]{1,0:T(8,128)(2,1)} %collective-permute-done.44.refs_2_, bf16[1024,512]{1,0:T(8,128)(2,1)S(1)} %collective-permute-done.45.refs_3_, ...), custom_call_target="tpu_custom_call" | custom-call | flops 25769803776 | bytes 62914560 | tf_op jit(solution)/shard_map/outproj/pallas_call | solution.py:393
  710.1 8.7 %outproj.3.refs_0_ = bf16[4,1024,2048]{2,1,0:T(8,128)(2,1)} custom-call(bf16[512,512]{1,0:T(8,128)(2,1)S(1)} %copy-done.5, bf16[512,512]{1,0:T(8,128)(2,1)S(1)} %collective-permute-done.40.refs_1_, bf16[512,512]{1,0:T(8,128)(2,1)S(1)} %collective-permute-done.41.refs_2_, ...), custom_call_target="tpu_custom_call", output_to_operand_aliasing={{}: (9, {})} | custom-call | flops 4294967296 | bytes 14680064 | tf_op jit(solution)/shard_map/outproj/pallas_call | solution.py:393
  (172 shorter events, 115.3 us)
Async XLA Ops:
  8.5 87.2 %collective-permute-start.2 = (bf16[512,2048]{1,0:T(8,128)(2,1)}, bf16[512,2048]{1,0:T(8,128)(2,1)}, u32[]{:S(2)}, u32[]{:S(2)}) collective-permute-start(bf16[512,2048]{1,0:T(8,128)(2,1)} %norm.6.h1_ref), channel_id=1, source_target_pairs={{0,2},{1,3},{2,0},{3,1},{4,6},{5,7},{6,4},{7,5}} | collective-permute-start | bytes 6291464 | tf_op jit(solution)/shard_map/ppermute | solution.py:466
  51.7 50.9 %collective-permute-start.1 = (bf16[512,2048]{1,0:T(8,128)(2,1)S(1)}, bf16[512,2048]{1,0:T(8,128)(2,1)}, u32[]{:S(2)}, u32[]{:S(2)}) collective-permute-start(bf16[512,2048]{1,0:T(8,128)(2,1)S(1)} %copy-done.8), channel_id=1, source_target_pairs={{0,2},{1,3},{2,0},{3,1},{4,6},{5,7},{6,4},{7,5}} | collective-permute-start | bytes 6291464 | tf_op jit(solution)/shard_map/ppermute | solution.py:466
  109.3 49.0 %collective-permute-start = (bf16[512,2048]{1,0:T(8,128)(2,1)}, bf16[512,2048]{1,0:T(8,128)(2,1)}, u32[]{:S(2)}, u32[]{:S(2)}) collective-permute-start(bf16[512,2048]{1,0:T(8,128)(2,1)} %get-tuple-element.130.h0_ref), channel_id=1, source_target_pairs={{0,2},{1,3},{2,0},{3,1},{4,6},{5,7},{6,4},{7,5}} | collective-permute-start | bytes 6291464 | tf_op jit(solution)/shard_map/ppermute | solution.py:466
  158.3 71.0 %collective-permute-start.16 = (bf16[512,2048]{1,0:T(8,128)(2,1)}, bf16[512,2048]{1,0:T(8,128)(2,1)}, u32[]{:S(2)}, u32[]{:S(2)}) collective-permute-start(bf16[512,2048]{1,0:T(8,128)(2,1)} %collective-permute-done.h0_ref), channel_id=1, source_target_pairs={{0,1},{1,0},{2,3},{3,2},{4,5},{5,4},{6,7},{7,6}} | collective-permute-start | bytes 6291464 | tf_op jit(solution)/shard_map/ppermute | solution.py:466
  158.8 69.6 %collective-permute-start.11 = (bf16[512,2048]{1,0:T(8,128)(2,1)S(1)}, bf16[512,2048]{1,0:T(8,128)(2,1)}, u32[]{:S(2)}, u32[]{:S(2)}) collective-permute-start(bf16[512,2048]{1,0:T(8,128)(2,1)S(1)} %copy-done.13), channel_id=1, source_target_pairs={{0,2},{1,3},{2,0},{3,1},{4,6},{5,7},{6,4},{7,5}} | collective-permute-start | bytes 6291464 | tf_op jit(solution)/shard_map/ppermute | solution.py:466
  228.4 49.8 %collective-permute-start.19 = (bf16[512,2048]{1,0:T(8,128)(2,1)}, bf16[512,2048]{1,0:T(8,128)(2,1)S(1)}, u32[]{:S(2)}, u32[]{:S(2)}) collective-permute-start(bf16[512,2048]{1,0:T(8,128)(2,1)} %get-tuple-element.166.h0_ref), channel_id=1, source_target_pairs={{0,2},{1,3},{2,0},{3,1},{4,6},{5,7},{6,4},{7,5}} | collective-permute-start | bytes 6291464 | tf_op jit(solution)/shard_map/ppermute | solution.py:466
  278.2 70.2 %collective-permute-start.23 = (bf16[512,2048]{1,0:T(8,128)(2,1)S(1)}, bf16[512,2048]{1,0:T(8,128)(2,1)}, u32[]{:S(2)}, u32[]{:S(2)}) collective-permute-start(bf16[512,2048]{1,0:T(8,128)(2,1)S(1)} %collective-permute-done.19.h0_ref), channel_id=1, source_target_pairs={{0,1},{1,0},{2,3},{3,2},{4,5},{5,4},{6,7},{7,6}} | collective-permute-start | bytes 6291464 | tf_op jit(solution)/shard_map/ppermute | solution.py:466
  278.7 68.3 %collective-permute-start.20 = (bf16[512,2048]{1,0:T(8,128)(2,1)}, bf16[512,2048]{1,0:T(8,128)(2,1)}, u32[]{:S(2)}, u32[]{:S(2)}) collective-permute-start(bf16[512,2048]{1,0:T(8,128)(2,1)} %get-tuple-element.167.h1_ref), channel_id=1, source_target_pairs={{0,2},{1,3},{2,0},{3,1},{4,6},{5,7},{6,4},{7,5}} | collective-permute-start | bytes 6291464 | tf_op jit(solution)/shard_map/ppermute | solution.py:466
  347.2 49.6 %collective-permute-start.18 = (bf16[512,2048]{1,0:T(8,128)(2,1)}, bf16[512,2048]{1,0:T(8,128)(2,1)}, u32[]{:S(2)}, u32[]{:S(2)}) collective-permute-start(bf16[512,2048]{1,0:T(8,128)(2,1)} %get-tuple-element.165.h0_ref), channel_id=1, source_target_pairs={{0,2},{1,3},{2,0},{3,1},{4,6},{5,7},{6,4},{7,5}} | collective-permute-start | bytes 6291464 | tf_op jit(solution)/shard_map/ppermute | solution.py:466
  396.8 73.1 %collective-permute-start.28 = (bf16[512,2048]{1,0:T(8,128)(2,1)}, bf16[512,2048]{1,0:T(8,128)(2,1)}, u32[]{:S(2)}, u32[]{:S(2)}) collective-permute-start(bf16[512,2048]{1,0:T(8,128)(2,1)} %collective-permute-done.18.h0_ref), channel_id=1, source_target_pairs={{0,1},{1,0},{2,3},{3,2},{4,5},{5,4},{6,7},{7,6}} | collective-permute-start | bytes 6291464 | tf_op jit(solution)/shard_map/ppermute | solution.py:466
  397.3 69.2 %collective-permute-start.25 = (bf16[512,2048]{1,0:T(8,128)(2,1)S(1)}, bf16[512,2048]{1,0:T(8,128)(2,1)}, u32[]{:S(2)}, u32[]{:S(2)}) collective-permute-start(bf16[512,2048]{1,0:T(8,128)(2,1)S(1)} %copy-done.12), channel_id=1, source_target_pairs={{0,2},{1,3},{2,0},{3,1},{4,6},{5,7},{6,4},{7,5}} | collective-permute-start | bytes 6291464 | tf_op jit(solution)/shard_map/ppermute | solution.py:466
  493.6 82.9 %collective-permute-start.45 = (bf16[1024,512]{1,0:T(8,128)(2,1)}, bf16[1024,512]{1,0:T(8,128)(2,1)S(1)}, u32[]{:S(2)}, u32[]{:S(2)}) collective-permute-start(bf16[1024,512]{1,0:T(8,128)(2,1)} %get-tuple-element.228), channel_id=1, source_target_pairs={{0,3},{1,2},{2,1},{3,0},{4,7},{5,6},{6,5},{7,4}} | collective-permute-start | bytes 3145736 | tf_op jit(solution)/shard_map/ppermute | solution.py:466
  494.3 83.0 %collective-permute-start.44 = (bf16[1024,512]{1,0:T(8,128)(2,1)}, bf16[1024,512]{1,0:T(8,128)(2,1)}, u32[]{:S(2)}, u32[]{:S(2)}) collective-permute-start(bf16[1024,512]{1,0:T(8,128)(2,1)} %get-tuple-element.226), channel_id=1, source_target_pairs={{0,2},{1,3},{2,0},{3,1},{4,6},{5,7},{6,4},{7,5}} | collective-permute-start | bytes 3145736 | tf_op jit(solution)/shard_map/ppermute | solution.py:466
  496.0 81.5 %collective-permute-start.43 = (bf16[1024,512]{1,0:T(8,128)(2,1)}, bf16[1024,512]{1,0:T(8,128)(2,1)}, u32[]{:S(2)}, u32[]{:S(2)}) collective-permute-start(bf16[1024,512]{1,0:T(8,128)(2,1)} %get-tuple-element.224), channel_id=1, source_target_pairs={{0,1},{1,0},{2,3},{3,2},{4,5},{5,4},{6,7},{7,6}} | collective-permute-start | bytes 3145736 | tf_op jit(solution)/shard_map/ppermute | solution.py:466
  505.2 70.3 %collective-permute-start.36 = (bf16[128,2048]{1,0:T(8,128)(2,1)}, bf16[128,2048]{1,0:T(8,128)(2,1)S(1)}, u32[]{:S(2)}, u32[]{:S(2)}) collective-permute-start(bf16[128,2048]{1,0:T(8,128)(2,1)} %slice.10), channel_id=1, source_target_pairs={{0,2},{1,3},{2,0},{3,1},{4,6},{5,7},{6,4},{7,5}} | collective-permute-start | bytes 1572872 | tf_op jit(solution)/shard_map/ppermute | solution.py:466
  507.3 117.9 %collective-permute-start.39 = (bf16[512,2048]{1,0:T(8,128)(2,1)}, bf16[512,2048]{1,0:T(8,128)(2,1)}, u32[]{:S(2)}, u32[]{:S(2)}) collective-permute-start(bf16[512,2048]{1,0:T(8,128)(2,1)} %refs_4_.1), channel_id=1, source_target_pairs={{0,1},{1,0},{2,3},{3,2},{4,5},{5,4},{6,7},{7,6}} | collective-permute-start | bytes 6291464 | tf_op jit(solution)/shard_map/ppermute | solution.py:466
  576.5 47.2 %collective-permute-start.47 = (bf16[1024,512]{1,0:T(8,128)(2,1)}, bf16[1024,512]{1,0:T(8,128)(2,1)S(1)}, u32[]{:S(2)}, u32[]{:S(2)}) collective-permute-start(bf16[1024,512]{1,0:T(8,128)(2,1)} %get-tuple-element.232), channel_id=1, source_target_pairs={{0,2},{1,3},{2,0},{3,1},{4,6},{5,7},{6,4},{7,5}} | collective-permute-start | bytes 3145736 | tf_op jit(solution)/shard_map/ppermute | solution.py:466
  577.4 96.3 %collective-permute-start.37 = (bf16[512,2048]{1,0:T(8,128)(2,1)S(1)}, bf16[512,2048]{1,0:T(8,128)(2,1)S(1)}, u32[]{:S(2)}, u32[]{:S(2)}) collective-permute-start(bf16[512,2048]{1,0:T(8,128)(2,1)S(1)} %constant_dynamic-update-slice_fusion.refs_14_.refs_6_.w2_ref), channel_id=1, source_target_pairs={{0,1},{1,0},{2,3},{3,2},{4,5},{5,4},{6,7},{7,6}} | collective-permute-start | bytes 6291464 | tf_op jit(solution)/shard_map/ppermute | solution.py:466
  577.5 46.9 %collective-permute-start.38 = (bf16[512,512]{1,0:T(8,128)(2,1)}, bf16[512,512]{1,0:T(8,128)(2,1)S(1)}, u32[]{:S(2)}, u32[]{:S(2)}) collective-permute-start(bf16[512,512]{1,0:T(8,128)(2,1)} %get-tuple-element.217), channel_id=1, source_target_pairs={{0,1},{1,0},{2,3},{3,2},{4,5},{5,4},{6,7},{7,6}} | collective-permute-start | bytes 1572872 | tf_op jit(solution)/shard_map/ppermute | solution.py:466
  624.4 47.5 %collective-permute-start.50 = (bf16[1024,512]{1,0:T(8,128)(2,1)}, bf16[1024,512]{1,0:T(8,128)(2,1)}, u32[]{:S(2)}, u32[]{:S(2)}) collective-permute-start(bf16[1024,512]{1,0:T(8,128)(2,1)} %get-tuple-element.238), channel_id=1, source_target_pairs={{0,2},{1,3},{2,0},{3,1},{4,6},{5,7},{6,4},{7,5}} | collective-permute-start | bytes 3145736 | tf_op jit(solution)/shard_map/ppermute | solution.py:466
  625.2 47.7 %collective-permute-start.49 = (bf16[1024,512]{1,0:T(8,128)(2,1)}, bf16[1024,512]{1,0:T(8,128)(2,1)}, u32[]{:S(2)}, u32[]{:S(2)}) collective-permute-start(bf16[1024,512]{1,0:T(8,128)(2,1)} %get-tuple-element.236), channel_id=1, source_target_pairs={{0,1},{1,0},{2,3},{3,2},{4,5},{5,4},{6,7},{7,6}} | collective-permute-start | bytes 3145736 | tf_op jit(solution)/shard_map/ppermute | solution.py:466
  632.8 77.2 %collective-permute-start.40 = (bf16[512,512]{1,0:T(8,128)(2,1)}, bf16[512,512]{1,0:T(8,128)(2,1)S(1)}, u32[]{:S(2)}, u32[]{:S(2)}) collective-permute-start(bf16[512,512]{1,0:T(8,128)(2,1)} %get-tuple-element.219), channel_id=1, source_target_pairs={{0,1},{1,0},{2,3},{3,2},{4,5},{5,4},{6,7},{7,6}} | collective-permute-start | bytes 1572872 | tf_op jit(solution)/shard_map/ppermute | solution.py:466
  649.4 60.7 %collective-permute-start.41 = (bf16[512,512]{1,0:T(8,128)(2,1)}, bf16[512,512]{1,0:T(8,128)(2,1)S(1)}, u32[]{:S(2)}, u32[]{:S(2)}) collective-permute-start(bf16[512,512]{1,0:T(8,128)(2,1)} %get-tuple-element.220), channel_id=1, source_target_pairs={{0,2},{1,3},{2,0},{3,1},{4,6},{5,7},{6,4},{7,5}} | collective-permute-start | bytes 1572872 | tf_op jit(solution)/shard_map/ppermute | solution.py:466
  672.9 45.9 %collective-permute-start.32 = (bf16[512,512]{1,0:T(8,128)(2,1)}, bf16[512,512]{1,0:T(8,128)(2,1)S(1)}, u32[]{:S(2)}, u32[]{:S(2)}) collective-permute-start(bf16[512,512]{1,0:T(8,128)(2,1)} %get-tuple-element.208), channel_id=1, source_target_pairs={{0,2},{1,3},{2,0},{3,1},{4,6},{5,7},{6,4},{7,5}} | collective-permute-start | bytes 1572872 | tf_op jit(solution)/shard_map/ppermute | solution.py:466
  (51 other events, 1070.9 us)
